TPU v7x, 32 devices: a whole 2x2x4 slice. The times are simulated.
32 devices in a mesh: ty: 4 (over z), tx: 8 (over y, x, core).
Axes of the slice: x: 2, y: 2, z: 4, core: 2. Of those that a mesh axis runs over, the one named last changes fastest.
Arguments:
- object_slices: float32 [2, 2, 2048, 4096], P(None, None, 'ty', 'tx'), may hold values from -4 to 4
- probe_modes: float32 [4, 2, 128, 128], replicated, may hold values from -12 to 12
- patterns: bfloat16 [256, 128, 128], P(('ty', 'tx')), may hold values from 0 to 2
- positions: int32 [256, 2], replicated, may hold values from 0 to 4095, as said below
- counts: int32 [32], replicated, may hold values from 6 to 8, as said below
Outputs:
- new_object: float32 [2, 2, 2048, 4096], P(None, None, 'ty', 'tx')
- new_probe: float32 [4, 2, 128, 128], replicated
Inputs may be any that keep to these rules, and one draw needn't show every extreme that they name: positions[j] is the centre of pattern j, which was acquired by device j // 8 of ty+tx (ty slowest); its column lies in that device's column of tiles of 512 x 512 cells. Of the live patterns of one device, at most 2 lie in any one row of tiles; in every column of tiles some row of tiles holds exactly 2 live patterns from every device of that column. The live patterns of device d are its first counts[d] slots; some device has 8.
All inputs are finite; a program needn't handle non-finite values.
Results may differ from a plain program's by a relative error of at most 0.0085.
The roundings to bfloat16 on the way count: a program that leaves them out, or rounds other values in their place, can miss the bound.
Values may be sent and summed in bfloat16 or wider, within the bound.
No kernel may reach another device: no remote copies, remote signals or barrier semaphores. Data moves between devices by JAX's collectives and lax.ppermute only.
A program may use at most 128 MiB of HBM per device.

v0:
```python
import math

import jax
import jax.numpy as jnp
from jax import lax
from jax.sharding import PartitionSpec as P

CAP = 2


PROPAGATION = 0.37


def extended_2(block, sides, width):
    for axis, dim in sides:
        count = lax.axis_size(axis)
        forward = [(i, i + 1) for i in range(count - 1)]
        backward = [(target, source) for source, target in forward]
        low = lax.ppermute(
            lax.slice_in_dim(block, block.shape[dim] - width, None, axis=dim), axis, forward
        )
        high = lax.ppermute(lax.slice_in_dim(block, 0, width, axis=dim), axis, backward)
        block = jnp.concatenate([low, block, high], axis=dim)
    return block


def make_tables(extent):
    indices = jnp.arange(extent, dtype=jnp.int32)
    product = indices[:, None] * indices[None, :] % extent
    angles = 2.0 * jnp.pi / extent * product.astype(jnp.float32)
    norm_scale = 1.0 / math.sqrt(extent)
    real_table = (jnp.cos(angles) * norm_scale).astype(jnp.bfloat16)
    imag_table = (-jnp.sin(angles) * norm_scale).astype(jnp.bfloat16)
    right_fwd = jnp.concatenate(
        [
            jnp.concatenate([real_table, imag_table], 1),
            jnp.concatenate([-imag_table, real_table], 1),
        ],
        0,
    )
    right_inv = jnp.concatenate(
        [
            jnp.concatenate([real_table, -imag_table], 1),
            jnp.concatenate([imag_table, real_table], 1),
        ],
        0,
    )
    left_fwd = jnp.concatenate([real_table, imag_table], 0)
    left_inv = jnp.concatenate([real_table, -imag_table], 0)
    frequency = jnp.where(indices < extent // 2, indices, indices - extent).astype(jnp.float32)
    phases = -jnp.pi * PROPAGATION / extent * (frequency[:, None] ** 2 + frequency[None, :] ** 2)
    kernel = jnp.stack([jnp.cos(phases), jnp.sin(phases)])
    return (right_fwd, left_fwd, right_inv, left_inv, kernel)


def transform(wave_field, right_table, left_table):
    extent = wave_field.shape[-1]
    rounded = wave_field.astype(jnp.bfloat16)
    joined = jnp.concatenate([rounded[:, 0], rounded[:, 1]], axis=-1)
    partial_value = jnp.einsum(
        "bpk,kq->bpq", joined, right_table, preferred_element_type=jnp.float32
    ).astype(jnp.bfloat16)
    stacked = jnp.einsum(
        "ij,bjq->biq", left_table, partial_value, preferred_element_type=jnp.float32
    )
    real_part = stacked[:, :extent, :extent] - stacked[:, extent:, extent:]
    imag_part = stacked[:, extent:, :extent] + stacked[:, :extent, extent:]
    return jnp.stack([real_part, imag_part], axis=1)


def complex_product(former, latter):
    former_re = former[..., 0, :, :]
    former_im = former[..., 1, :, :]
    latter_re = latter[..., 0, :, :]
    latter_im = latter[..., 1, :, :]
    return jnp.stack(
        [
            former_re * latter_re - former_im * latter_im,
            former_re * latter_im + former_im * latter_re,
        ],
        axis=-3,
    )


def conjugate(values):
    return jnp.stack([values[..., 0, :, :], -values[..., 1, :, :]], axis=-3)


def pattern_terms(window, amplitude, live_flag, probe_modes, tables):
    right_fwd, left_fwd, right_inv, left_inv, kernel = tables
    slices = window.shape[0]
    inputs = [probe_modes]
    far_field = None
    for slice_index in range(slices):
        exit_wave = complex_product(inputs[slice_index], window[slice_index])
        if slice_index + 1 < slices:
            spread_wave = complex_product(kernel, transform(exit_wave, right_fwd, left_fwd))
            inputs.append(transform(spread_wave, right_inv, left_inv))
        else:
            far_field = transform(exit_wave, right_fwd, left_fwd)
    intensity = jnp.sum(far_field[:, 0] ** 2 + far_field[:, 1] ** 2, axis=0)
    factor = (1.0 - amplitude / jnp.sqrt(jnp.maximum(intensity, 0.25))) * live_flag
    residue = far_field * factor
    backward = transform(residue, right_inv, left_inv)
    slice_grads = [None] * slices
    for slice_index in reversed(range(slices)):
        slice_grads[slice_index] = jnp.sum(
            complex_product(conjugate(inputs[slice_index]), backward), axis=0
        )
        if slice_index > 0:
            inner_wave = transform(
                complex_product(conjugate(window[slice_index]), backward), right_fwd, left_fwd
            )
            backward = transform(
                complex_product(conjugate(kernel), inner_wave), right_inv, left_inv
            )
    probe_term = complex_product(conjugate(window[0]), backward)
    return (jnp.stack(slice_grads), probe_term)


def settle(centre, leading, trailing, axis, margin):
    length = centre.shape[axis]
    top_part = lax.slice_in_dim(centre, 0, margin, axis=axis) + leading
    middle_part = lax.slice_in_dim(centre, margin, length - margin, axis=axis)
    bottom_part = lax.slice_in_dim(centre, length - margin, length, axis=axis) + trailing
    return jnp.concatenate([top_part, middle_part, bottom_part], axis=axis)


def on_device(object_slices, probe_modes, patterns, positions, counts):
    slices = object_slices.shape[0]
    tile_cells = object_slices.shape[2]
    extent = probe_modes.shape[-1]
    margin = extent // 2
    per_device = patterns.shape[0]
    row_count = lax.axis_size("ty")
    column_count = lax.axis_size("tx")
    row_index = lax.axis_index("ty")
    column_index = lax.axis_index("tx")
    position_grid = positions.reshape(row_count, column_count, per_device, 2)
    column = lax.dynamic_index_in_dim(position_grid, column_index, axis=1, keepdims=False)
    count_grid = counts.reshape(row_count, column_count)
    column_counts = lax.dynamic_index_in_dim(count_grid, column_index, axis=1, keepdims=False)
    ordinal = jnp.arange(per_device, dtype=jnp.int32)
    is_live = ordinal[None, :] < column_counts[:, None]
    target = column[:, :, 0] // tile_cells
    earlier = ordinal[None, :] < ordinal[:, None]
    same_row = is_live[:, None, :] & (target[:, None, :] == target[:, :, None]) & earlier[None]
    row_rank = jnp.sum(same_row.astype(jnp.int32), axis=2)
    slot_count = row_count * CAP
    slot_ids = jnp.arange(slot_count, dtype=jnp.int32)
    own_live = lax.dynamic_index_in_dim(is_live, row_index, axis=0, keepdims=False)
    own_slot = lax.dynamic_index_in_dim(target * CAP + row_rank, row_index, axis=0, keepdims=False)
    choose = (own_live[None, :] & (own_slot[None, :] == slot_ids[:, None])).astype(jnp.bfloat16)
    outgoing = jnp.einsum(
        "sj,jab->sab", choose, patterns, preferred_element_type=jnp.float32
    ).astype(jnp.bfloat16)
    incoming = lax.all_to_all(outgoing, "ty", split_axis=0, concat_axis=0, tiled=True)
    rank_ids = jnp.arange(CAP, dtype=jnp.int32)
    matched = (
        is_live[:, None, :]
        & (target[:, None, :] == row_index)
        & (row_rank[:, None, :] == rank_ids[None, :, None])
    )
    slot_live = jnp.any(matched, axis=2).reshape(-1)
    chosen = matched.astype(jnp.int32)
    centre_row = jnp.sum(chosen * column[:, None, :, 0], axis=2).reshape(-1)
    centre_col = jnp.sum(chosen * column[:, None, :, 1], axis=2).reshape(-1)
    local_row = jnp.where(slot_live, centre_row - row_index * tile_cells, 0)
    local_col = jnp.where(slot_live, centre_col - column_index * tile_cells, 0)
    extended = extended_2(object_slices, (("ty", 2), ("tx", 3)), margin)
    tables = make_tables(extent)

    def visit_slot(running, element):
        gradient, probe_grad = running
        amplitude, row_start, col_start, live_flag = element
        corner = (jnp.int32(0), jnp.int32(0), row_start, col_start)
        window = lax.dynamic_slice(extended, corner, (slices, 2, extent, extent))
        slice_grads, probe_term = pattern_terms(
            window, amplitude.astype(jnp.float32), live_flag, probe_modes, tables
        )
        current = lax.dynamic_slice(gradient, corner, (slices, 2, extent, extent))
        gradient = lax.dynamic_update_slice(gradient, current + slice_grads, corner)
        return ((gradient, probe_grad + probe_term), None)

    span_cells = tile_cells + extent
    initial = (
        jnp.zeros((slices, 2, span_cells, span_cells), jnp.float32),
        jnp.zeros(probe_modes.shape, jnp.float32),
    )
    (gradient, probe_grad), unused = lax.scan(
        visit_slot, initial, (incoming, local_row, local_col, slot_live.astype(jnp.float32))
    )
    row_edges = jnp.concatenate([gradient[:, :, :margin], gradient[:, :, -margin:]], axis=2)
    row_halo = extended_2(row_edges, (("ty", 2),), margin)
    row_folded = settle(
        gradient[:, :, margin : margin + tile_cells],
        row_halo[:, :, :margin],
        row_halo[:, :, -margin:],
        2,
        margin,
    )
    col_edges = jnp.concatenate([row_folded[..., :margin], row_folded[..., -margin:]], axis=3)
    col_halo = extended_2(col_edges, (("tx", 3),), margin)
    folded = settle(
        row_folded[..., margin : margin + tile_cells],
        col_halo[..., :margin],
        col_halo[..., -margin:],
        3,
        margin,
    )
    probe_power = jnp.mean(jnp.sum(probe_modes**2, axis=(0, 1)))
    new_object = object_slices - folded / (probe_power + 1e-06)
    summed = lax.psum(probe_grad, ("ty", "tx"))
    spread = jnp.sqrt(jnp.mean(summed * summed) + 1e-06)
    new_probe = probe_modes - 0.5 * summed / spread
    return (new_object, new_probe)


def solution(mesh):
    return jax.shard_map(
        on_device,
        mesh=mesh,
        in_specs=(P(None, None, "ty", "tx"), P(), P(("ty", "tx"), None, None), P(), P()),
        out_specs=(P(None, None, "ty", "tx"), P()),
        check_vma=False,
    )
```

profile of v0, /device:TPU:0, one launch (start us, length us, event | category | flops | bytes accessed | tf_op | source)
XLA Modules:
  0.0 498.3 jit_solution(16212770416473145393)
XLA Ops:
  10.3 6.3 %all-to-all-start = ((bf16[8,128,128]{2,1,0:T(8,128)(2,1)}), bf16[8,128,128]{2,1,0:T(8,128)(2,1)}, u32[]{:S(2)}, u32[]{:S(2)}) async-start(bf16[8,128,128]{2,1,0:T(8,128)(2,1)} %copy.108), calls=%async_computation | async-start | bytes 524288 | tf_op jit(solution)/shard_map/all_to_all | solution.py:157
  18.0 4.0 collective-permute-start
  23.2 5.2 %copy.120 = f32[2,2,512,512]{2,3,1,0:T(8,128)} copy(f32[2,2,512,512]{3,2,1,0:T(8,128)} %param.7) | data formatting | bytes 8388608 | tf_op args[0]
  30.5 2.0 collective-permute-done
  32.8 4.0 collective-permute-done.1
  37.2 2.8 pad_maximum_fusion.4
  40.0 2.1 collective-permute-start.2
  47.4 5.9 %pad_maximum_fusion = f32[2,2,640,640]{2,3,1,0:T(8,128)} fusion(f32[2,2,640,64]{2,3,1,0:T(8,128)} %collective-permute-done.3, f32[2,2,64,512]{2,3,1,0:T(8,128)S(1)} %copy.106, f32[2,2,512,512]{2,3,1,0:T(8,128)} %copy.120, f32[2,2,64,512]{2,3,1,0:T(8,128)S(1)} %copy.104, f32[2,2,640,64]{2,3,1,0:T(8,128)} %collective-permute-done.2), kind=kLoop, calls=%fused_computation.110 | loop fusion | flops 6553600 | bytes 13107200 | tf_op jit(solution)/shard_map/concatenate | solution.py:23
  53.3 3.2 broadcast_in_dim.8
  56.5 217.3 %while.18 = (s32[]{:T(128)}, f32[2,2,640,640]{2,3,1,0:T(8,128)}, f32[4,2,128,128]{3,2,0,1:T(8,128)S(1)}, s32[8]{0:T(128)S(1)}, s32[8]{0:T(128)S(1)}, /*index=5*/...) while((s32[]{:T(128)}, f32[2,2,640,640]{2,3,1,0:T(8,128)}, ...), condition=%wide.region_8.9_spmd.clone.clone.clone.clone, body=%wide.region_4.8_spmd.clone.clone.clone.clone.sunk | while | flops 815677440 | bytes 33391468 | solution.py:190
  79.3 4.4 dynamic_update_slice.10
  106.5 4.4 dynamic_update_slice.10
  133.7 4.3 dynamic_update_slice.10
  160.8 4.3 dynamic_update_slice.10
  187.9 4.3 dynamic_update_slice.10
  215.0 4.4 dynamic_update_slice.10
  242.2 4.4 dynamic_update_slice.10
  269.4 4.3 dynamic_update_slice.10
  273.7 8.2 %copy.114 = f32[2,2,640,640]{3,2,1,0:T(8,128)} copy(f32[2,2,640,640]{2,3,1,0:T(8,128)} %get-tuple-element.206) | data formatting | bytes 13107200 | tf_op jit(solution)/shard_map/while | solution.py:190
  283.0 3.2 collective-permute-start.4
  286.2 8.0 %collective-permute-done.4 = f32[2,2,64,640]{3,2,1,0:T(8,128)S(1)} collective-permute-done((f32[2,2,64,640]{3,2,1,0:T(8,128)S(1)}, f32[2,2,64,640]{3,2,1,0:T(8,128)S(1)}, u32[]{:S(2)}, u32[]{:S(2)}) %collective-permute-start.4) | collective-permute-done | bytes 655392 | tf_op jit(solution)/shard_map/ppermute | solution.py:19
  294.3 2.3 slice_add_fusion.7
  298.0 4.2 slice.281
  302.6 7.1 %collective-permute-done.5 = f32[2,2,64,640]{3,2,1,0:T(8,128)S(1)} collective-permute-done((f32[2,2,64,640]{3,2,1,0:T(8,128)}, f32[2,2,64,640]{3,2,1,0:T(8,128)S(1)}, u32[]{:S(2)}, u32[]{:S(2)}) %collective-permute-start.5) | collective-permute-done | bytes 655392 | tf_op jit(solution)/shard_map/ppermute | solution.py:22
  313.2 2.0 pad_maximum_fusion.6
  315.2 13.6 %collective-permute-start.6 = (f32[2,2,512,64]{2,3,1,0:T(8,128)}, f32[2,2,512,64]{2,3,1,0:T(8,128)}, u32[]{:S(2)}, u32[]{:S(2)}) collective-permute-start(f32[2,2,512,64]{2,3,1,0:T(8,128)} %pad_maximum_fusion.6), channel_id=1, source_target_pairs={{0,1},{1,2},{2,3},{3,4},{4,5},{5,6},{6,7},{8,9},{9,10},{10,11},{11... | collective-permute-start | bytes 1572872 | tf_op jit(solution)/shard_map/ppermute | solution.py:19
  329.9 2.7 maximum_add_fusion.3
  333.8 136.1 %all-reduce.2.cloned.1.call-done = f32[4,2,128,128]{3,2,1,0:T(8,128)} async-done(((f32[4,2,128,128]{3,2,1,0:T(8,128)}), f32[4,2,128,128]{3,2,1,0:T(8,128)}) %all-reduce.2.cloned.1.call-update) | async-done | bytes 524304 | tf_op jit(solution)/shard_map/psum | solution.py:213
  472.4 2.5 divide_subtract_fusion
  475.5 3.9 pad_maximum_fusion.1
  483.2 3.0 fusion.85
  486.2 5.2 %copy.122 = f32[2,2,512,512]{3,2,1,0:T(8,128)} copy(f32[2,2,512,512]{2,3,1,0:T(8,128)} %fusion.85) | data formatting | bytes 8388608
  (387 shorter events, 177.6 us)
Async XLA Ops:
  7.2 2.1 copy-start
  10.3 43.0 %all-to-all-start = ((bf16[8,128,128]{2,1,0:T(8,128)(2,1)}), bf16[8,128,128]{2,1,0:T(8,128)(2,1)}, u32[]{:S(2)}, u32[]{:S(2)}) async-start(bf16[8,128,128]{2,1,0:T(8,128)(2,1)} %copy.108), calls=%async_computation | async-start | bytes 524288 | tf_op jit(solution)/shard_map/all_to_all | solution.py:157
  16.7 453.2 %all-reduce.2.cloned.1.call-start = ((), (), s32[]{:S(2)}) async-start(), calls=%async_computation.1 | async-start | bytes 1048576 | tf_op jit(solution)/shard_map/psum | solution.py:213
  18.0 14.5 %collective-permute-start = (f32[2,2,64,512]{3,2,1,0:T(8,128)S(1)}, f32[2,2,64,512]{3,2,1,0:T(8,128)S(1)}, u32[]{:S(2)}, u32[]{:S(2)}) collective-permute-start(f32[2,2,64,512]{3,2,1,0:T(8,128)S(1)} %get-tuple-element.545), channel_id=1, source_target_pairs={{0,8},{8,16},{16,24},{1,9},{9,17},{17,25},{2,10},{10,18},{18,26},{... | collective-permute-start | bytes 1572872 | tf_op jit(solution)/shard_map/ppermute | solution.py:19
  21.9 14.9 %collective-permute-start.1 = (f32[2,2,64,512]{3,2,1,0:T(8,128)S(1)}, f32[2,2,64,512]{3,2,1,0:T(8,128)S(1)}, u32[]{:S(2)}, u32[]{:S(2)}) collective-permute-start(f32[2,2,64,512]{3,2,1,0:T(8,128)S(1)} %get-tuple-element.546), channel_id=1, source_target_pairs={{8,0},{16,8},{24,16},{9,1},{17,9},{25,17},{10,2},{18,10},{26,18},{... | collective-permute-start | bytes 1572872 | tf_op jit(solution)/shard_map/ppermute | solution.py:22
  29.8 0.6 copy-start.10
  29.9 0.6 copy-start.12
  37.1 6.3 %copy-start.9 = (bf16[128,128]{1,0:T(8,128)(2,1)S(1)}, bf16[128,128]{1,0:T(8,128)(2,1)}, u32[]{:S(2)}) copy-start(bf16[128,128]{1,0:T(8,128)(2,1)} %copy-done.8) | copy-start | bytes 98308
  37.2 6.3 %copy-start.11 = (bf16[128,128]{1,0:T(8,128)(2,1)S(1)}, bf16[128,128]{1,0:T(8,128)(2,1)}, u32[]{:S(2)}) copy-start(bf16[128,128]{1,0:T(8,128)(2,1)} %copy-done.10) | copy-start | bytes 98308
  37.2 6.3 %copy-start.13 = (bf16[128,128]{1,0:T(8,128)(2,1)S(1)}, bf16[128,128]{1,0:T(8,128)(2,1)}, u32[]{:S(2)}) copy-start(bf16[128,128]{1,0:T(8,128)(2,1)} %copy-done.12) | copy-start | bytes 98308
  37.2 6.3 %copy-start.14 = (pred[4,2]{0,1:T(4,128)(4,1)S(1)}, pred[4,2]{0,1:T(4,128)(4,1)}, u32[]{:S(2)}) copy-start(pred[4,2]{0,1:T(4,128)(4,1)} %reduce_or.9) | copy-start | bytes 28
  37.2 6.3 %copy-start.5 = (f32[4,2,128,128]{3,2,1,0:T(8,128)S(1)}, f32[4,2,128,128]{3,2,1,0:T(8,128)}, u32[]{:S(2)}) copy-start(f32[4,2,128,128]{3,2,1,0:T(8,128)} %param.8) | copy-start | bytes 1572868
  40.0 6.6 %collective-permute-start.2 = (f32[2,2,640,64]{2,3,1,0:T(8,128)}, f32[2,2,640,64]{2,3,1,0:T(8,128)}, u32[]{:S(2)}, u32[]{:S(2)}) collective-permute-start(f32[2,2,640,64]{2,3,1,0:T(8,128)} %get-tuple-element.543), channel_id=1, source_target_pairs={{0,1},{1,2},{2,3},{3,4},{4,5},{5,6},{6,7},{8,9},{9,10},{10,11},{11... | collective-permute-start | bytes 1966088 | tf_op jit(solution)/shard_map/ppermute | solution.py:19
  42.1 5.2 %collective-permute-start.3 = (f32[2,2,640,64]{2,3,1,0:T(8,128)}, f32[2,2,640,64]{2,3,1,0:T(8,128)}, u32[]{:S(2)}, u32[]{:S(2)}) collective-permute-start(f32[2,2,640,64]{2,3,1,0:T(8,128)} %get-tuple-element.544), channel_id=1, source_target_pairs={{1,0},{2,1},{3,2},{4,3},{5,4},{6,5},{7,6},{9,8},{10,9},{11,10},{12... | collective-permute-start | bytes 1966088 | tf_op jit(solution)/shard_map/ppermute | solution.py:22
  53.3 3.2 copy-start.15
  75.3 2.3 copy-start.4
  102.5 2.3 copy-start.4
  129.7 2.3 copy-start.4
  156.8 2.3 copy-start.4
  184.0 2.3 copy-start.4
  211.1 2.3 copy-start.4
  238.2 2.3 copy-start.4
  265.4 2.3 copy-start.4
  283.0 11.2 %collective-permute-start.4 = (f32[2,2,64,640]{3,2,1,0:T(8,128)S(1)}, f32[2,2,64,640]{3,2,1,0:T(8,128)S(1)}, u32[]{:S(2)}, u32[]{:S(2)}) collective-permute-start(f32[2,2,64,640]{3,2,1,0:T(8,128)S(1)} %slice.455), channel_id=1, source_target_pairs={{0,8},{8,16},{16,24},{1,9},{9,17},{17,25},{2,10},{10,18},{18,26},{... | collective-permute-start | bytes 1966088 | tf_op jit(solution)/shard_map/ppermute | solution.py:19
  296.5 13.1 %collective-permute-start.5 = (f32[2,2,64,640]{3,2,1,0:T(8,128)}, f32[2,2,64,640]{3,2,1,0:T(8,128)S(1)}, u32[]{:S(2)}, u32[]{:S(2)}) collective-permute-start(f32[2,2,64,640]{3,2,1,0:T(8,128)} %get-tuple-element.542), channel_id=1, source_target_pairs={{8,0},{16,8},{24,16},{9,1},{17,9},{25,17},{10,2},{18,10},{26,18},{... | collective-permute-start | bytes 1966088 | tf_op jit(solution)/shard_map/ppermute | solution.py:22
  315.2 14.7 %collective-permute-start.6 = (f32[2,2,512,64]{2,3,1,0:T(8,128)}, f32[2,2,512,64]{2,3,1,0:T(8,128)}, u32[]{:S(2)}, u32[]{:S(2)}) collective-permute-start(f32[2,2,512,64]{2,3,1,0:T(8,128)} %pad_maximum_fusion.6), channel_id=1, source_target_pairs={{0,1},{1,2},{2,3},{3,4},{4,5},{5,6},{6,7},{8,9},{9,10},{10,11},{11... | collective-permute-start | bytes 1572872 | tf_op jit(solution)/shard_map/ppermute | solution.py:19
  329.7 142.7 %copy-start.6 = (f32[4,2,128,128]{3,2,1,0:T(8,128)S(1)}, f32[4,2,128,128]{3,2,1,0:T(8,128)}, u32[]{:S(2)}) copy-start(f32[4,2,128,128]{3,2,1,0:T(8,128)} %param.8) | copy-start | bytes 1572868
  332.5 147.2 %collective-permute-start.7 = (f32[2,2,512,64]{2,3,1,0:T(8,128)}, f32[2,2,512,64]{2,3,1,0:T(8,128)}, u32[]{:S(2)}, u32[]{:S(2)}) collective-permute-start(f32[2,2,512,64]{2,3,1,0:T(8,128)} %get-tuple-element.540), channel_id=1, source_target_pairs={{1,0},{2,1},{3,2},{4,3},{5,4},{6,5},{7,6},{9,8},{10,9},{11,10},{12... | collective-permute-start | bytes 1572872 | tf_op jit(solution)/shard_map/ppermute | solution.py:22
  479.4 2.1 copy-start.2
  479.7 3.5 copy-start.3
  479.7 3.5 copy-start.7
  483.2 8.2 %copy-start.1 = (bf16[8,128,128]{2,1,0:T(8,128)(2,1)S(1)}, bf16[8,128,128]{2,1,0:T(8,128)(2,1)}, u32[]{:S(2)}) copy-start(bf16[8,128,128]{2,1,0:T(8,128)(2,1)} %param.9) | copy-start | bytes 786436
  (1 other events, 0.6 us)
Sparse Core Ops, SparseCore 0:
  329.8 140.0 all-reduce.1
where the time goes:
time: 503 us; the launch traced here: 498 us
  waiting for transfers between devices  158 us (31%)
  local copies, waits for them, and re-layouts  119 us (24%)
  other arithmetic  88.5 us (18%)
  matrix products  49.7 us (10%)
  starting transfers between devices  34.6 us (7%)
  loops' own time  32.6 us (6%)
  between operations  15.8 us (3%)
    psum x1, waiting for transfers between devices, on_device(): summed = lax.psum(probe_grad, ('ty', 'tx'))  136 us
    dot_general x48, matrix products, transform(): jnp.einsum('ij,bjq->biq', left_table, partial_value, preferred_element_ty...  49.5 us
    dynamic_update_slice x8, local copies, waits for them, and re-layouts, visit_slot(): gradient = lax.dynamic_update_slice(gradient, current + slice_grads, corner)  34.8 us
    another operation x1, loops' own time, on_device(): lax.scan(visit_slot, initial, (incoming, local_row, local_col, slot_live....  32.6 us
    dynamic_slice x40, local copies, waits for them, and re-layouts, on_device(): lax.scan(visit_slot, initial, (incoming, local_row, local_col, slot_live....  26.4 us
    ppermute x4, starting transfers between devices, extended_2(): lax.ppermute(lax.slice_in_dim(block, block.shape[dim] - width, None, axis...  22.9 us
    squeeze x48, other arithmetic, transform(): joined = jnp.concatenate([rounded[:, 0], rounded[:, 1]], axis=-1)  20.9 us
    unnamed x33, local copies, waits for them, and re-layouts  12.9 us
  transfers between devices with their start and end apart: 10, of which 7 were waited for; matrix products, arithmetic and copies ran while one was open for 7% of the time, Pallas kernels for 0%

commit v1 on v0

v1 whole, which is shorter than its diff:
```python
import math

import numpy as np
import jax
import jax.numpy as jnp
from jax import lax
from jax.experimental import pallas as pl
from jax.experimental.pallas import tpu as pltpu
from jax.sharding import PartitionSpec as P

CAP = 2
PROPAGATION = 0.37
LANES = 128
BF16 = jnp.bfloat16
F32 = jnp.float32


def make_tables(extent):
    indices = np.arange(extent, dtype=np.int32)
    product = indices[:, None] * indices[None, :] % extent
    angles = np.float32(2.0 * math.pi / extent) * product.astype(np.float32)
    norm_scale = np.float32(1.0 / math.sqrt(extent))
    real_table = jnp.asarray(np.cos(angles) * norm_scale, F32).astype(BF16)
    imag_table = jnp.asarray(-np.sin(angles) * norm_scale, F32).astype(BF16)
    first = jnp.concatenate(
        [
            jnp.concatenate([real_table, imag_table], 1),
            jnp.concatenate([-imag_table, real_table], 1),
        ],
        0,
    )
    second = jnp.concatenate(
        [
            jnp.concatenate([real_table, -imag_table], 1),
            jnp.concatenate([imag_table, real_table], 1),
        ],
        0,
    )
    frequency = np.where(indices < extent // 2, indices, indices - extent).astype(np.float32)
    phases = np.float32(-math.pi * PROPAGATION / extent) * (
        frequency[:, None] ** 2 + frequency[None, :] ** 2
    )
    kernel = jnp.asarray(np.stack([np.cos(phases), np.sin(phases)]), F32)
    return first, second, kernel


def pairings(n):
    if n == 2:
        return [[1, 0]]
    assert n % 2 == 0 and all((n - 1) % d for d in range(2, n - 1))
    odd = n - 1
    rounds = []
    for k in range(odd):
        partner = [0] * n
        partner[odd], partner[k] = k, odd
        for i in range(1, n // 2):
            a, b = (k + i) % odd, (k - i) % odd
            partner[a], partner[b] = b, a
        rounds.append(partner)
    order = [odd]
    while len(order) < n:
        order.append(rounds[(len(order) - 1) % 2][order[-1]])
    label = {v: i for i, v in enumerate(order)}
    return [[label[r[order[i]]] for i in range(n)] for r in rounds]


def neighbour(side, i):
    return 1 if (i + side) % 2 == 0 else -1


def neighbour_pairs(side, n):
    steps = [(i, i + neighbour(side, i)) for i in range(n)]
    return [(i, j) for i, j in steps if 0 <= j < n]


def pick(index, values):
    chosen = jnp.int32(values[0])
    for i in range(1, len(values)):
        chosen = jnp.where(index == i, jnp.int32(values[i]), chosen)
    return chosen


def lane_ids(rows):
    return lax.broadcasted_iota(jnp.int32, (rows, LANES), 1)


def half_mask(rows, upper):
    return (lane_ids(rows) >= LANES // 2).astype(jnp.int32) == upper


def ups(index):
    even = 1 - lax.rem(index, 2)
    return [even, 1 - even]


def pack_kernel(sizes, obj, pat, pos, cnt, *outs):
    n_ty, n_tx, rounds = sizes
    ty_out, tx_out, diag_out = outs[: len(rounds)], outs[len(rounds) : len(rounds) + 2], outs[len(rounds) + 2 :]
    slices, tile, extent = obj.shape[0], obj.shape[2], pat.shape[1]
    margin, tiles = extent // 2, obj.shape[3] // LANES
    row, col = lax.axis_index("ty"), lax.axis_index("tx")
    up_y, up_x = ups(row), ups(col)
    base = (row * n_tx + col) * pat.shape[0]
    count = cnt[row * n_tx + col]
    parts = slices * 2 * tiles
    for k, partner in enumerate(rounds):
        out = ty_out[k]
        if k < 2:
            start = pl.multiple_of(up_y[k] * (tile - margin), margin)
            nxt = row + 2 * up_y[k] - 1
            keep = jnp.where((nxt >= 0) & (nxt < n_ty), 1.0, 0.0).astype(F32)
            for p in range(slices * 2):
                for t in range(tiles):
                    block = obj[p // 2, p % 2, pl.ds(start, margin), t * LANES : (t + 1) * LANES]
                    out[p * tiles + t] = (block * keep).astype(BF16)
        low = pick(row, partner) * tile
        found = [jnp.int32(0)] * CAP
        seen = jnp.int32(0)
        for i in range(pat.shape[0]):
            y = pos[base + i, 0]
            hit = (i < count) & (y >= low) & (y < low + tile)
            for c in range(CAP):
                found[c] = jnp.where(hit & (seen == c), i, found[c])
            seen = seen + hit.astype(jnp.int32)
        first = parts if k < 2 else 0
        for c in range(CAP):
            for h in range(2):
                out[first + 2 * c + h] = pat[found[c], h * margin : (h + 1) * margin, :]
    for j in range(2):
        lane = pl.multiple_of(up_x[j] * (tile - LANES), LANES)
        for s in range(slices):
            re = obj[s, 0, :, pl.ds(lane, LANES)]
            im = obj[s, 1, :, pl.ds(lane, LANES)]
            packed = jnp.where(half_mask(tile, up_x[j]), re, pltpu.roll(im, LANES // 2, 1))
            tx_out[j][s] = packed.astype(BF16)
            for k in range(2):
                start = pl.multiple_of(up_y[k] * (tile - margin), margin)
                re = obj[s, 0, pl.ds(start, margin), pl.ds(lane, LANES)]
                im = obj[s, 1, pl.ds(start, margin), pl.ds(lane, LANES)]
                packed = jnp.where(half_mask(margin, up_x[j]), re, pltpu.roll(im, LANES // 2, 1))
                diag_out[2 * k + j][s] = packed.astype(BF16)


def cmul(a, b):
    return a[0] * b[0] - a[1] * b[1], a[0] * b[1] + a[1] * b[0]


def cmul_conj(a, b):
    return a[0] * b[0] + a[1] * b[1], a[0] * b[1] - a[1] * b[0]


def transform(fields, right, left):
    extent = fields[0][0].shape[0]
    joined = jnp.concatenate([jnp.concatenate([re, im], 1) for re, im in fields], 0).astype(BF16)
    half = jnp.dot(joined, right, preferred_element_type=F32).astype(BF16)
    blocks = []
    for m in range(len(fields)):
        part = half[m * extent : (m + 1) * extent]
        blocks.append(jnp.concatenate([part[:, :extent], part[:, extent:]], 0))
    whole = jnp.dot(left, jnp.concatenate(blocks, 1), preferred_element_type=F32)
    return [
        (whole[:extent, m * extent : (m + 1) * extent], whole[extent:, m * extent : (m + 1) * extent])
        for m in range(len(fields))
    ]


def main_kernel(sizes, obj, pat, pos, cnt, probe, first, second, kern, *refs):
    n_ty, n_tx, rounds = sizes
    k_n = len(rounds)
    ty_in, tx_in, diag_in = refs[:k_n], refs[k_n : k_n + 2], refs[k_n + 2 : k_n + 6]
    refs = refs[k_n + 6 :]
    grad, probe_grad, ty_out, tx_out, diag_out = refs[0], refs[1], refs[2:4], refs[4:6], refs[6:10]
    ext, amp, acc, row_of, col_of, live_of = refs[10:]
    slices, tile, extent = obj.shape[0], obj.shape[2], pat.shape[1]
    modes = probe.shape[0]
    margin, tiles = extent // 2, obj.shape[3] // LANES
    parts = slices * 2 * tiles
    per_device = pat.shape[0]
    row, col = lax.axis_index("ty"), lax.axis_index("tx")
    up_y, up_x = ups(row), ups(col)

    low, left = row * tile, col * tile
    for k in range(k_n + 1):
        source = row if k == 0 else pick(row, rounds[k - 1])
        base = (source * n_tx + col) * per_device
        count = cnt[source * n_tx + col]
        ys, xs = [jnp.int32(0)] * CAP, [jnp.int32(0)] * CAP
        lives, found = [jnp.float32(0)] * CAP, [jnp.int32(0)] * CAP
        seen = jnp.int32(0)
        for i in range(per_device):
            y, x = pos[base + i, 0], pos[base + i, 1]
            hit = (i < count) & (y >= low) & (y < low + tile)
            for c in range(CAP):
                this = hit & (seen == c)
                ys[c] = jnp.where(this, y - low, ys[c])
                xs[c] = jnp.where(this, x - left, xs[c])
                lives[c] = jnp.where(this, 1.0, lives[c])
                found[c] = jnp.where(this, i, found[c])
            seen = seen + hit.astype(jnp.int32)
        for c in range(CAP):
            slot = k * CAP + c
            row_of[slot], col_of[slot], live_of[slot] = ys[c], xs[c], lives[c]
            if k == 0:
                amp[slot] = pat[found[c]]
            else:
                start = (parts if k < 3 else 0) + 2 * c
                for h in range(2):
                    amp[slot, h * margin : (h + 1) * margin] = ty_in[k - 1][start + h]

    for p in range(slices * 2):
        for t in range(tiles):
            ext[p, 1 + t, margin : margin + tile] = obj[p // 2, p % 2, :, t * LANES : (t + 1) * LANES]
            for k in range(2):
                start = pl.multiple_of(up_y[k] * (tile + margin), margin)
                ext[p, 1 + t, pl.ds(start, margin)] = ty_in[k][p * tiles + t].astype(F32)
    for s in range(slices):
        for j in range(2):
            side = up_x[j] * (tiles + 1)
            strip = tx_in[j][s].astype(F32)
            ext[2 * s, side, margin : margin + tile] = strip
            ext[2 * s + 1, side, margin : margin + tile] = pltpu.roll(strip, LANES // 2, 1)
            for k in range(2):
                start = pl.multiple_of(up_y[k] * (tile + margin), margin)
                strip = diag_in[2 * k + j][s].astype(F32)
                ext[2 * s, side, pl.ds(start, margin)] = strip
                ext[2 * s + 1, side, pl.ds(start, margin)] = pltpu.roll(strip, LANES // 2, 1)
    grad[...] = jnp.zeros(grad.shape, F32)
    acc[...] = jnp.zeros(acc.shape, F32)

    lanes = lane_ids(extent)

    def visit(slot):
        y = row_of[slot]
        x = col_of[slot] + margin
        side = lax.shift_right_logical(x, 7)
        off = x & (LANES - 1)
        upper = lanes >= off
        back = (LANES - off) & (LANES - 1)

        def window(p):
            v0 = ext[p, side, pl.ds(y, extent), :]
            v1 = ext[p, side + 1, pl.ds(y, extent), :]
            return pltpu.roll(jnp.where(upper, v0, v1), back, 1)

        def scatter(p, value):
            moved = pltpu.roll(value, off, 1)
            grad[p, side, pl.ds(y, extent), :] += jnp.where(upper, moved, 0.0)
            grad[p, side + 1, pl.ds(y, extent), :] += jnp.where(upper, 0.0, moved)

        p_tab, q_tab = first[...], second[...]
        prop = (kern[0], kern[1])
        waves = [(probe[m, 0], probe[m, 1]) for m in range(modes)]
        inputs = [waves]
        cells = []
        for s in range(slices):
            cells.append((window(2 * s), window(2 * s + 1)))
            exits = [cmul(w, cells[s]) for w in inputs[s]]
            far = transform(exits, p_tab, q_tab)
            if s + 1 < slices:
                inputs.append(transform([cmul(prop, f) for f in far], q_tab, p_tab))
        total = far[0][0] * far[0][0] + far[0][1] * far[0][1]
        for re, im in far[1:]:
            total = total + (re * re + im * im)
        scale = amp[slot].astype(F32) * lax.rsqrt(jnp.maximum(total, 0.25))
        factor = (1.0 - scale) * live_of[slot]
        back_waves = transform([(re * factor, im * factor) for re, im in far], q_tab, p_tab)
        for s in reversed(range(slices)):
            q_re, q_im = cmul_conj(inputs[s][0], back_waves[0])
            for m in range(1, modes):
                re, im = cmul_conj(inputs[s][m], back_waves[m])
                q_re, q_im = q_re + re, q_im + im
            scatter(2 * s, q_re)
            scatter(2 * s + 1, q_im)
            terms = [cmul_conj(cells[s], g) for g in back_waves]
            if s > 0:
                inner = transform(terms, p_tab, q_tab)
                back_waves = transform([cmul_conj(prop, f) for f in inner], q_tab, p_tab)
        for m in range(modes):
            acc[2 * m] += terms[m][0]
            acc[2 * m + 1] += terms[m][1]

    def body(i, carry):
        visit(i)
        return carry

    lax.fori_loop(0, (k_n + 1) * CAP, body, 0)

    per_chunk = probe_grad.shape[1]
    flat_rows = extent // per_chunk if per_chunk < extent else 1
    for q in range(2 * modes):
        value = acc[q].astype(BF16)
        for f in range(flat_rows):
            at = q * extent + f * per_chunk if flat_rows > 1 else q * extent
            width = per_chunk if flat_rows > 1 else extent
            probe_grad[at // per_chunk, at % per_chunk : at % per_chunk + width] = value[
                f * width : (f + 1) * width
            ]
    for k in range(2):
        start = pl.multiple_of(up_y[k] * (tile + margin), margin)
        for p in range(slices * 2):
            for t in range(tiles):
                ty_out[k][p * tiles + t] = grad[p, 1 + t, pl.ds(start, margin)].astype(BF16)
    for s in range(slices):
        for j in range(2):
            side = up_x[j] * (tiles + 1)
            re = grad[2 * s, side, margin : margin + tile]
            im = grad[2 * s + 1, side, margin : margin + tile]
            mask = half_mask(tile, 1 - up_x[j])
            tx_out[j][s] = jnp.where(mask, re, pltpu.roll(im, LANES // 2, 1)).astype(BF16)
            for k in range(2):
                start = pl.multiple_of(up_y[k] * (tile + margin), margin)
                re = grad[2 * s, side, pl.ds(start, margin)]
                im = grad[2 * s + 1, side, pl.ds(start, margin)]
                mask = half_mask(margin, 1 - up_x[j])
                diag_out[2 * k + j][s] = jnp.where(mask, re, pltpu.roll(im, LANES // 2, 1)).astype(BF16)


def update_kernel(obj, grad, probe, *refs):
    ty_in, tx_in, diag_in, out = refs[:2], refs[2:4], refs[4:8], refs[8]
    slices, tile, extent = obj.shape[0], obj.shape[2], probe.shape[2]
    margin, tiles = extent // 2, obj.shape[3] // LANES
    row, col = lax.axis_index("ty"), lax.axis_index("tx")
    up_y, up_x = ups(row), ups(col)
    power = jnp.sum(probe[...] * probe[...]) / (extent * extent)
    rate = jnp.full((1, 1), 1.0, F32) / (power + 1e-06)
    for p in range(slices * 2):
        for t in range(tiles):
            span = slice(t * LANES, (t + 1) * LANES)
            piece = grad[p, 1 + t, margin : margin + tile]
            out[p // 2, p % 2, :, span] = obj[p // 2, p % 2, :, span] - piece * rate
    for p in range(slices * 2):
        for k in range(2):
            start = pl.multiple_of(up_y[k] * (tile - margin), margin)
            for t in range(tiles):
                span = slice(t * LANES, (t + 1) * LANES)
                out[p // 2, p % 2, pl.ds(start, margin), span] -= (
                    ty_in[k][p * tiles + t].astype(F32) * rate
                )
    for s in range(slices):
        for j in range(2):
            lane = pl.multiple_of(up_x[j] * (tile - LANES), LANES)
            strip = tx_in[j][s].astype(F32) * rate
            mask = half_mask(tile, up_x[j])
            out[s, 0, :, pl.ds(lane, LANES)] -= jnp.where(mask, strip, 0.0)
            out[s, 1, :, pl.ds(lane, LANES)] -= jnp.where(mask, pltpu.roll(strip, LANES // 2, 1), 0.0)
            for k in range(2):
                start = pl.multiple_of(up_y[k] * (tile - margin), margin)
                strip = diag_in[2 * k + j][s].astype(F32) * rate
                mask = half_mask(margin, up_x[j])
                out[s, 0, pl.ds(start, margin), pl.ds(lane, LANES)] -= jnp.where(mask, strip, 0.0)
                out[s, 1, pl.ds(start, margin), pl.ds(lane, LANES)] -= jnp.where(
                    mask, pltpu.roll(strip, LANES // 2, 1), 0.0
                )


def sum_kernel(sizes, own, *refs):
    rounds = sizes[2]
    parts, out, held = refs[: len(rounds)], refs[len(rounds)], refs[len(rounds) + 1]
    row = lax.axis_index("ty")
    held[row] = own[...]
    for k, partner in enumerate(rounds):
        held[pick(row, partner)] = parts[k][...]
    total = held[0]
    for i in range(1, held.shape[0]):
        total = total + held[i]
    out[...] = total.astype(out.dtype)


def probe_kernel(probe, gathered, out):
    modes, extent = probe.shape[0], probe.shape[2]
    summed = gathered[...].astype(F32)
    mean = jnp.sum(summed * summed) / summed.size
    rate = jnp.full((1, 1), 0.5, F32) * lax.rsqrt(jnp.full((1, 1), 1.0, F32) * (mean + 1e-06))
    for m in range(modes):
        for c in range(2):
            at = (2 * m + c) * extent
            out[m, c] = probe[m, c] - gathered[at : at + extent].astype(F32) * rate


VMEM = pl.BlockSpec(memory_space=pltpu.VMEM)
SMEM = pl.BlockSpec(memory_space=pltpu.SMEM)


def call(kernel, name, operands, specs, outs, scratch=()):
    return pl.pallas_call(
        kernel,
        out_shape=outs,
        in_specs=specs,
        out_specs=[VMEM] * len(outs) if isinstance(outs, (list, tuple)) else VMEM,
        scratch_shapes=list(scratch),
        compiler_params=pltpu.CompilerParams(vmem_limit_bytes=56 * 1024 * 1024),
        name=name,
    )(*operands)


def swap(value, axis, side):
    return lax.ppermute(value, axis, neighbour_pairs(side, lax.axis_size(axis)))


def swap_diagonal(value, side_y, side_x):
    n_ty, n_tx = lax.axis_size("ty"), lax.axis_size("tx")
    pairs = [
        (y0 * n_tx + x0, y1 * n_tx + x1)
        for y0, y1 in neighbour_pairs(side_y, n_ty)
        for x0, x1 in neighbour_pairs(side_x, n_tx)
    ]
    return lax.ppermute(value, ("ty", "tx"), pairs)


def on_device(object_slices, probe_modes, patterns, positions, counts):
    slices, _, tile, _ = object_slices.shape
    modes, _, extent, _ = probe_modes.shape
    margin, tiles = extent // 2, tile // LANES
    n_ty, n_tx = lax.axis_size("ty"), lax.axis_size("tx")
    rounds = pairings(n_ty)
    sizes = (n_ty, n_tx, rounds)
    parts = slices * 2 * tiles
    struct = jax.ShapeDtypeStruct
    strips = [struct((slices, tile, LANES), BF16)] * 2
    corners = [struct((slices, margin, LANES), BF16)] * 4
    k_n = len(rounds)
    packed = call(
        lambda *r: pack_kernel(sizes, *r),
        "pack",
        (object_slices, patterns, positions, counts),
        [VMEM, VMEM, SMEM, SMEM],
        [struct(((parts if k < 2 else 0) + 2 * CAP, margin, LANES), BF16) for k in range(k_n)]
        + strips
        + corners,
    )
    ty_in = [
        lax.ppermute(packed[k], "ty", [(i, rounds[k][i]) for i in range(n_ty)]) for k in range(k_n)
    ]
    tx_in = [swap(packed[k_n + j], "tx", j) for j in range(2)]
    diag_in = [swap_diagonal(packed[k_n + 2 + q], q // 2, q % 2) for q in range(4)]

    first, second, kern = make_tables(extent)
    slots = (k_n + 1) * CAP
    ext_shape = (slices * 2, tiles + 2, tile + extent, LANES)
    chunk = modes * 2 * extent // n_tx
    results = call(
        lambda *r: main_kernel(sizes, *r),
        "patterns",
        (object_slices, patterns, positions, counts, probe_modes, first, second, kern)
        + tuple(ty_in + tx_in + diag_in),
        [VMEM, VMEM, SMEM, SMEM] + [VMEM] * (4 + k_n + 6),
        [struct(ext_shape, F32), struct((n_tx, chunk, LANES), BF16)]
        + [struct((parts, margin, LANES), BF16)] * 2
        + strips
        + corners,
        [
            pltpu.VMEM(ext_shape, F32),
            pltpu.VMEM((slots, extent, extent), BF16),
            pltpu.VMEM((2 * modes, extent, extent), F32),
            pltpu.SMEM((slots,), jnp.int32),
            pltpu.SMEM((slots,), jnp.int32),
            pltpu.SMEM((slots,), F32),
        ],
    )
    grad, probe_grad = results[0], results[1]
    ty_back = [swap(results[2 + k], "ty", k) for k in range(2)]
    tx_back = [swap(results[4 + j], "tx", j) for j in range(2)]
    diag_back = [swap_diagonal(results[6 + q], q // 2, q % 2) for q in range(4)]

    shares = lax.all_to_all(probe_grad, "tx", split_axis=0, concat_axis=0, tiled=True)
    mine = jnp.sum(shares.astype(F32), axis=0)
    others = [
        lax.ppermute(mine, "ty", [(i, rounds[k][i]) for i in range(n_ty)]) for k in range(k_n)
    ]
    full = call(
        lambda *r: sum_kernel(sizes, *r),
        "sum_rows",
        tuple([mine] + others),
        [VMEM] * (k_n + 1),
        struct((chunk, LANES), BF16),
        [pltpu.VMEM((n_ty, chunk, LANES), F32)],
    )
    gathered = lax.all_gather(full, "tx", axis=0, tiled=True)
    new_object = call(
        update_kernel,
        "update",
        (object_slices, grad, probe_modes) + tuple(ty_back + tx_back + diag_back),
        [VMEM] * 11,
        struct(object_slices.shape, F32),
    )
    new_probe = call(
        probe_kernel,
        "probe",
        (probe_modes, gathered),
        [VMEM] * 2,
        struct(probe_modes.shape, F32),
    )
    return (new_object, new_probe)


def solution(mesh):
    return jax.shard_map(
        on_device,
        mesh=mesh,
        in_specs=(P(None, None, "ty", "tx"), P(), P(("ty", "tx"), None, None), P(), P()),
        out_specs=(P(None, None, "ty", "tx"), P()),
        check_vma=False,
    )
```

time: 503 us -> 142 us (0.28)
  waiting for transfers between devices: 158 us -> 15.2 us
  local copies, waits for them, and re-layouts: 119 us -> 5.05 us
  other arithmetic: 88.5 us -> 0.04 us
  matrix products: 49.7 us -> 0 us
  Pallas kernels: 0 us -> 45.4 us
  loops' own time: 32.6 us -> 0 us
  starting transfers between devices: 34.6 us -> 56.2 us
  blocking collectives: 0 us -> 18.2 us
  between operations: 15.8 us -> 1 us
    psum x1 -> x0, waiting for transfers between devices: 136 us -> none  [on_device(): summed = lax.psum(probe_grad, ('ty', 'tx'))]
    dot_general x49 -> x0, matrix products: 49.7 us -> none  [the longest x48 49.5 us: transform(): jnp.einsum('ij,bjq->biq', left_table, partial_value, preferred_element_ty...]
    pallas_call x0 -> x5, Pallas kernels: none -> 45.4 us  [call(): pl.pallas_call(kernel, out_shape=outs, in_specs=specs, out_specs=[VMEM] *...]
    dynamic_update_slice x8 -> x0, local copies, waits for them, and re-layouts: 34.8 us -> none  [visit_slot(): gradient = lax.dynamic_update_slice(gradient, current + slice_grads, corner)]
    another operation x1 -> x0, loops' own time: 32.6 us -> none  [on_device(): lax.scan(visit_slot, initial, (incoming, local_row, local_col, slot_live....]
    dynamic_slice x42 -> x0, local copies, waits for them, and re-layouts: 26.6 us -> none  [the longest x40 26.4 us: on_device(): lax.scan(visit_slot, initial, (incoming, local_row, local_col, slot_live....]
    squeeze x48 -> x0, other arithmetic: 20.9 us -> none  [transform(): joined = jnp.concatenate([rounded[:, 0], rounded[:, 1]], axis=-1)]
    mul x16 -> x0, other arithmetic: 19.2 us -> none  [the longest x8 11.6 us: pattern_terms(): (1.0 - amplitude / jnp.sqrt(jnp.maximum(intensity, 0.25))) * live_flag]
  transfers between devices with their start and end apart: 10 -> 21, of which waited for: 7 -> 3; matrix products, arithmetic and copies ran while one was open for 7% -> 0% of each run, Pallas kernels for 0% -> 6%
where the time goes in v1:
time: 142 us; the launch traced here: 141 us
  starting transfers between devices  56.2 us (40%)
  Pallas kernels  45.4 us (32%)
  blocking collectives  18.2 us (13%)
  waiting for transfers between devices  15.2 us (11%)
  local copies, waits for them, and re-layouts  5.05 us (4%)
    pallas_call x5, Pallas kernels, call(): pl.pallas_call(kernel, out_shape=outs, in_specs=specs, out_specs=[VMEM] *...  45.4 us
    all_gather x1, blocking collectives, on_device(): gathered = lax.all_gather(full, 'tx', axis=0, tiled=True)  18.2 us
    ppermute x3, starting transfers between devices, on_device(): lax.ppermute(packed[k], 'ty', [(i, rounds[k][i]) for i in range(n_ty)])  17.8 us
    ppermute x3, starting transfers between devices, on_device(): lax.ppermute(mine, 'ty', [(i, rounds[k][i]) for i in range(n_ty)])  13.1 us
    ppermute x8, waiting for transfers between devices, swap_diagonal(): return lax.ppermute(value, ('ty', 'tx'), pairs)  12.7 us
    all_to_all x1, starting transfers between devices, on_device(): lax.all_to_all(probe_grad, 'tx', split_axis=0, concat_axis=0, tiled=True)  12.3 us
    ppermute x8, starting transfers between devices, swap_diagonal(): return lax.ppermute(value, ('ty', 'tx'), pairs)  9.92 us
    unnamed x43, local copies, waits for them, and re-layouts  5.05 us
  transfers between devices with their start and end apart: 21, of which 3 were waited for; matrix products, arithmetic and copies ran while one was open for 0% of the time, Pallas kernels for 6%

profile of v1, /device:TPU:0, one launch (start us, length us, event | category | flops | bytes accessed | tf_op | source)
XLA Modules:
  0.0 141.1 jit_solution(6183257706531002067)
XLA Ops:
  0.6 1.5 %copy.11.r_2_ = s32[256,2]{1,0:T(8,128)} copy(s32[256,2]{0,1:T(2,128)} %param.11) | data formatting | bytes 4096 | tf_op args[3]
  2.1 4.4 %pack.1 = (bf16[20,64,128]{2,1,0:T(8,128)(2,1)}, bf16[20,64,128]{2,1,0:T(8,128)(2,1)}, bf16[4,64,128]{2,1,0:T(8,128)(2,1)}, bf16[2,512,128]{2,1,0:T(8,128)(2,1)}...) custom-call(f32[2,2,512,512]{3,2,1,0:T(8,128)} %obj.1, ...), custom_call_target="tpu_custom_call" | custom-call | tf_op jit(solution)/shard_map/pack/pallas_call | solution.py:385
  6.5 3.1 %collective-permute-start = (bf16[20,64,128]{2,1,0:T(8,128)(2,1)}, bf16[20,64,128]{2,1,0:T(8,128)(2,1)S(1)}, u32[]{:S(2)}, u32[]{:S(2)}) collective-permute-start(bf16[20,64,128]{2,1,0:T(8,128)(2,1)} %get-tuple-element.21), channel_id=1, source_target_pairs={{0,8},{8,0},{16,24},{24,16},{1,9},{9,1},{17,25},{25,17},{2,10},{10... | collective-permute-start | bytes 983048 | tf_op jit(solution)/shard_map/ppermute | solution.py:432
  9.6 2.5 %collective-permute-start.1 = (bf16[20,64,128]{2,1,0:T(8,128)(2,1)}, bf16[20,64,128]{2,1,0:T(8,128)(2,1)S(1)}, u32[]{:S(2)}, u32[]{:S(2)}) collective-permute-start(bf16[20,64,128]{2,1,0:T(8,128)(2,1)} %get-tuple-element.22), channel_id=1, source_target_pairs={{0,24},{8,16},{16,8},{24,0},{1,25},{9,17},{17,9},{25,1},{2,26},{10... | collective-permute-start | bytes 983048 | tf_op jit(solution)/shard_map/ppermute | solution.py:432
  12.1 0.7 collective-permute-start.4
  12.7 3.2 %collective-permute-start.5 = (bf16[2,64,128]{2,1,0:T(8,128)(2,1)}, bf16[2,64,128]{2,1,0:T(8,128)(2,1)S(1)}, u32[]{:S(2)}, u32[]{:S(2)}) collective-permute-start(bf16[2,64,128]{2,1,0:T(8,128)(2,1)} %get-tuple-element.26), channel_id=1, source_target_pairs={{0,9},{1,8},{2,11},{3,10},{4,13},{5,12},{6,15},{7,14},{8,1},{9,0},... | collective-permute-start | bytes 98312 | tf_op jit(solution)/shard_map/ppermute | solution.py:407
  15.9 8.7 %collective-permute-done.5.r_13_ = bf16[2,64,128]{2,1,0:T(8,128)(2,1)S(1)} collective-permute-done((bf16[2,64,128]{2,1,0:T(8,128)(2,1)}, bf16[2,64,128]{2,1,0:T(8,128)(2,1)S(1)}, u32[]{:S(2)}, u32[]{:S(2)}) %collective-permute-start.5) | collective-permute-done | bytes 32800 | tf_op jit(solution)/shard_map/ppermute | solution.py:407
  24.6 0.7 collective-permute-start.6
  25.3 0.7 collective-permute-start.7
  26.0 0.7 collective-permute-start.8
  26.7 12.3 %collective-permute-start.2 = (bf16[4,64,128]{2,1,0:T(8,128)(2,1)}, bf16[4,64,128]{2,1,0:T(8,128)(2,1)S(1)}, u32[]{:S(2)}, u32[]{:S(2)}) collective-permute-start(bf16[4,64,128]{2,1,0:T(8,128)(2,1)} %get-tuple-element.23), channel_id=1, source_target_pairs={{0,16},{8,24},{16,0},{24,8},{1,17},{9,25},{17,1},{25,9},{2,18},{10... | collective-permute-start | bytes 196616 | tf_op jit(solution)/shard_map/ppermute | solution.py:432
  39.0 2.5 %collective-permute-done.2.r_10_ = bf16[4,64,128]{2,1,0:T(8,128)(2,1)S(1)} collective-permute-done((bf16[4,64,128]{2,1,0:T(8,128)(2,1)}, bf16[4,64,128]{2,1,0:T(8,128)(2,1)S(1)}, u32[]{:S(2)}, u32[]{:S(2)}) %collective-permute-start.2) | collective-permute-done | bytes 65568 | tf_op jit(solution)/shard_map/ppermute | solution.py:432
  41.5 0.5 copy-done.9
  42.3 0.7 copy-done.1
  43.1 28.5 %patterns.1 = (f32[4,6,640,128]{3,2,1,0:T(8,128)}, bf16[8,128,128]{2,1,0:T(8,128)(2,1)}, bf16[16,64,128]{2,1,0:T(8,128)(2,1)}, bf16[16,64,128]{2,1,0:T(8,128)(2,...) custom-call(f32[2,2,512,512]{3,2,1,0:T(8,128)} %obj.1, ...), custom_call_target="tpu_custom_call" | custom-call | tf_op jit(solution)/shard_map/patterns/pallas_call | solution.py:385
  71.6 12.3 %all-to-all-start = ((bf16[8,128,128]{2,1,0:T(8,128)(2,1)}), bf16[8,128,128]{2,1,0:T(8,128)(2,1)S(1)}, u32[]{:S(2)}, u32[]{:S(2)}) async-start(bf16[8,128,128]{2,1,0:T(8,128)(2,1)} %get-tuple-element.39), calls=%async_computation | async-start | bytes 524288 | tf_op jit(solution)/shard_map/all_to_all | solution.py:465
  83.9 0.8 collective-permute-start.9
  84.6 0.7 collective-permute-start.10
  85.3 2.8 %collective-permute-start.13 = (bf16[2,64,128]{2,1,0:T(8,128)(2,1)}, bf16[2,64,128]{2,1,0:T(8,128)(2,1)S(1)}, u32[]{:S(2)}, u32[]{:S(2)}) collective-permute-start(bf16[2,64,128]{2,1,0:T(8,128)(2,1)} %get-tuple-element.35), channel_id=1, source_target_pairs={{0,9},{1,8},{2,11},{3,10},{4,13},{5,12},{6,15},{7,14},{8,1},{9,0},... | collective-permute-start | bytes 98312 | tf_op jit(solution)/shard_map/ppermute | solution.py:407
  88.4 0.7 collective-permute-start.12
  89.1 4.0 %collective-permute-done.13.refs_4_ = bf16[2,64,128]{2,1,0:T(8,128)(2,1)S(1)} collective-permute-done((bf16[2,64,128]{2,1,0:T(8,128)(2,1)}, bf16[2,64,128]{2,1,0:T(8,128)(2,1)S(1)}, u32[]{:S(2)}, u32[]{:S(2)}) %collective-permute-start.13) | collective-permute-done | bytes 32800 | tf_op jit(solution)/shard_map/ppermute | solution.py:407
  93.1 0.7 collective-permute-start.14
  93.7 0.7 collective-permute-start.15
  94.4 0.7 collective-permute-start.16
  95.2 11.5 %collective-permute-start.17 = (f32[128,128]{1,0:T(8,128)S(1)}, f32[128,128]{1,0:T(8,128)S(1)}, u32[]{:S(2)}, u32[]{:S(2)}) collective-permute-start(f32[128,128]{1,0:T(8,128)S(1)} %convert_reduce_fusion.r_0_), channel_id=1, source_target_pairs={{0,8},{8,0},{16,24},{24,16},{1,9},{9,1},{17,25},{25,17},{2,10},{10... | collective-permute-start | bytes 196616 | tf_op jit(solution)/shard_map/ppermute | solution.py:468
  106.7 1.4 collective-permute-start.18
  109.1 8.7 %update.1 = f32[2,2,512,512]{3,2,1,0:T(8,128)} custom-call(f32[2,2,512,512]{3,2,1,0:T(8,128)} %obj.1, f32[4,6,640,128]{3,2,1,0:T(8,128)} %get-tuple-element.30.grad, f32[4,2,128,128]{3,2,1,0:T(8,128)} %probe.5, bf16[16,64,128]{2,1,0:T(8,128)(2,1)} %copy-done.2, bf16[16,64,128]{2,1,0:T(8,128)(2,1)} %copy-done.3, bf16[2,512,128]{2,1,0:T(8,128)(2,1)} %copy-done.4, ...), custom_call_target="tpu_custom_call" | custom-call | tf_op jit(solution)/shard_map/update/pallas_call | solution.py:385
  117.9 0.6 copy-done.10
  118.5 0.6 copy-done.12
  119.1 1.6 %sum_rows.1 = bf16[128,128]{1,0:T(8,128)(2,1)} custom-call(f32[128,128]{1,0:T(8,128)} %copy-done.8, f32[128,128]{1,0:T(8,128)} %copy-done.10, f32[128,128]{1,0:T(8,128)} %copy-done.11, f32[128,128]{1,0:T(8,128)} %copy-done.12), custom_call_target="tpu_custom_call" | custom-call | tf_op jit(solution)/shard_map/sum_rows/pallas_call | solution.py:385
  120.7 18.2 %all_gather.3.gathered = bf16[1024,128]{1,0:T(8,128)(2,1)} all-gather(bf16[128,128]{1,0:T(8,128)(2,1)} %sum_rows.1), channel_id=1, replica_groups=mesh['ty'=4,'tx'=8] {'tx'}, dimensions={0}, use_global_device_ids=true | all-gather | bytes 294912 | tf_op jit(solution)/shard_map/all_gather | solution.py:478
  138.9 2.2 %probe.4 = f32[4,2,128,128]{3,2,1,0:T(8,128)} custom-call(f32[4,2,128,128]{3,2,1,0:T(8,128)} %probe.5, bf16[1024,128]{1,0:T(8,128)(2,1)} %all_gather.3.gathered), custom_call_target="tpu_custom_call" | custom-call | tf_op jit(solution)/shard_map/probe/pallas_call | solution.py:385
  (60 shorter events, 1.7 us)
Async XLA Ops:
  6.5 35.0 %collective-permute-start = (bf16[20,64,128]{2,1,0:T(8,128)(2,1)}, bf16[20,64,128]{2,1,0:T(8,128)(2,1)S(1)}, u32[]{:S(2)}, u32[]{:S(2)}) collective-permute-start(bf16[20,64,128]{2,1,0:T(8,128)(2,1)} %get-tuple-element.21), channel_id=1, source_target_pairs={{0,8},{8,0},{16,24},{24,16},{1,9},{9,1},{17,25},{25,17},{2,10},{10... | collective-permute-start | bytes 983048 | tf_op jit(solution)/shard_map/ppermute | solution.py:432
  9.6 31.9 %collective-permute-start.1 = (bf16[20,64,128]{2,1,0:T(8,128)(2,1)}, bf16[20,64,128]{2,1,0:T(8,128)(2,1)S(1)}, u32[]{:S(2)}, u32[]{:S(2)}) collective-permute-start(bf16[20,64,128]{2,1,0:T(8,128)(2,1)} %get-tuple-element.22), channel_id=1, source_target_pairs={{0,24},{8,16},{16,8},{24,0},{1,25},{9,17},{17,9},{25,1},{2,26},{10... | collective-permute-start | bytes 983048 | tf_op jit(solution)/shard_map/ppermute | solution.py:432
  12.1 29.4 %collective-permute-start.3 = (bf16[2,512,128]{2,1,0:T(8,128)(2,1)}, bf16[2,512,128]{2,1,0:T(8,128)(2,1)S(1)}, u32[]{:S(2)}, u32[]{:S(2)}) collective-permute-start(bf16[2,512,128]{2,1,0:T(8,128)(2,1)} %get-tuple-element.24), channel_id=1, source_target_pairs={{0,1},{1,0},{2,3},{3,2},{4,5},{5,4},{6,7},{7,6},{8,9},{9,8},{10,11... | collective-permute-start | bytes 786440 | tf_op jit(solution)/shard_map/ppermute | solution.py:397
  12.1 29.4 %collective-permute-start.4 = (bf16[2,512,128]{2,1,0:T(8,128)(2,1)}, bf16[2,512,128]{2,1,0:T(8,128)(2,1)S(1)}, u32[]{:S(2)}, u32[]{:S(2)}) collective-permute-start(bf16[2,512,128]{2,1,0:T(8,128)(2,1)} %get-tuple-element.25), channel_id=1, source_target_pairs={{1,2},{2,1},{3,4},{4,3},{5,6},{6,5},{9,10},{10,9},{11,12},{12,11},... | collective-permute-start | bytes 786440 | tf_op jit(solution)/shard_map/ppermute | solution.py:397
  12.7 11.9 %collective-permute-start.5 = (bf16[2,64,128]{2,1,0:T(8,128)(2,1)}, bf16[2,64,128]{2,1,0:T(8,128)(2,1)S(1)}, u32[]{:S(2)}, u32[]{:S(2)}) collective-permute-start(bf16[2,64,128]{2,1,0:T(8,128)(2,1)} %get-tuple-element.26), channel_id=1, source_target_pairs={{0,9},{1,8},{2,11},{3,10},{4,13},{5,12},{6,15},{7,14},{8,1},{9,0},... | collective-permute-start | bytes 98312 | tf_op jit(solution)/shard_map/ppermute | solution.py:407
  24.6 16.8 %copy-start.14 = (bf16[2,64,128]{2,1,0:T(8,128)(2,1)}, bf16[2,64,128]{2,1,0:T(8,128)(2,1)S(1)}, u32[]{:S(2)}) copy-start(bf16[2,64,128]{2,1,0:T(8,128)(2,1)S(1)} %collective-permute-done.5.r_13_) | copy-start | bytes 98308
  24.6 0.7 collective-permute-start.6
  25.3 16.2 %copy-start.15 = (bf16[2,64,128]{2,1,0:T(8,128)(2,1)}, bf16[2,64,128]{2,1,0:T(8,128)(2,1)S(1)}, u32[]{:S(2)}) copy-start(bf16[2,64,128]{2,1,0:T(8,128)(2,1)S(1)} %collective-permute-done.6.r_14_) | copy-start | bytes 98308
  25.3 0.7 collective-permute-start.7
  26.0 15.5 %copy-start.17 = (bf16[2,64,128]{2,1,0:T(8,128)(2,1)}, bf16[2,64,128]{2,1,0:T(8,128)(2,1)S(1)}, u32[]{:S(2)}) copy-start(bf16[2,64,128]{2,1,0:T(8,128)(2,1)S(1)} %collective-permute-done.7.r_15_) | copy-start | bytes 98308
  26.0 0.7 collective-permute-start.8
  26.7 14.8 %copy-start.19 = (bf16[2,64,128]{2,1,0:T(8,128)(2,1)}, bf16[2,64,128]{2,1,0:T(8,128)(2,1)S(1)}, u32[]{:S(2)}) copy-start(bf16[2,64,128]{2,1,0:T(8,128)(2,1)S(1)} %collective-permute-done.8.r_16_) | copy-start | bytes 98308
  26.7 14.7 %collective-permute-start.2 = (bf16[4,64,128]{2,1,0:T(8,128)(2,1)}, bf16[4,64,128]{2,1,0:T(8,128)(2,1)S(1)}, u32[]{:S(2)}, u32[]{:S(2)}) collective-permute-start(bf16[4,64,128]{2,1,0:T(8,128)(2,1)} %get-tuple-element.23), channel_id=1, source_target_pairs={{0,16},{8,24},{16,0},{24,8},{1,17},{9,25},{17,1},{25,9},{2,18},{10... | collective-permute-start | bytes 196616 | tf_op jit(solution)/shard_map/ppermute | solution.py:432
  41.5 0.9 copy-start
  71.6 23.5 %all-to-all-start = ((bf16[8,128,128]{2,1,0:T(8,128)(2,1)}), bf16[8,128,128]{2,1,0:T(8,128)(2,1)S(1)}, u32[]{:S(2)}, u32[]{:S(2)}) async-start(bf16[8,128,128]{2,1,0:T(8,128)(2,1)} %get-tuple-element.39), calls=%async_computation | async-start | bytes 524288 | tf_op jit(solution)/shard_map/all_to_all | solution.py:465
  83.9 22.8 %collective-permute-start.9 = (bf16[16,64,128]{2,1,0:T(8,128)(2,1)}, bf16[16,64,128]{2,1,0:T(8,128)(2,1)S(1)}, u32[]{:S(2)}, u32[]{:S(2)}) collective-permute-start(bf16[16,64,128]{2,1,0:T(8,128)(2,1)} %get-tuple-element.31), channel_id=1, source_target_pairs={{0,8},{8,0},{16,24},{24,16},{1,9},{9,1},{17,25},{25,17},{2,10},{10... | collective-permute-start | bytes 786440 | tf_op jit(solution)/shard_map/ppermute | solution.py:397
  84.6 23.5 %collective-permute-start.10 = (bf16[16,64,128]{2,1,0:T(8,128)(2,1)}, bf16[16,64,128]{2,1,0:T(8,128)(2,1)S(1)}, u32[]{:S(2)}, u32[]{:S(2)}) collective-permute-start(bf16[16,64,128]{2,1,0:T(8,128)(2,1)} %get-tuple-element.32), channel_id=1, source_target_pairs={{8,16},{16,8},{9,17},{17,9},{10,18},{18,10},{11,19},{19,11},{12,20... | collective-permute-start | bytes 786440 | tf_op jit(solution)/shard_map/ppermute | solution.py:397
  85.3 7.7 %collective-permute-start.13 = (bf16[2,64,128]{2,1,0:T(8,128)(2,1)}, bf16[2,64,128]{2,1,0:T(8,128)(2,1)S(1)}, u32[]{:S(2)}, u32[]{:S(2)}) collective-permute-start(bf16[2,64,128]{2,1,0:T(8,128)(2,1)} %get-tuple-element.35), channel_id=1, source_target_pairs={{0,9},{1,8},{2,11},{3,10},{4,13},{5,12},{6,15},{7,14},{8,1},{9,0},... | collective-permute-start | bytes 98312 | tf_op jit(solution)/shard_map/ppermute | solution.py:407
  88.1 20.2 %collective-permute-start.11 = (bf16[2,512,128]{2,1,0:T(8,128)(2,1)}, bf16[2,512,128]{2,1,0:T(8,128)(2,1)S(1)}, u32[]{:S(2)}, u32[]{:S(2)}) collective-permute-start(bf16[2,512,128]{2,1,0:T(8,128)(2,1)} %get-tuple-element.33), channel_id=1, source_target_pairs={{0,1},{1,0},{2,3},{3,2},{4,5},{5,4},{6,7},{7,6},{8,9},{9,8},{10,11... | collective-permute-start | bytes 786440 | tf_op jit(solution)/shard_map/ppermute | solution.py:397
  88.4 19.9 %collective-permute-start.12 = (bf16[2,512,128]{2,1,0:T(8,128)(2,1)}, bf16[2,512,128]{2,1,0:T(8,128)(2,1)S(1)}, u32[]{:S(2)}, u32[]{:S(2)}) collective-permute-start(bf16[2,512,128]{2,1,0:T(8,128)(2,1)} %get-tuple-element.34), channel_id=1, source_target_pairs={{1,2},{2,1},{3,4},{4,3},{5,6},{6,5},{9,10},{10,9},{11,12},{12,11},... | collective-permute-start | bytes 786440 | tf_op jit(solution)/shard_map/ppermute | solution.py:397
  93.0 15.3 %copy-start.13 = (bf16[2,64,128]{2,1,0:T(8,128)(2,1)}, bf16[2,64,128]{2,1,0:T(8,128)(2,1)S(1)}, u32[]{:S(2)}) copy-start(bf16[2,64,128]{2,1,0:T(8,128)(2,1)S(1)} %collective-permute-done.13.refs_4_) | copy-start | bytes 98308
  93.1 0.7 collective-permute-start.14
  93.7 14.6 %copy-start.16 = (bf16[2,64,128]{2,1,0:T(8,128)(2,1)}, bf16[2,64,128]{2,1,0:T(8,128)(2,1)S(1)}, u32[]{:S(2)}) copy-start(bf16[2,64,128]{2,1,0:T(8,128)(2,1)S(1)} %collective-permute-done.14.refs_5_) | copy-start | bytes 98308
  93.7 0.7 collective-permute-start.15
  94.4 13.9 %copy-start.18 = (bf16[2,64,128]{2,1,0:T(8,128)(2,1)}, bf16[2,64,128]{2,1,0:T(8,128)(2,1)S(1)}, u32[]{:S(2)}) copy-start(bf16[2,64,128]{2,1,0:T(8,128)(2,1)S(1)} %collective-permute-done.15.refs_6_) | copy-start | bytes 98308
  94.4 0.7 collective-permute-start.16
  95.1 22.7 %copy-start.8 = (f32[128,128]{1,0:T(8,128)}, f32[128,128]{1,0:T(8,128)S(1)}, u32[]{:S(2)}) copy-start(f32[128,128]{1,0:T(8,128)S(1)} %convert_reduce_fusion.r_0_) | copy-start | bytes 196612
  95.2 13.2 %copy-start.20 = (bf16[2,64,128]{2,1,0:T(8,128)(2,1)}, bf16[2,64,128]{2,1,0:T(8,128)(2,1)S(1)}, u32[]{:S(2)}) copy-start(bf16[2,64,128]{2,1,0:T(8,128)(2,1)S(1)} %collective-permute-done.16.refs_7_) | copy-start | bytes 98308
  95.2 22.7 %collective-permute-start.17 = (f32[128,128]{1,0:T(8,128)S(1)}, f32[128,128]{1,0:T(8,128)S(1)}, u32[]{:S(2)}, u32[]{:S(2)}) collective-permute-start(f32[128,128]{1,0:T(8,128)S(1)} %convert_reduce_fusion.r_0_), channel_id=1, source_target_pairs={{0,8},{8,0},{16,24},{24,16},{1,9},{9,1},{17,25},{25,17},{2,10},{10... | collective-permute-start | bytes 196616 | tf_op jit(solution)/shard_map/ppermute | solution.py:468
  106.7 1.6 %copy-start.2 = (bf16[16,64,128]{2,1,0:T(8,128)(2,1)}, bf16[16,64,128]{2,1,0:T(8,128)(2,1)S(1)}, u32[]{:S(2)}) copy-start(bf16[16,64,128]{2,1,0:T(8,128)(2,1)S(1)} %collective-permute-done.9.refs_0_) | copy-start | bytes 786436
  106.7 11.1 %collective-permute-start.18 = (f32[128,128]{1,0:T(8,128)S(1)}, f32[128,128]{1,0:T(8,128)S(1)}, u32[]{:S(2)}, u32[]{:S(2)}) collective-permute-start(f32[128,128]{1,0:T(8,128)S(1)} %convert_reduce_fusion.r_0_), channel_id=1, source_target_pairs={{0,24},{8,16},{16,8},{24,0},{1,25},{9,17},{17,9},{25,1},{2,26},{10... | collective-permute-start | bytes 196616 | tf_op jit(solution)/shard_map/ppermute | solution.py:468
  108.1 9.7 %collective-permute-start.19 = (f32[128,128]{1,0:T(8,128)S(1)}, f32[128,128]{1,0:T(8,128)S(1)}, u32[]{:S(2)}, u32[]{:S(2)}) collective-permute-start(f32[128,128]{1,0:T(8,128)S(1)} %convert_reduce_fusion.r_0_), channel_id=1, source_target_pairs={{0,16},{8,24},{16,0},{24,8},{1,17},{9,25},{17,1},{25,9},{2,18},{10... | collective-permute-start | bytes 196616 | tf_op jit(solution)/shard_map/ppermute | solution.py:468
  (10 other events, 7.1 us)

commit v2 on v1

v2 whole, which is shorter than its diff:
```python
import math

import numpy as np
import jax
import jax.numpy as jnp
from jax import lax
from jax.experimental import pallas as pl
from jax.experimental.pallas import tpu as pltpu
from jax.sharding import PartitionSpec as P


CAP = 2
PROPAGATION = 0.37
LANES = 128
BF16 = jnp.bfloat16
F32 = jnp.float32


def make_tables(extent):
    indices = np.arange(extent, dtype=np.int32)
    product = indices[:, None] * indices[None, :] % extent
    angles = np.float32(2.0 * math.pi / extent) * product.astype(np.float32)
    norm_scale = np.float32(1.0 / math.sqrt(extent))
    real_table = jnp.asarray(np.cos(angles) * norm_scale, F32).astype(BF16)
    imag_table = jnp.asarray(-np.sin(angles) * norm_scale, F32).astype(BF16)
    first = jnp.concatenate(
        [
            jnp.concatenate([real_table, imag_table], 1),
            jnp.concatenate([-imag_table, real_table], 1),
        ],
        0,
    )
    second = jnp.concatenate(
        [
            jnp.concatenate([real_table, -imag_table], 1),
            jnp.concatenate([imag_table, real_table], 1),
        ],
        0,
    )
    frequency = np.where(indices < extent // 2, indices, indices - extent).astype(np.float32)
    phases = np.float32(-math.pi * PROPAGATION / extent) * (
        frequency[:, None] ** 2 + frequency[None, :] ** 2
    )
    kernel = jnp.asarray(np.stack([np.cos(phases), np.sin(phases)]), F32)
    return first, second, kernel


def pairings(n):
    if n == 2:
        return [[1, 0]]
    assert n % 2 == 0 and all((n - 1) % d for d in range(2, n - 1))
    odd = n - 1
    rounds = []
    for k in range(odd):
        partner = [0] * n
        partner[odd], partner[k] = k, odd
        for i in range(1, n // 2):
            a, b = (k + i) % odd, (k - i) % odd
            partner[a], partner[b] = b, a
        rounds.append(partner)
    order = [odd]
    while len(order) < n:
        order.append(rounds[(len(order) - 1) % 2][order[-1]])
    label = {v: i for i, v in enumerate(order)}
    return [[label[r[order[i]]] for i in range(n)] for r in rounds]


def neighbour(side, i):
    return 1 if (i + side) % 2 == 0 else -1


def neighbour_pairs(side, n):
    steps = [(i, i + neighbour(side, i)) for i in range(n)]
    return [(i, j) for i, j in steps if 0 <= j < n]


def pick(index, values):
    chosen = jnp.int32(values[0])
    for i in range(1, len(values)):
        chosen = jnp.where(index == i, jnp.int32(values[i]), chosen)
    return chosen


def lane_ids(rows):
    return lax.broadcasted_iota(jnp.int32, (rows, LANES), 1)


def half_mask(rows, upper):
    return (lane_ids(rows) >= LANES // 2).astype(jnp.int32) == upper


def ups(index):
    even = 1 - lax.rem(index, 2)
    return [even, 1 - even]


def slot_scan(pos, cnt, sizes, source, col, per_device, low, height):
    n_tx = sizes[1]
    base = (source * n_tx + col) * per_device
    count = cnt[source * n_tx + col]
    zero = jnp.int32(0)
    found, ys, xs, lives = [zero] * CAP, [zero] * CAP, [zero] * CAP, [zero] * CAP
    seen = zero
    for i in range(per_device):
        y, x = pos[0, base + i], pos[1, base + i]
        hit = (i < count) & (y >= low) & (y < low + height)
        for c in range(CAP):
            this = hit & (seen == c)
            found[c] = jnp.where(this, i, found[c])
            ys[c] = jnp.where(this, y - low, ys[c])
            xs[c] = jnp.where(this, x, xs[c])
            lives[c] = jnp.where(this, 1, lives[c])
        seen = seen + hit.astype(jnp.int32)
    return found, ys, xs, lives


def rows_kernel(sizes, obj, pat, pos, cnt, ty_a, ty_b, held, rows, sems):
    planes, tile, margin = obj.shape[0] * 2, obj.shape[2], rows.shape[3]
    tiles = obj.shape[3] // LANES
    row, col = lax.axis_index("ty"), lax.axis_index("tx")
    up_y = ups(row)
    copies = [pltpu.make_async_copy(pat, held, sems.at[2])]
    for k in range(2):
        start = pl.multiple_of(up_y[k] * (tile - margin), margin)
        copies.append(pltpu.make_async_copy(obj.at[:, :, pl.ds(start, margin), :], rows.at[k], sems.at[k]))
    for copy in copies:
        copy.start()
    target = pick(row, sizes[2][0]) * tile
    found = slot_scan(pos, cnt, sizes, row, col, pat.shape[0], target, tile)[0]
    copies[0].wait()
    for c in range(CAP):
        for h in range(2):
            ty_a[planes * tiles + 2 * c + h] = held[found[c], h * margin : (h + 1) * margin, :]
    for k, out in enumerate((ty_a, ty_b)):
        copies[1 + k].wait()
        for p in range(planes):
            for t in range(tiles):
                block = rows[k, p // 2, p % 2, :, t * LANES : (t + 1) * LANES]
                out[p * tiles + t] = block.astype(BF16)


def columns_kernel(obj, tx_a, tx_b):
    slices, tile = obj.shape[0], obj.shape[2]
    up_x = ups(lax.axis_index("tx"))
    for j, out in enumerate((tx_a, tx_b)):
        lane = pl.ds(pl.multiple_of(up_x[j] * (tile - LANES), LANES), LANES)
        for s in range(slices):
            re, im = obj[s, 0, :, lane], obj[s, 1, :, lane]
            packed = jnp.where(half_mask(tile, up_x[j]), re, pltpu.roll(im, LANES // 2, 1))
            out[s] = packed.astype(BF16)


def tile_kernel(sizes, obj, pat, pos, cnt, ext, grad, *routed):
    rounds = sizes[2]
    slices, tile = obj.shape[0], obj.shape[2]
    tiles = obj.shape[3] // LANES
    margin = (ext.shape[2] - tile) // 2
    row, col = lax.axis_index("ty"), lax.axis_index("tx")
    targets = [pick(row, partner) * tile for partner in rounds[1:]]
    found = [slot_scan(pos, cnt, sizes, row, col, pat.shape[0], t, tile)[0] for t in targets]
    for k, out in enumerate(routed):
        for c in range(CAP):
            out[c] = pat[found[k][c]]
    for p in range(slices * 2):
        for t in range(tiles):
            ext[p, 1 + t, margin : margin + tile] = obj[p // 2, p % 2, :, t * LANES : (t + 1) * LANES]
    grad[...] = jnp.zeros(grad.shape, F32)


def corner_kernel(slices, tiles, ty_a, ty_b, out_a, out_b):
    up_x = ups(lax.axis_index("tx"))
    for j, out in enumerate((out_a, out_b)):
        at = up_x[j] * (tiles - 1)
        for k, rows in enumerate((ty_a, ty_b)):
            for s in range(slices):
                re = rows[2 * s * tiles + at].astype(F32)
                im = rows[(2 * s + 1) * tiles + at].astype(F32)
                packed = jnp.where(half_mask(re.shape[0], up_x[j]), re, pltpu.roll(im, LANES // 2, 1))
                out[k * slices + s] = packed.astype(BF16)


def cmul(a, b):
    return a[0] * b[0] - a[1] * b[1], a[0] * b[1] + a[1] * b[0]


def cmul_conj(a, b):
    return a[0] * b[0] + a[1] * b[1], a[0] * b[1] - a[1] * b[0]


def transform(fields, right, left):
    extent = fields[0][0].shape[0]
    joined = jnp.concatenate([jnp.concatenate([re, im], 1) for re, im in fields], 0).astype(BF16)
    half = jnp.dot(joined, right, preferred_element_type=F32).astype(BF16)
    blocks = []
    for m in range(len(fields)):
        part = half[m * extent : (m + 1) * extent]
        blocks.append(jnp.concatenate([part[:, :extent], part[:, extent:]], 0))
    whole = jnp.dot(left, jnp.concatenate(blocks, 1), preferred_element_type=F32)
    return [
        (whole[:extent, m * extent : (m + 1) * extent], whole[extent:, m * extent : (m + 1) * extent])
        for m in range(len(fields))
    ]


def find_slots(sizes, pos, cnt, per_device, tile, row_of, col_of, live_of):
    rounds = sizes[2]
    row, col = lax.axis_index("ty"), lax.axis_index("tx")
    own = None
    for k in range(len(rounds) + 1):
        source = row if k == 0 else pick(row, rounds[k - 1])
        found, ys, xs, lives = slot_scan(pos, cnt, sizes, source, col, per_device, row * tile, tile)
        own = found if k == 0 else own
        for c in range(CAP):
            slot = k * CAP + c
            row_of[slot] = ys[c]
            col_of[slot] = jnp.where(lives[c] == 1, xs[c] - col * tile, 0)
            if live_of is not None:
                live_of[slot] = lives[c].astype(F32)
    return own


def places(row_of, col_of, slot, margin, lanes):
    x = col_of[slot] + margin
    off = x & (LANES - 1)
    return row_of[slot], lax.shift_right_logical(x, 7), off, lanes >= off


def window(ext, place, p):
    y, side, off, upper = place
    v0 = ext[p, side, pl.ds(y, LANES), :]
    v1 = ext[p, side + 1, pl.ds(y, LANES), :]
    return pltpu.roll(jnp.where(upper, v0, v1), (LANES - off) & (LANES - 1), 1)


def forward_kernel(sizes, per_device, pos, cnt, probe, *refs):
    sources, refs = refs[:3], refs[3:]
    ty_in, tx_in, corner_in = refs[:2], refs[2:4], refs[4:6]
    ext, psi, waves, first, second, kern, row_of, col_of, sems = refs[7:]
    copies = [
        pltpu.make_async_copy(a, b, sems.at[i])
        for i, (a, b) in enumerate(zip(sources, (first, second, kern)))
    ]
    for copy in copies:
        copy.start()
    modes, extent = probe.shape[0], probe.shape[2]
    planes, margin, tiles = ext.shape[0], extent // 2, ext.shape[1] - 2
    slices, tile = planes // 2, ext.shape[2] - extent
    up_y, up_x = ups(lax.axis_index("ty")), ups(lax.axis_index("tx"))
    find_slots(sizes, pos, cnt, per_device, tile, row_of, col_of, None)
    for k in range(2):
        rows = pl.ds(pl.multiple_of(up_y[k] * (tile + margin), margin), margin)
        for p in range(planes):
            for t in range(tiles):
                ext[p, 1 + t, rows] = ty_in[k][p * tiles + t].astype(F32)
        for s in range(slices):
            for j in range(2):
                side = up_x[j] * (tiles + 1)
                strip = corner_in[j][k * slices + s].astype(F32)
                ext[2 * s, side, rows] = strip
                ext[2 * s + 1, side, rows] = pltpu.roll(strip, LANES // 2, 1)
    for s in range(slices):
        for j in range(2):
            side = up_x[j] * (tiles + 1)
            strip = tx_in[j][s].astype(F32)
            ext[2 * s, side, margin : margin + tile] = strip
            ext[2 * s + 1, side, margin : margin + tile] = pltpu.roll(strip, LANES // 2, 1)
    lanes = lane_ids(extent)
    for copy in copies:
        copy.wait()

    def body(i, carry):
        slots = [i * BATCH + b for b in range(BATCH)]
        p_tab, q_tab = first[...], second[...]
        prop = (kern[0], kern[1])
        where = [places(row_of, col_of, slot, margin, lanes) for slot in slots]
        fields = [(probe[m, 0], probe[m, 1]) for m in range(modes)] * BATCH
        for s in range(slices):
            cells = [(window(ext, w, 2 * s), window(ext, w, 2 * s + 1)) for w in where]
            exits = [cmul(w, cells[n // modes]) for n, w in enumerate(fields)]
            far_field = transform(exits, p_tab, q_tab)
            if s + 1 < slices:
                fields = transform([cmul(prop, f) for f in far_field], q_tab, p_tab)
            kept = fields if s + 1 < slices else far_field
            for n, (re, im) in enumerate(kept):
                at = 2 * (n % modes)
                if s + 1 < slices:
                    waves[s, slots[n // modes], at] = re
                    waves[s, slots[n // modes], at + 1] = im
                else:
                    psi[slots[n // modes], at] = re
                    psi[slots[n // modes], at + 1] = im
        return carry

    lax.fori_loop(0, psi.shape[0] // BATCH, body, 0)


def backward_kernel(sizes, pat, pos, cnt, probe, first, second, kern, ext, psi, waves, *refs):
    _, n_tx, rounds = sizes
    k_n = len(rounds)
    pat_in, refs = refs[:k_n], refs[k_n + 1 :]
    grad, ty_out, keep, share = refs[0], refs[1:3], refs[3], refs[4]
    amp, acc, row_of, col_of, live_of = refs[5:]
    modes, extent = probe.shape[0], probe.shape[2]
    planes, margin, tiles = ext.shape[0], extent // 2, ext.shape[1] - 2
    slices, tile = planes // 2, ext.shape[2] - extent
    parts = planes * tiles
    row, col = lax.axis_index("ty"), lax.axis_index("tx")
    up_y, up_x = ups(row), ups(col)
    start_y = [pl.multiple_of(up_y[k] * (tile + margin), margin) for k in range(2)]
    own = find_slots(sizes, pos, cnt, pat.shape[0], tile, row_of, col_of, live_of)
    for c in range(CAP):
        amp[c] = pat[own[c]]
        for h in range(2):
            amp[CAP + c, h * margin : (h + 1) * margin] = pat_in[0][parts + 2 * c + h]
        for k in range(1, k_n):
            amp[(k + 1) * CAP + c] = pat_in[k][c]
    acc[...] = jnp.zeros(acc.shape, F32)
    lanes = lane_ids(extent)

    def scatter(place, p, value):
        y, side, off, upper = place
        moved = pltpu.roll(value, off, 1)
        grad[p, side, pl.ds(y, extent), :] += jnp.where(upper, moved, 0.0)
        grad[p, side + 1, pl.ds(y, extent), :] += jnp.where(upper, 0.0, moved)

    def body(i, carry):
        slots = [i * BATCH + b for b in range(BATCH)]
        p_tab, q_tab = first[...], second[...]
        prop = (kern[0], kern[1])
        where = [places(row_of, col_of, slot, margin, lanes) for slot in slots]
        residues = []
        for slot in slots:
            mine = [(psi[slot, 2 * m], psi[slot, 2 * m + 1]) for m in range(modes)]
            total = mine[0][0] * mine[0][0] + mine[0][1] * mine[0][1]
            for re, im in mine[1:]:
                total = total + (re * re + im * im)
            scale = amp[slot].astype(F32) * lax.rsqrt(jnp.maximum(total, 0.25))
            factor = (1.0 - scale) * live_of[slot]
            residues += [(re * factor, im * factor) for re, im in mine]
        back_waves = transform(residues, q_tab, p_tab)
        for s in reversed(range(slices)):
            for n, slot in enumerate(slots):
                for m in range(modes):
                    if s == 0:
                        wave = (probe[m, 0], probe[m, 1])
                    else:
                        wave = (waves[s - 1, slot, 2 * m], waves[s - 1, slot, 2 * m + 1])
                    re, im = cmul_conj(wave, back_waves[n * modes + m])
                    q_re, q_im = (re, im) if m == 0 else (q_re + re, q_im + im)
                scatter(where[n], 2 * s, q_re)
                scatter(where[n], 2 * s + 1, q_im)
            cells = [(window(ext, w, 2 * s), window(ext, w, 2 * s + 1)) for w in where]
            terms = [cmul_conj(cells[n // modes], g) for n, g in enumerate(back_waves)]
            if s > 0:
                inner = transform(terms, p_tab, q_tab)
                back_waves = transform([cmul_conj(prop, f) for f in inner], q_tab, p_tab)
        for m in range(modes):
            for c in range(2):
                value = terms[m][c]
                for n in range(1, BATCH):
                    value = value + terms[n * modes + m][c]
                acc[2 * m + c] += value
        return carry

    lax.fori_loop(0, psi.shape[0] // BATCH, body, 0)

    chunk = keep.shape[1]
    core = lax.rem(col, 2)
    for i in range(n_tx // 2):
        for out, parity in ((keep, core), (share, 1 - core)):
            at = (2 * i + parity) * chunk
            index = lax.div(at, extent)
            inside = pl.multiple_of(at - index * extent, chunk)
            out[i] = acc[index, pl.ds(inside, chunk), :]
    for k in range(2):
        for p in range(planes):
            for t in range(tiles):
                ty_out[k][p * tiles + t] = grad[p, 1 + t, pl.ds(start_y[k], margin)].astype(BF16)
        for j in range(2):
            side, mask = up_x[j] * (tiles + 1), half_mask(margin, 1 - up_x[j])
            for s in range(slices):
                re = grad[2 * s, side, pl.ds(start_y[k], margin)]
                im = grad[2 * s + 1, side, pl.ds(start_y[k], margin)]
                packed = jnp.where(mask, re, pltpu.roll(im, LANES // 2, 1))
                ty_out[k][parts + j * slices + s] = packed.astype(BF16)


def pair_kernel(keep, share, own, *outs):
    at = lax.shift_right_logical(lax.axis_index("tx"), 1)
    own[...] = keep[at] + share[at]
    for k, out in enumerate(outs, 1):
        other = jnp.bitwise_xor(at, k)
        out[...] = (keep[other] + share[other]).astype(BF16)


def join_kernel(*refs):
    parts, out = refs[:-1], refs[-1]
    at = lax.shift_right_logical(lax.axis_index("tx"), 1)
    for k, part in enumerate(parts):
        out[jnp.bitwise_xor(at, k)] = part[...]


def share_kernel(own, *refs):
    parts, out = refs[:-1], refs[-1]
    total = own[...]
    for part in parts:
        total = total + part[...].astype(F32)
    out[...] = total.astype(out.dtype)


def update_rate(probe):
    extent = probe.shape[2]
    power = jnp.sum(probe[...] * probe[...]) / (extent * extent)
    return jnp.full((1, 1), 1.0, F32) / (power + 1e-06)


def fold_kernel(tile, old, ty_a, ty_b, tx_a, tx_b, grad):
    planes, tiles = grad.shape[0], grad.shape[1] - 2
    slices, margin = planes // 2, (grad.shape[2] - tile) // 2
    up_y, up_x = ups(lax.axis_index("ty")), ups(lax.axis_index("tx"))
    for k, strips in enumerate((ty_a, ty_b)):
        rows = pl.ds(pl.multiple_of(margin + up_y[k] * (tile - margin), margin), margin)
        for p in range(planes):
            for t in range(tiles):
                grad[p, 1 + t, rows] += strips[p * tiles + t].astype(F32)
        for j in range(2):
            side, mask = up_x[j] * (tiles + 1), half_mask(margin, 1 - up_x[j])
            for s in range(slices):
                strip = strips[planes * tiles + j * slices + s].astype(F32)
                grad[2 * s, side, rows] += jnp.where(mask, strip, 0.0)
                grad[2 * s + 1, side, rows] += jnp.where(mask, pltpu.roll(strip, LANES // 2, 1), 0.0)
    inner = slice(margin, margin + tile)
    for j, out in enumerate((tx_a, tx_b)):
        side, mask = up_x[j] * (tiles + 1), half_mask(tile, 1 - up_x[j])
        for s in range(slices):
            re, im = grad[2 * s, side, inner], grad[2 * s + 1, side, inner]
            out[s] = jnp.where(mask, re, pltpu.roll(im, LANES // 2, 1)).astype(BF16)


def middle_kernel(obj, grad, probe, out, fresh, sems):
    tile, tiles = obj.shape[2], obj.shape[3] // LANES
    margin = (grad.shape[2] - tile) // 2
    rate = update_rate(probe)
    copies = []
    for p in range(obj.shape[0] * 2):
        s, c = p // 2, p % 2
        for t in range(1, tiles - 1):
            piece = obj[s, c, :, t * LANES : (t + 1) * LANES] - grad[p, 1 + t, margin : margin + tile] * rate
            fresh[s, c, :, (t - 1) * LANES : t * LANES] = piece
        copies.append(
            pltpu.make_async_copy(
                fresh.at[s, c], out.at[s, c, :, LANES : (tiles - 1) * LANES], sems.at[p]
            )
        )
        copies[-1].start()
    for copy in copies:
        copy.wait()


def edges_kernel(obj, grad, tx_a, tx_b, probe, old, out, fresh, sems):
    slices, tile, tiles = obj.shape[0], obj.shape[2], obj.shape[3] // LANES
    margin = (grad.shape[2] - tile) // 2
    up_x = ups(lax.axis_index("tx"))
    rate = update_rate(probe)
    copies = []
    for high in range(2):
        t, mask = high * (tiles - 1), half_mask(tile, high)
        span = slice(t * LANES, (t + 1) * LANES)
        for s in range(slices):
            strip = jnp.where(up_x[0] == high, tx_a[s].astype(F32), tx_b[s].astype(F32))
            for c in range(2):
                if c == 1:
                    strip = pltpu.roll(strip, LANES // 2, 1)
                total = grad[2 * s + c, 1 + t, margin : margin + tile] + jnp.where(mask, strip, 0.0)
                fresh[high, s, c] = obj[s, c, :, span] - total * rate
            copies.append(
                pltpu.make_async_copy(fresh.at[high, s], out.at[s, :, :, span], sems.at[high * slices + s])
            )
            copies[-1].start()
    for copy in copies:
        copy.wait()


def probe_kernel(probe, joined, other, out, held):
    modes, extent, chunk = probe.shape[0], probe.shape[2], joined.shape[1]
    core = lax.rem(lax.axis_index("tx"), 2)
    for i in range(joined.shape[0]):
        for part, parity in ((joined, core), (other, 1 - core)):
            at = pl.multiple_of((2 * i + parity) * chunk, chunk)
            held[pl.ds(at, chunk), :] = part[i].astype(F32)
    summed = held[...]
    mean = jnp.sum(summed * summed) / summed.size
    step = jnp.full((1, 1), 0.5, F32) * lax.rsqrt(jnp.full((1, 1), 1.0, F32) * (mean + 1e-06))
    for m in range(modes):
        for c in range(2):
            at = (2 * m + c) * extent
            out[m, c] = probe[m, c] - held[at : at + extent] * step


def sum_kernel(sizes, own, *refs):
    rounds = sizes[2]
    parts, out, held = refs[: len(rounds)], refs[len(rounds)], refs[len(rounds) + 1]
    row = lax.axis_index("ty")
    held[row] = own[...].astype(F32)
    for k, partner in enumerate(rounds):
        held[pick(row, partner)] = parts[k][...].astype(F32)
    total = held[0]
    for i in range(1, held.shape[0]):
        total = total + held[i]
    out[...] = total.astype(out.dtype)


BATCH = 4
VMEM_BYTES = 10 * 1024 * 1024
VMEM = pl.BlockSpec(memory_space=pltpu.VMEM)
SMEM = pl.BlockSpec(memory_space=pltpu.SMEM)
ANY = pl.BlockSpec(memory_space=pl.ANY)


def call(kernel, operands, specs, outs, scratch=(), aliases=None, out_specs=None):
    single = not isinstance(outs, (list, tuple))
    return pl.pallas_call(
        kernel,
        out_shape=outs,
        in_specs=specs,
        out_specs=out_specs or (VMEM if single else [VMEM] * len(outs)),
        scratch_shapes=list(scratch),
        input_output_aliases=aliases or {},
        compiler_params=pltpu.CompilerParams(vmem_limit_bytes=VMEM_BYTES),
    )(*operands)


def near(value):
    return pltpu.with_memory_space_constraint(value, pltpu.VMEM)


def far(value):
    return pltpu.with_memory_space_constraint(value, pltpu.HBM)


def send(value, axis, pairs):
    return near(lax.ppermute(value, axis, pairs))


def step(object_slices, probe_modes, patterns, positions, counts):
    slices, _, tile, _ = object_slices.shape
    modes, _, extent, _ = probe_modes.shape
    margin, tiles = extent // 2, tile // LANES
    n_ty, n_tx = lax.axis_size("ty"), lax.axis_size("tx")
    rounds = pairings(n_ty)
    sizes = (n_ty, n_tx, rounds)
    parts = slices * 2 * tiles
    k_n = len(rounds)
    places = positions.T
    planes = slices * 2
    block = (margin, LANES)
    strips = [pltpu.VMEM((slices, tile, LANES), BF16)] * 2
    strips = [pltpu.VMEM((slices, tile, LANES), BF16)] * 2
    rows_out = [pltpu.VMEM((parts + 2 * slices,) + block, BF16)] * 2
    ty_a, ty_b, near_patterns = call(
        lambda *r: rows_kernel(sizes, *r),
        (far(object_slices), far(patterns), far(places), far(counts)),
        [ANY, ANY, SMEM, SMEM],
        [pltpu.VMEM((parts + extra,) + block, BF16) for extra in (2 * CAP, 0)]
        + [pltpu.VMEM(patterns.shape, BF16)],
        [pltpu.VMEM((2, slices, 2, margin, tile), F32), pltpu.SemaphoreType.DMA((3,))],
    )
    near_object, near_patterns = near(object_slices), near(near_patterns)
    tx_a, tx_b = call(columns_kernel, (near_object,), [VMEM], strips)

    def pair_rows(value, k):
        return send(value, "ty", [(i, rounds[k][i]) for i in range(n_ty)])

    def swap(value, axis, side):
        return send(value, axis, neighbour_pairs(side, lax.axis_size(axis)))

    def cross(value, k):
        return send(value, "tx", [(i, i ^ k) for i in range(n_tx)])

    ext_shape = (planes, tiles + 2, tile + extent, LANES)
    ty_in = [swap(ty_a, "ty", 0), swap(ty_b, "ty", 1)]
    tx_in = [swap(tx_a, "tx", 0), swap(tx_b, "tx", 1)]
    ext, grad, *routed = call(
        lambda *r: tile_kernel(sizes, *r),
        (near_object, near_patterns, far(places), far(counts)),
        [VMEM, VMEM, SMEM, SMEM],
        [pltpu.VMEM(ext_shape, F32)] * 2 + [pltpu.VMEM((CAP, extent, extent), BF16)] * (k_n - 1),
    )
    corners = call(
        lambda *r: corner_kernel(slices, tiles, *r),
        tuple(ty_in),
        [VMEM] * 2,
        [pltpu.VMEM((2 * slices,) + block, BF16)] * 2,
    )
    corner_in = [swap(corners[j], "tx", j) for j in range(2)]
    pat_in = [ty_in[0]] + [pair_rows(routed[k - 1], k) for k in range(1, k_n)]

    first, second, kern = make_tables(extent)
    slots = (k_n + 1) * CAP
    chunk = modes * 2 * extent // n_tx
    constants = (first, second, kern)
    field = (slots, 2 * modes, extent, extent)
    tables = [pltpu.SMEM((slots,), jnp.int32)] * 2
    ext, psi, waves, *constants = call(
        lambda *r: forward_kernel(sizes, patterns.shape[0], *r),
        (places, counts, near(probe_modes))
        + tuple(far(c) for c in constants)
        + tuple(ty_in + tx_in + corner_in)
        + (near(ext),),
        [SMEM, SMEM, VMEM] + [ANY] * 3 + [VMEM] * 7,
        [pltpu.VMEM(ext_shape, F32), pltpu.VMEM(field, F32), pltpu.VMEM((slices - 1,) + field, F32)]
        + [pltpu.VMEM(c.shape, c.dtype) for c in constants],
        tables + [pltpu.SemaphoreType.DMA((3,))],
        {12: 0},
    )
    results = call(
        lambda *r: backward_kernel(sizes, *r),
        (near_patterns, places, counts, near(probe_modes))
        + tuple(near(c) for c in constants)
        + (near(ext), near(psi), near(waves), *pat_in, near(grad)),
        [VMEM, SMEM, SMEM] + [VMEM] * (7 + k_n + 1),
        [pltpu.VMEM(ext_shape, F32)]
        + rows_out
        + [pltpu.VMEM((n_tx // 2, chunk, LANES), F32)] * 2,
        [pltpu.VMEM((slots, extent, extent), BF16), pltpu.VMEM((2 * modes, extent, extent), F32)]
        + tables
        + [pltpu.SMEM((slots,), F32)],
        {10 + k_n: 0},
    )
    grad, ty_a, ty_b, keep, share = results
    ty_back = [swap(ty_a, "ty", 0), swap(ty_b, "ty", 1)]
    mine, *shares = call(
        pair_kernel,
        (near(keep), cross(share, 1)),
        [VMEM] * 2,
        [pltpu.VMEM((chunk, LANES), F32)] + [pltpu.VMEM((chunk, LANES), BF16)] * (n_tx // 2 - 1),
    )
    others = tuple(cross(shares[k - 1], 2 * k) for k in range(1, n_tx // 2))
    mine = call(
        share_kernel, (near(mine),) + others, [VMEM] * (n_tx // 2), pltpu.VMEM((chunk, LANES), BF16)
    )
    rows_in = tuple(pair_rows(mine, k) for k in range(k_n))
    tx_a, tx_b, grad = call(
        lambda *r: fold_kernel(tile, *r),
        (near(grad), *ty_back),
        [VMEM] * 3,
        strips + [pltpu.VMEM(ext_shape, F32)],
        (),
        {0: 2},
    )
    tx_back = [swap(tx_a, "tx", 0), swap(tx_b, "tx", 1)]
    full = call(
        lambda *r: sum_kernel(sizes, *r),
        (near(mine),) + rows_in,
        [VMEM] * (k_n + 1),
        pltpu.VMEM((chunk, LANES), BF16),
        [pltpu.VMEM((n_ty, chunk, LANES), F32)],
    )
    gathered = tuple(cross(full, 2 * k) for k in range(1, n_tx // 2))
    joined = call(
        join_kernel,
        (near(full),) + gathered,
        [VMEM] * (n_tx // 2),
        pltpu.VMEM((n_tx // 2, chunk, LANES), BF16),
    )
    other = cross(joined, 1)
    partial = call(
        middle_kernel,
        (near_object, near(grad), near(probe_modes)),
        [VMEM] * 3,
        pltpu.HBM(object_slices.shape, F32),
        [pltpu.VMEM((slices, 2, tile, tile - 2 * LANES), F32), pltpu.SemaphoreType.DMA((planes,))],
        None,
        ANY,
    )
    new_object = call(
        edges_kernel,
        (near_object, near(grad), *tx_back, near(probe_modes), far(partial)),
        [VMEM] * 5 + [ANY],
        pltpu.HBM(object_slices.shape, F32),
        [
            pltpu.VMEM((2, slices, 2, tile, LANES), F32),
            pltpu.SemaphoreType.DMA((2 * slices,)),
        ],
        {5: 0},
        ANY,
    )
    new_probe = call(
        probe_kernel,
        (near(probe_modes), near(joined), other),
        [VMEM] * 3,
        jax.ShapeDtypeStruct(probe_modes.shape, F32),
        [pltpu.VMEM((modes * 2 * extent, LANES), F32)],
    )
    return (new_object, new_probe)


def solution(mesh):
    return jax.shard_map(
        step,
        mesh=mesh,
        in_specs=(P(None, None, "ty", "tx"), P(), P(("ty", "tx"), None, None), P(), P()),
        out_specs=(P(None, None, "ty", "tx"), P()),
        check_vma=False,
    )
```

time: 142 us -> 83.4 us (0.59)
  Pallas kernels: 45.4 us -> 24.8 us
  starting transfers between devices: 56.2 us -> 35.9 us
  blocking collectives: 18.2 us -> 0 us
  waiting for transfers between devices: 15.2 us -> 19.3 us
  local copies, waits for them, and re-layouts: 5.05 us -> 2.21 us
    pallas_call x5 -> x14, Pallas kernels: 45.4 us -> 24.8 us  [call(): pl.pallas_call(kernel, out_shape=outs, in_specs=specs, out_specs=out_spec...]
    all_gather x1 -> x0, blocking collectives: 18.2 us -> none  [on_device(): gathered = lax.all_gather(full, 'tx', axis=0, tiled=True)]
    all_to_all x1 -> x0, starting transfers between devices: 12.3 us -> none  [on_device(): lax.all_to_all(probe_grad, 'tx', split_axis=0, concat_axis=0, tiled=True)]
    ppermute x20 -> x23, starting transfers between devices: 43.9 us -> 35.9 us  [send(): return near(lax.ppermute(value, axis, pairs))]
    ppermute x20 -> x23, waiting for transfers between devices: 15.2 us -> 19.3 us  [send(): return near(lax.ppermute(value, axis, pairs))]
    unnamed x43 -> x10, local copies, waits for them, and re-layouts: 5.05 us -> 2.21 us
  transfers between devices with their start and end apart: 21 -> 23, of which waited for: 3 -> 8; matrix products, arithmetic and copies ran while one was open for 0% -> 0% of each run, Pallas kernels for 6% -> 14%
where the time goes in v2:
time: 83.4 us; the launch traced here: 83.1 us
  starting transfers between devices  35.9 us (43%)
  Pallas kernels  24.8 us (30%)
  waiting for transfers between devices  19.3 us (23%)
  local copies, waits for them, and re-layouts  2.21 us (3%)
  between operations  0.89 us (1%)
    ppermute x23, starting transfers between devices, send(): return near(lax.ppermute(value, axis, pairs))  35.9 us
    pallas_call x14, Pallas kernels, call(): pl.pallas_call(kernel, out_shape=outs, in_specs=specs, out_specs=out_spec...  24.8 us
    ppermute x23, waiting for transfers between devices, send(): return near(lax.ppermute(value, axis, pairs))  19.3 us
    unnamed x10, local copies, waits for them, and re-layouts  2.21 us
  transfers between devices with their start and end apart: 23, of which 8 were waited for; matrix products, arithmetic and copies ran while one was open for 0% of the time, Pallas kernels for 14%

profile of v2, /device:TPU:0, one launch (start us, length us, event | category | flops | bytes accessed | tf_op | source)
XLA Modules:
  0.0 83.1 jit_solution(14027949611717675823)
XLA Ops:
  0.7 2.6 %shard_map.95 = (bf16[20,64,128]{2,1,0:T(8,128)(2,1)S(1)}, bf16[16,64,128]{2,1,0:T(8,128)(2,1)S(1)}, bf16[8,128,128]{2,1,0:T(8,128)(2,1)S(1)}) custom-call(f32[2,2,512,512]{3,2,1,0:T(8,128)} %obj.5, bf16[8,128,128]{2,1,0:T(8,128)(2,1)} %r_1_.2, s32[2,256]{1,0:T(2,128)} %bitcast.1, s32[32]{0:T(128)} %r_2_.3), custom_call_target="tpu_custom_call" | custom-call | tf_op jit(solution)/shard_map/pallas_call | solution.py:522
  3.3 3.1 %collective-permute-start = (bf16[20,64,128]{2,1,0:T(8,128)(2,1)S(1)}, bf16[20,64,128]{2,1,0:T(8,128)(2,1)S(1)}, u32[]{:S(2)}, u32[]{:S(2)}) collective-permute-start(bf16[20,64,128]{2,1,0:T(8,128)(2,1)S(1)} %get-tuple-element.32), channel_id=1, source_target_pairs={{0,8},{8,0},{16,24},{24,16},{1,9},{9,1},{17,25},{25,17},{2,10},{10... | collective-permute-start | bytes 983048 | tf_op jit(solution)/shard_map/ppermute | solution.py:542
  6.4 0.7 collective-permute-start.1
  7.1 2.2 %copy-done = f32[2,2,512,512]{3,2,1,0:T(8,128)S(1)} copy-done((f32[2,2,512,512]{3,2,1,0:T(8,128)S(1)}, f32[2,2,512,512]{3,2,1,0:T(8,128)}, u32[]{:S(2)}) %copy-start) | copy-done | bytes 4194328
  9.6 0.7 collective-permute-start.3
  10.3 3.8 %collective-permute-done.r_0_.r_6_.r_10_ = bf16[20,64,128]{2,1,0:T(8,128)(2,1)S(1)} collective-permute-done((bf16[20,64,128]{2,1,0:T(8,128)(2,1)S(1)}, bf16[20,64,128]{2,1,0:T(8,128)(2,1)S(1)}, u32[]{:S(2)}, u32[]{:S(2)}) %collective-permute-start) | collective-permute-done | bytes 327712 | tf_op jit(solution)/shard_map/ppermute | solution.py:542
  14.3 0.7 collective-permute-start.5
  15.0 1.5 %shard_map.98 = (f32[4,6,640,128]{3,2,1,0:T(8,128)S(1)}, f32[4,6,640,128]{3,2,1,0:T(8,128)S(1)}, bf16[2,128,128]{2,1,0:T(8,128)(2,1)S(1)}, bf16[2,128,128]{2,1,0:T(8,128)(2,1)S(1)}) custom-call(f32[2,2,512,512]{3,2,1,0:T(8,128)S(1)} %copy-done.1, bf16[8,128,128]{2,1,0:T(8,128)(2,1)S(1)} %get-tuple-element.31.r_1_.r_0_, s32[2,256]{1,0:T(2,128)} %bitcast.2, ...), custom_call_target="tpu_custom_call" | custom-call | tf_op jit(solution)/shard_map/pallas_call | solution.py:522
  16.5 3.8 %collective-permute-start.6 = (bf16[2,128,128]{2,1,0:T(8,128)(2,1)S(1)}, bf16[2,128,128]{2,1,0:T(8,128)(2,1)S(1)}, u32[]{:S(2)}, u32[]{:S(2)}) collective-permute-start(bf16[2,128,128]{2,1,0:T(8,128)(2,1)S(1)} %get-tuple-element.45), channel_id=1, source_target_pairs={{0,24},{8,16},{16,8},{24,0},{1,25},{9,17},{17,9},{25,1},{2,26},{10... | collective-permute-start | bytes 196616 | tf_op jit(solution)/shard_map/ppermute | solution.py:542
  20.3 1.1 %collective-permute-start.7 = (bf16[2,128,128]{2,1,0:T(8,128)(2,1)S(1)}, bf16[2,128,128]{2,1,0:T(8,128)(2,1)S(1)}, u32[]{:S(2)}, u32[]{:S(2)}) collective-permute-start(bf16[2,128,128]{2,1,0:T(8,128)(2,1)S(1)} %get-tuple-element.46), channel_id=1, source_target_pairs={{0,16},{8,24},{16,0},{24,8},{1,17},{9,25},{17,1},{25,9},{2,18},{10... | collective-permute-start | bytes 196616 | tf_op jit(solution)/shard_map/ppermute | solution.py:542
  21.5 6.7 %shard_map.99 = (f32[4,6,640,128]{3,2,1,0:T(8,128)S(1)}, f32[8,8,128,128]{3,2,1,0:T(8,128)S(1)}, f32[1,8,8,128,128]{4,3,2,1,0:T(8,128)S(1)}, bf16[256,256]{1,0:T...) custom-call(s32[2,256]{1,0:T(2,128)S(1)} %bitcast.3, ...), custom_call_target="tpu_custom_call", output_to_operand_aliasing={{0}: (12, {})} | custom-call | tf_op jit(solution)/shard_map/pallas_call | solution.py:522
  28.2 8.2 %shard_map.100 = (f32[4,6,640,128]{3,2,1,0:T(8,128)S(1)}, bf16[20,64,128]{2,1,0:T(8,128)(2,1)S(1)}, bf16[20,64,128]{2,1,0:T(8,128)(2,1)S(1)}, f32[4,128,128]{2,1,0:T(8,128)S(1)}, f32[4,128,128]{2,1,0:T(8,128)S(1)}) custom-call(bf16[8,128,128]{2,1,0:T(8,128)(2,1)S(1)} %get-tuple-element.31.r_1_.r_0_, ...), custom_call_target="tpu_custom_call", output_to_operand_aliasing={{0}: (13, {})} | custom-call | tf_op jit(solution)/shard_map/pallas_call | solution.py:522
  36.7 0.7 collective-permute-start.9
  37.4 4.5 %collective-permute-start.12 = (f32[4,128,128]{2,1,0:T(8,128)S(1)}, f32[4,128,128]{2,1,0:T(8,128)S(1)}, u32[]{:S(2)}, u32[]{:S(2)}) collective-permute-start(f32[4,128,128]{2,1,0:T(8,128)S(1)} %get-tuple-element.55), channel_id=1, source_target_pairs={{0,1},{1,0},{2,3},{3,2},{4,5},{5,4},{6,7},{7,6},{8,9},{9,8},{10,11... | collective-permute-start | bytes 786440 | tf_op jit(solution)/shard_map/ppermute | solution.py:542
  41.8 3.1 %collective-permute-done.8.r_1_ = bf16[20,64,128]{2,1,0:T(8,128)(2,1)S(1)} collective-permute-done((bf16[20,64,128]{2,1,0:T(8,128)(2,1)S(1)}, bf16[20,64,128]{2,1,0:T(8,128)(2,1)S(1)}, u32[]{:S(2)}, u32[]{:S(2)}) %collective-permute-start.8) | collective-permute-done | bytes 327712 | tf_op jit(solution)/shard_map/ppermute | solution.py:542
  45.4 2.1 %collective-permute-start.10 = (bf16[2,512,128]{2,1,0:T(8,128)(2,1)S(1)}, bf16[2,512,128]{2,1,0:T(8,128)(2,1)S(1)}, u32[]{:S(2)}, u32[]{:S(2)}) collective-permute-start(bf16[2,512,128]{2,1,0:T(8,128)(2,1)S(1)} %get-tuple-element.52), channel_id=1, source_target_pairs={{0,1},{1,0},{2,3},{3,2},{4,5},{5,4},{6,7},{7,6},{8,9},{9,8},{10,11... | collective-permute-start | bytes 786440 | tf_op jit(solution)/shard_map/ppermute | solution.py:542
  47.4 0.7 collective-permute-start.11
  48.1 4.5 %collective-permute-start.13 = (bf16[128,128]{1,0:T(8,128)(2,1)S(1)}, bf16[128,128]{1,0:T(8,128)(2,1)S(1)}, u32[]{:S(2)}, u32[]{:S(2)}) collective-permute-start(bf16[128,128]{1,0:T(8,128)(2,1)S(1)} %get-tuple-element.57), channel_id=1, source_target_pairs={{0,2},{1,3},{2,0},{3,1},{4,6},{5,7},{6,4},{7,5},{8,10},{9,11},{10,... | collective-permute-start | bytes 98312 | tf_op jit(solution)/shard_map/ppermute | solution.py:542
  52.7 1.9 %collective-permute-start.14 = (bf16[128,128]{1,0:T(8,128)(2,1)S(1)}, bf16[128,128]{1,0:T(8,128)(2,1)S(1)}, u32[]{:S(2)}, u32[]{:S(2)}) collective-permute-start(bf16[128,128]{1,0:T(8,128)(2,1)S(1)} %get-tuple-element.58), channel_id=1, source_target_pairs={{0,4},{1,5},{2,6},{3,7},{4,0},{5,1},{6,2},{7,3},{8,12},{9,13},{10,... | collective-permute-start | bytes 98312 | tf_op jit(solution)/shard_map/ppermute | solution.py:542
  54.5 0.7 collective-permute-start.15
  55.2 4.5 %collective-permute-done.13.refs_0_ = bf16[128,128]{1,0:T(8,128)(2,1)S(1)} collective-permute-done((bf16[128,128]{1,0:T(8,128)(2,1)S(1)}, bf16[128,128]{1,0:T(8,128)(2,1)S(1)}, u32[]{:S(2)}, u32[]{:S(2)}) %collective-permute-start.13) | collective-permute-done | bytes 32800 | tf_op jit(solution)/shard_map/ppermute | solution.py:542
  59.8 4.4 %collective-permute-start.18 = (bf16[128,128]{1,0:T(8,128)(2,1)S(1)}, bf16[128,128]{1,0:T(8,128)(2,1)S(1)}, u32[]{:S(2)}, u32[]{:S(2)}) collective-permute-start(bf16[128,128]{1,0:T(8,128)(2,1)S(1)} %shard_map.105.r_0_), channel_id=1, source_target_pairs={{0,16},{8,24},{16,0},{24,8},{1,17},{9,25},{17,1},{25,9},{2,18},{10... | collective-permute-start | bytes 98312 | tf_op jit(solution)/shard_map/ppermute | solution.py:542
  64.2 2.4 %collective-permute-start.17 = (bf16[128,128]{1,0:T(8,128)(2,1)S(1)}, bf16[128,128]{1,0:T(8,128)(2,1)S(1)}, u32[]{:S(2)}, u32[]{:S(2)}) collective-permute-start(bf16[128,128]{1,0:T(8,128)(2,1)S(1)} %shard_map.105.r_0_), channel_id=1, source_target_pairs={{0,24},{8,16},{16,8},{24,0},{1,25},{9,17},{17,9},{25,1},{2,26},{10... | collective-permute-start | bytes 98312 | tf_op jit(solution)/shard_map/ppermute | solution.py:542
  66.5 3.7 %collective-permute-done.17.r_2_ = bf16[128,128]{1,0:T(8,128)(2,1)S(1)} collective-permute-done((bf16[128,128]{1,0:T(8,128)(2,1)S(1)}, bf16[128,128]{1,0:T(8,128)(2,1)S(1)}, u32[]{:S(2)}, u32[]{:S(2)}) %collective-permute-start.17) | collective-permute-done | bytes 32800 | tf_op jit(solution)/shard_map/ppermute | solution.py:542
  70.6 1.8 %collective-permute-start.21 = (bf16[128,128]{1,0:T(8,128)(2,1)S(1)}, bf16[128,128]{1,0:T(8,128)(2,1)S(1)}, u32[]{:S(2)}, u32[]{:S(2)}) collective-permute-start(bf16[128,128]{1,0:T(8,128)(2,1)S(1)} %shard_map.106.refs_0_), channel_id=1, source_target_pairs={{0,6},{1,7},{2,4},{3,5},{4,2},{5,3},{6,0},{7,1},{8,14},{9,15},{10,... | collective-permute-start | bytes 98312 | tf_op jit(solution)/shard_map/ppermute | solution.py:542
  72.4 1.8 %collective-permute-start.20 = (bf16[128,128]{1,0:T(8,128)(2,1)S(1)}, bf16[128,128]{1,0:T(8,128)(2,1)S(1)}, u32[]{:S(2)}, u32[]{:S(2)}) collective-permute-start(bf16[128,128]{1,0:T(8,128)(2,1)S(1)} %shard_map.106.refs_0_), channel_id=1, source_target_pairs={{0,4},{1,5},{2,6},{3,7},{4,0},{5,1},{6,2},{7,3},{8,12},{9,13},{10,... | collective-permute-start | bytes 98312 | tf_op jit(solution)/shard_map/ppermute | solution.py:542
  74.2 1.5 %collective-permute-done.21.refs_3_ = bf16[128,128]{1,0:T(8,128)(2,1)S(1)} collective-permute-done((bf16[128,128]{1,0:T(8,128)(2,1)S(1)}, bf16[128,128]{1,0:T(8,128)(2,1)S(1)}, u32[]{:S(2)}, u32[]{:S(2)}) %collective-permute-start.21) | collective-permute-done | bytes 32800 | tf_op jit(solution)/shard_map/ppermute | solution.py:542
  75.7 0.6 collective-permute-done.20.refs_2_
  76.3 1.8 %collective-permute-done.19.refs_1_ = bf16[128,128]{1,0:T(8,128)(2,1)S(1)} collective-permute-done((bf16[128,128]{1,0:T(8,128)(2,1)S(1)}, bf16[128,128]{1,0:T(8,128)(2,1)S(1)}, u32[]{:S(2)}, u32[]{:S(2)}) %collective-permute-start.19) | collective-permute-done | bytes 32800 | tf_op jit(solution)/shard_map/ppermute | solution.py:542
  78.2 1.7 %shard_map.102.old = f32[2,2,512,512]{3,2,1,0:T(8,128)} custom-call(f32[2,2,512,512]{3,2,1,0:T(8,128)S(1)} %copy-done.1, f32[4,6,640,128]{3,2,1,0:T(8,128)S(1)} %get-tuple-element.51.grad, f32[4,2,128,128]{3,2,1,0:T(8,128)S(1)} %copy-done.2), custom_call_target="tpu_custom_call" | custom-call | tf_op jit(solution)/shard_map/pallas_call | solution.py:522
  79.9 1.1 %shard_map.108 = f32[4,2,128,128]{3,2,1,0:T(8,128)} custom-call(f32[4,2,128,128]{3,2,1,0:T(8,128)S(1)} %copy-done.2, bf16[4,128,128]{2,1,0:T(8,128)(2,1)S(1)} %shard_map.107.joined, bf16[4,128,128]{2,1,0:T(8,128)(2,1)S(1)} %collective-permute-done.22.other), custom_call_target="tpu_custom_call" | custom-call | tf_op jit(solution)/shard_map/pallas_call | solution.py:522
  81.1 2.0 %shard_map.103 = f32[2,2,512,512]{3,2,1,0:T(8,128)} custom-call(f32[2,2,512,512]{3,2,1,0:T(8,128)S(1)} %copy-done.1, f32[4,6,640,128]{3,2,1,0:T(8,128)S(1)} %get-tuple-element.51.grad, bf16[2,512,128]{2,1,0:T(8,128)(2,1)S(1)} %collective-permute-done.10.tx_a, bf16[2,512,128]{2,1,0:T(8,128)(2,1)S(1)} %collective-permute-done.11.tx_b, ...), custom_call_target="tpu_custom_call", output_to_operand_aliasing={{}: (5, {})} | custom-call | tf_op jit(solution)/shard_map/pallas_call | solution.py:522
  (38 shorter events, 1.7 us)
Async XLA Ops:
  0.6 14.3 %copy-start.1 = (f32[2,2,512,512]{3,2,1,0:T(8,128)S(1)}, f32[2,2,512,512]{3,2,1,0:T(8,128)}, u32[]{:S(2)}) copy-start(f32[2,2,512,512]{3,2,1,0:T(8,128)} %obj.5) | copy-start | bytes 12582916
  0.6 20.8 %copy-start.4 = (s32[32]{0:T(128)S(1)}, s32[32]{0:T(128)}, u32[]{:S(2)}) copy-start(s32[32]{0:T(128)} %r_2_.3) | copy-start | bytes 388
  0.7 20.8 %copy-start.3 = (s32[256,2]{0,1:T(2,128)S(1)}, s32[256,2]{0,1:T(2,128)}, u32[]{:S(2)}) copy-start(s32[256,2]{0,1:T(2,128)} %param.11) | copy-start | bytes 6148
  3.3 10.8 %collective-permute-start = (bf16[20,64,128]{2,1,0:T(8,128)(2,1)S(1)}, bf16[20,64,128]{2,1,0:T(8,128)(2,1)S(1)}, u32[]{:S(2)}, u32[]{:S(2)}) collective-permute-start(bf16[20,64,128]{2,1,0:T(8,128)(2,1)S(1)} %get-tuple-element.32), channel_id=1, source_target_pairs={{0,8},{8,0},{16,24},{24,16},{1,9},{9,1},{17,25},{25,17},{2,10},{10... | collective-permute-start | bytes 983048 | tf_op jit(solution)/shard_map/ppermute | solution.py:542
  6.4 3.9 %collective-permute-start.1 = (bf16[16,64,128]{2,1,0:T(8,128)(2,1)S(1)}, bf16[16,64,128]{2,1,0:T(8,128)(2,1)S(1)}, u32[]{:S(2)}, u32[]{:S(2)}) collective-permute-start(bf16[16,64,128]{2,1,0:T(8,128)(2,1)S(1)} %get-tuple-element.33), channel_id=1, source_target_pairs={{8,16},{16,8},{9,17},{17,9},{10,18},{18,10},{11,19},{19,11},{12,20... | collective-permute-start | bytes 786440 | tf_op jit(solution)/shard_map/ppermute | solution.py:542
  7.1 2.2 %copy-start = (f32[2,2,512,512]{3,2,1,0:T(8,128)S(1)}, f32[2,2,512,512]{3,2,1,0:T(8,128)}, u32[]{:S(2)}) copy-start(f32[2,2,512,512]{3,2,1,0:T(8,128)} %obj.5) | copy-start | bytes 12582916
  9.2 12.2 %copy-start.2 = (f32[4,2,128,128]{3,2,1,0:T(8,128)S(1)}, f32[4,2,128,128]{3,2,1,0:T(8,128)}, u32[]{:S(2)}) copy-start(f32[4,2,128,128]{3,2,1,0:T(8,128)} %probe.5) | copy-start | bytes 1572868
  9.5 10.8 %collective-permute-start.2 = (bf16[2,512,128]{2,1,0:T(8,128)(2,1)S(1)}, bf16[2,512,128]{2,1,0:T(8,128)(2,1)S(1)}, u32[]{:S(2)}, u32[]{:S(2)}) collective-permute-start(bf16[2,512,128]{2,1,0:T(8,128)(2,1)S(1)} %get-tuple-element.34), channel_id=1, source_target_pairs={{0,1},{1,0},{2,3},{3,2},{4,5},{5,4},{6,7},{7,6},{8,9},{9,8},{10,11... | collective-permute-start | bytes 786440 | tf_op jit(solution)/shard_map/ppermute | solution.py:542
  9.6 11.8 %collective-permute-start.3 = (bf16[2,512,128]{2,1,0:T(8,128)(2,1)S(1)}, bf16[2,512,128]{2,1,0:T(8,128)(2,1)S(1)}, u32[]{:S(2)}, u32[]{:S(2)}) collective-permute-start(bf16[2,512,128]{2,1,0:T(8,128)(2,1)S(1)} %get-tuple-element.35), channel_id=1, source_target_pairs={{1,2},{2,1},{3,4},{4,3},{5,6},{6,5},{9,10},{10,9},{11,12},{12,11},... | collective-permute-start | bytes 786440 | tf_op jit(solution)/shard_map/ppermute | solution.py:542
  14.2 7.2 %collective-permute-start.4 = (bf16[4,64,128]{2,1,0:T(8,128)(2,1)S(1)}, bf16[4,64,128]{2,1,0:T(8,128)(2,1)S(1)}, u32[]{:S(2)}, u32[]{:S(2)}) collective-permute-start(bf16[4,64,128]{2,1,0:T(8,128)(2,1)S(1)} %get-tuple-element.36), channel_id=1, source_target_pairs={{0,1},{1,0},{2,3},{3,2},{4,5},{5,4},{6,7},{7,6},{8,9},{9,8},{10,11... | collective-permute-start | bytes 196616 | tf_op jit(solution)/shard_map/ppermute | solution.py:542
  14.3 7.1 %collective-permute-start.5 = (bf16[4,64,128]{2,1,0:T(8,128)(2,1)S(1)}, bf16[4,64,128]{2,1,0:T(8,128)(2,1)S(1)}, u32[]{:S(2)}, u32[]{:S(2)}) collective-permute-start(bf16[4,64,128]{2,1,0:T(8,128)(2,1)S(1)} %get-tuple-element.37), channel_id=1, source_target_pairs={{1,2},{2,1},{3,4},{4,3},{5,6},{6,5},{9,10},{10,9},{11,12},{12,11},... | collective-permute-start | bytes 196616 | tf_op jit(solution)/shard_map/ppermute | solution.py:542
  16.5 11.7 %collective-permute-start.6 = (bf16[2,128,128]{2,1,0:T(8,128)(2,1)S(1)}, bf16[2,128,128]{2,1,0:T(8,128)(2,1)S(1)}, u32[]{:S(2)}, u32[]{:S(2)}) collective-permute-start(bf16[2,128,128]{2,1,0:T(8,128)(2,1)S(1)} %get-tuple-element.45), channel_id=1, source_target_pairs={{0,24},{8,16},{16,8},{24,0},{1,25},{9,17},{17,9},{25,1},{2,26},{10... | collective-permute-start | bytes 196616 | tf_op jit(solution)/shard_map/ppermute | solution.py:542
  20.3 7.9 %collective-permute-start.7 = (bf16[2,128,128]{2,1,0:T(8,128)(2,1)S(1)}, bf16[2,128,128]{2,1,0:T(8,128)(2,1)S(1)}, u32[]{:S(2)}, u32[]{:S(2)}) collective-permute-start(bf16[2,128,128]{2,1,0:T(8,128)(2,1)S(1)} %get-tuple-element.46), channel_id=1, source_target_pairs={{0,16},{8,24},{16,0},{24,8},{1,17},{9,25},{17,1},{25,9},{2,18},{10... | collective-permute-start | bytes 196616 | tf_op jit(solution)/shard_map/ppermute | solution.py:542
  36.4 8.5 %collective-permute-start.8 = (bf16[20,64,128]{2,1,0:T(8,128)(2,1)S(1)}, bf16[20,64,128]{2,1,0:T(8,128)(2,1)S(1)}, u32[]{:S(2)}, u32[]{:S(2)}) collective-permute-start(bf16[20,64,128]{2,1,0:T(8,128)(2,1)S(1)} %get-tuple-element.49), channel_id=1, source_target_pairs={{0,8},{8,0},{16,24},{24,16},{1,9},{9,1},{17,25},{25,17},{2,10},{10... | collective-permute-start | bytes 983048 | tf_op jit(solution)/shard_map/ppermute | solution.py:542
  36.7 8.2 %collective-permute-start.9 = (bf16[20,64,128]{2,1,0:T(8,128)(2,1)S(1)}, bf16[20,64,128]{2,1,0:T(8,128)(2,1)S(1)}, u32[]{:S(2)}, u32[]{:S(2)}) collective-permute-start(bf16[20,64,128]{2,1,0:T(8,128)(2,1)S(1)} %get-tuple-element.50), channel_id=1, source_target_pairs={{8,16},{16,8},{9,17},{17,9},{10,18},{18,10},{11,19},{19,11},{12,20... | collective-permute-start | bytes 983048 | tf_op jit(solution)/shard_map/ppermute | solution.py:542
  37.4 10.7 %collective-permute-start.12 = (f32[4,128,128]{2,1,0:T(8,128)S(1)}, f32[4,128,128]{2,1,0:T(8,128)S(1)}, u32[]{:S(2)}, u32[]{:S(2)}) collective-permute-start(f32[4,128,128]{2,1,0:T(8,128)S(1)} %get-tuple-element.55), channel_id=1, source_target_pairs={{0,1},{1,0},{2,3},{3,2},{4,5},{5,4},{6,7},{7,6},{8,9},{9,8},{10,11... | collective-permute-start | bytes 786440 | tf_op jit(solution)/shard_map/ppermute | solution.py:542
  45.4 35.7 %collective-permute-start.10 = (bf16[2,512,128]{2,1,0:T(8,128)(2,1)S(1)}, bf16[2,512,128]{2,1,0:T(8,128)(2,1)S(1)}, u32[]{:S(2)}, u32[]{:S(2)}) collective-permute-start(bf16[2,512,128]{2,1,0:T(8,128)(2,1)S(1)} %get-tuple-element.52), channel_id=1, source_target_pairs={{0,1},{1,0},{2,3},{3,2},{4,5},{5,4},{6,7},{7,6},{8,9},{9,8},{10,11... | collective-permute-start | bytes 786440 | tf_op jit(solution)/shard_map/ppermute | solution.py:542
  47.4 33.7 %collective-permute-start.11 = (bf16[2,512,128]{2,1,0:T(8,128)(2,1)S(1)}, bf16[2,512,128]{2,1,0:T(8,128)(2,1)S(1)}, u32[]{:S(2)}, u32[]{:S(2)}) collective-permute-start(bf16[2,512,128]{2,1,0:T(8,128)(2,1)S(1)} %get-tuple-element.53), channel_id=1, source_target_pairs={{1,2},{2,1},{3,4},{4,3},{5,6},{6,5},{9,10},{10,9},{11,12},{12,11},... | collective-permute-start | bytes 786440 | tf_op jit(solution)/shard_map/ppermute | solution.py:542
  48.1 11.6 %collective-permute-start.13 = (bf16[128,128]{1,0:T(8,128)(2,1)S(1)}, bf16[128,128]{1,0:T(8,128)(2,1)S(1)}, u32[]{:S(2)}, u32[]{:S(2)}) collective-permute-start(bf16[128,128]{1,0:T(8,128)(2,1)S(1)} %get-tuple-element.57), channel_id=1, source_target_pairs={{0,2},{1,3},{2,0},{3,1},{4,6},{5,7},{6,4},{7,5},{8,10},{9,11},{10,... | collective-permute-start | bytes 98312 | tf_op jit(solution)/shard_map/ppermute | solution.py:542
  52.7 7.1 %collective-permute-start.14 = (bf16[128,128]{1,0:T(8,128)(2,1)S(1)}, bf16[128,128]{1,0:T(8,128)(2,1)S(1)}, u32[]{:S(2)}, u32[]{:S(2)}) collective-permute-start(bf16[128,128]{1,0:T(8,128)(2,1)S(1)} %get-tuple-element.58), channel_id=1, source_target_pairs={{0,4},{1,5},{2,6},{3,7},{4,0},{5,1},{6,2},{7,3},{8,12},{9,13},{10,... | collective-permute-start | bytes 98312 | tf_op jit(solution)/shard_map/ppermute | solution.py:542
  54.5 5.2 %collective-permute-start.15 = (bf16[128,128]{1,0:T(8,128)(2,1)S(1)}, bf16[128,128]{1,0:T(8,128)(2,1)S(1)}, u32[]{:S(2)}, u32[]{:S(2)}) collective-permute-start(bf16[128,128]{1,0:T(8,128)(2,1)S(1)} %get-tuple-element.59), channel_id=1, source_target_pairs={{0,6},{1,7},{2,4},{3,5},{4,2},{5,3},{6,0},{7,1},{8,14},{9,15},{10,... | collective-permute-start | bytes 98312 | tf_op jit(solution)/shard_map/ppermute | solution.py:542
  59.8 6.8 %collective-permute-start.18 = (bf16[128,128]{1,0:T(8,128)(2,1)S(1)}, bf16[128,128]{1,0:T(8,128)(2,1)S(1)}, u32[]{:S(2)}, u32[]{:S(2)}) collective-permute-start(bf16[128,128]{1,0:T(8,128)(2,1)S(1)} %shard_map.105.r_0_), channel_id=1, source_target_pairs={{0,16},{8,24},{16,0},{24,8},{1,17},{9,25},{17,1},{25,9},{2,18},{10... | collective-permute-start | bytes 98312 | tf_op jit(solution)/shard_map/ppermute | solution.py:542
  64.2 6.1 %collective-permute-start.17 = (bf16[128,128]{1,0:T(8,128)(2,1)S(1)}, bf16[128,128]{1,0:T(8,128)(2,1)S(1)}, u32[]{:S(2)}, u32[]{:S(2)}) collective-permute-start(bf16[128,128]{1,0:T(8,128)(2,1)S(1)} %shard_map.105.r_0_), channel_id=1, source_target_pairs={{0,24},{8,16},{16,8},{24,0},{1,25},{9,17},{17,9},{25,1},{2,26},{10... | collective-permute-start | bytes 98312 | tf_op jit(solution)/shard_map/ppermute | solution.py:542
  66.5 4.0 %collective-permute-start.16 = (bf16[128,128]{1,0:T(8,128)(2,1)S(1)}, bf16[128,128]{1,0:T(8,128)(2,1)S(1)}, u32[]{:S(2)}, u32[]{:S(2)}) collective-permute-start(bf16[128,128]{1,0:T(8,128)(2,1)S(1)} %shard_map.105.r_0_), channel_id=1, source_target_pairs={{0,8},{8,0},{16,24},{24,16},{1,9},{9,1},{17,25},{25,17},{2,10},{10... | collective-permute-start | bytes 98312 | tf_op jit(solution)/shard_map/ppermute | solution.py:542
  70.6 5.1 %collective-permute-start.21 = (bf16[128,128]{1,0:T(8,128)(2,1)S(1)}, bf16[128,128]{1,0:T(8,128)(2,1)S(1)}, u32[]{:S(2)}, u32[]{:S(2)}) collective-permute-start(bf16[128,128]{1,0:T(8,128)(2,1)S(1)} %shard_map.106.refs_0_), channel_id=1, source_target_pairs={{0,6},{1,7},{2,4},{3,5},{4,2},{5,3},{6,0},{7,1},{8,14},{9,15},{10,... | collective-permute-start | bytes 98312 | tf_op jit(solution)/shard_map/ppermute | solution.py:542
  72.4 3.9 %collective-permute-start.20 = (bf16[128,128]{1,0:T(8,128)(2,1)S(1)}, bf16[128,128]{1,0:T(8,128)(2,1)S(1)}, u32[]{:S(2)}, u32[]{:S(2)}) collective-permute-start(bf16[128,128]{1,0:T(8,128)(2,1)S(1)} %shard_map.106.refs_0_), channel_id=1, source_target_pairs={{0,4},{1,5},{2,6},{3,7},{4,0},{5,1},{6,2},{7,3},{8,12},{9,13},{10,... | collective-permute-start | bytes 98312 | tf_op jit(solution)/shard_map/ppermute | solution.py:542
  74.2 3.9 %collective-permute-start.19 = (bf16[128,128]{1,0:T(8,128)(2,1)S(1)}, bf16[128,128]{1,0:T(8,128)(2,1)S(1)}, u32[]{:S(2)}, u32[]{:S(2)}) collective-permute-start(bf16[128,128]{1,0:T(8,128)(2,1)S(1)} %shard_map.106.refs_0_), channel_id=1, source_target_pairs={{0,2},{1,3},{2,0},{3,1},{4,6},{5,7},{6,4},{7,5},{8,10},{9,11},{10,... | collective-permute-start | bytes 98312 | tf_op jit(solution)/shard_map/ppermute | solution.py:542
  78.1 1.8 %collective-permute-start.22 = (bf16[4,128,128]{2,1,0:T(8,128)(2,1)S(1)}, bf16[4,128,128]{2,1,0:T(8,128)(2,1)S(1)}, u32[]{:S(2)}, u32[]{:S(2)}) collective-permute-start(bf16[4,128,128]{2,1,0:T(8,128)(2,1)S(1)} %shard_map.107.joined), channel_id=1, source_target_pairs={{0,1},{1,0},{2,3},{3,2},{4,5},{5,4},{6,7},{7,6},{8,9},{9,8},{10,11... | collective-permute-start | bytes 393224 | tf_op jit(solution)/shard_map/ppermute | solution.py:542

commit v3 on v2

--- a/solution.py
+++ b/solution.py
@@ -114,57 +114,75 @@
     return found, ys, xs, lives
 
 
-def rows_kernel(sizes, obj, pat, pos, cnt, ty_a, ty_b, held, rows, sems):
-    planes, tile, margin = obj.shape[0] * 2, obj.shape[2], rows.shape[3]
-    tiles = obj.shape[3] // LANES
+def pack_kernel(sizes, obj, pat, pos_in, cnt_in, ty_a, ty_b, tx_a, tx_b, held, rows, columns, pos, cnt, sems):
+    slices, tile, margin = obj.shape[0], obj.shape[2], rows.shape[3]
+    planes, tiles = slices * 2, obj.shape[3] // LANES
     row, col = lax.axis_index("ty"), lax.axis_index("tx")
-    up_y = ups(row)
-    copies = [pltpu.make_async_copy(pat, held, sems.at[2])]
+    up_y, up_x = ups(row), ups(col)
+    copies = [
+        pltpu.make_async_copy(pos_in, pos, sems.at[0]),
+        pltpu.make_async_copy(cnt_in, cnt, sems.at[1]),
+        pltpu.make_async_copy(pat, held, sems.at[2]),
+    ]
     for k in range(2):
         start = pl.multiple_of(up_y[k] * (tile - margin), margin)
-        copies.append(pltpu.make_async_copy(obj.at[:, :, pl.ds(start, margin), :], rows.at[k], sems.at[k]))
+        copies.append(pltpu.make_async_copy(obj.at[:, :, pl.ds(start, margin), :], rows.at[k], sems.at[3 + k]))
+    for j in range(2):
+        lane = pl.multiple_of(up_x[j] * (tile - LANES), LANES)
+        copies.append(pltpu.make_async_copy(obj.at[:, :, :, pl.ds(lane, LANES)], columns.at[j], sems.at[5 + j]))
     for copy in copies:
         copy.start()
+    for copy in copies[:3]:
+        copy.wait()
     target = pick(row, sizes[2][0]) * tile
     found = slot_scan(pos, cnt, sizes, row, col, pat.shape[0], target, tile)[0]
-    copies[0].wait()
     for c in range(CAP):
         for h in range(2):
             ty_a[planes * tiles + 2 * c + h] = held[found[c], h * margin : (h + 1) * margin, :]
     for k, out in enumerate((ty_a, ty_b)):
-        copies[1 + k].wait()
+        copies[3 + k].wait()
         for p in range(planes):
             for t in range(tiles):
                 block = rows[k, p // 2, p % 2, :, t * LANES : (t + 1) * LANES]
                 out[p * tiles + t] = block.astype(BF16)
-
-
-def columns_kernel(obj, tx_a, tx_b):
-    slices, tile = obj.shape[0], obj.shape[2]
-    up_x = ups(lax.axis_index("tx"))
     for j, out in enumerate((tx_a, tx_b)):
-        lane = pl.ds(pl.multiple_of(up_x[j] * (tile - LANES), LANES), LANES)
+        copies[5 + j].wait()
         for s in range(slices):
-            re, im = obj[s, 0, :, lane], obj[s, 1, :, lane]
+            re, im = columns[j, s, 0], columns[j, s, 1]
             packed = jnp.where(half_mask(tile, up_x[j]), re, pltpu.roll(im, LANES // 2, 1))
             out[s] = packed.astype(BF16)
 
 
-def tile_kernel(sizes, obj, pat, pos, cnt, ext, grad, *routed):
+def tile_kernel(sizes, obj, pat, pos, cnt, *refs):
     rounds = sizes[2]
+    sources, ext, grad = refs[:3], refs[3], refs[4]
+    routed, near_tables, sems = refs[5:-4], refs[-4:-1], refs[-1]
     slices, tile = obj.shape[0], obj.shape[2]
     tiles = obj.shape[3] // LANES
     margin = (ext.shape[2] - tile) // 2
+    copies = []
+    for p in range(slices * 2):
+        for t in range(tiles):
+            copies.append(
+                pltpu.make_async_copy(
+                    obj.at[p // 2, p % 2, :, t * LANES : (t + 1) * LANES],
+                    ext.at[p, 1 + t, margin : margin + tile, :],
+                    sems.at[p * tiles + t],
+                )
+            )
+    for i, (a, b) in enumerate(zip(sources, near_tables)):
+        copies.append(pltpu.make_async_copy(a, b, sems.at[slices * 2 * tiles + i]))
+    for copy in copies:
+        copy.start()
     row, col = lax.axis_index("ty"), lax.axis_index("tx")
     targets = [pick(row, partner) * tile for partner in rounds[1:]]
     found = [slot_scan(pos, cnt, sizes, row, col, pat.shape[0], t, tile)[0] for t in targets]
     for k, out in enumerate(routed):
         for c in range(CAP):
             out[c] = pat[found[k][c]]
-    for p in range(slices * 2):
-        for t in range(tiles):
-            ext[p, 1 + t, margin : margin + tile] = obj[p // 2, p % 2, :, t * LANES : (t + 1) * LANES]
     grad[...] = jnp.zeros(grad.shape, F32)
+    for copy in copies:
+        copy.wait()
 
 
 def corner_kernel(slices, tiles, ty_a, ty_b, out_a, out_b):
@@ -232,16 +250,9 @@
     return pltpu.roll(jnp.where(upper, v0, v1), (LANES - off) & (LANES - 1), 1)
 
 
-def forward_kernel(sizes, per_device, pos, cnt, probe, *refs):
-    sources, refs = refs[:3], refs[3:]
+def forward_kernel(sizes, per_device, pos, cnt, probe, first, second, kern, *refs):
     ty_in, tx_in, corner_in = refs[:2], refs[2:4], refs[4:6]
-    ext, psi, waves, first, second, kern, row_of, col_of, sems = refs[7:]
-    copies = [
-        pltpu.make_async_copy(a, b, sems.at[i])
-        for i, (a, b) in enumerate(zip(sources, (first, second, kern)))
-    ]
-    for copy in copies:
-        copy.start()
+    ext, psi, waves, row_of, col_of = refs[7:]
     modes, extent = probe.shape[0], probe.shape[2]
     planes, margin, tiles = ext.shape[0], extent // 2, ext.shape[1] - 2
     slices, tile = planes // 2, ext.shape[2] - extent
@@ -265,8 +276,6 @@
             ext[2 * s, side, margin : margin + tile] = strip
             ext[2 * s + 1, side, margin : margin + tile] = pltpu.roll(strip, LANES // 2, 1)
     lanes = lane_ids(extent)
-    for copy in copies:
-        copy.wait()
 
     def body(i, carry):
         slots = [i * BATCH + b for b in range(BATCH)]
@@ -557,16 +566,22 @@
     strips = [pltpu.VMEM((slices, tile, LANES), BF16)] * 2
     strips = [pltpu.VMEM((slices, tile, LANES), BF16)] * 2
     rows_out = [pltpu.VMEM((parts + 2 * slices,) + block, BF16)] * 2
-    ty_a, ty_b, near_patterns = call(
-        lambda *r: rows_kernel(sizes, *r),
+    ty_a, ty_b, tx_a, tx_b, near_patterns = call(
+        lambda *r: pack_kernel(sizes, *r),
         (far(object_slices), far(patterns), far(places), far(counts)),
-        [ANY, ANY, SMEM, SMEM],
+        [ANY] * 4,
         [pltpu.VMEM((parts + extra,) + block, BF16) for extra in (2 * CAP, 0)]
+        + strips
         + [pltpu.VMEM(patterns.shape, BF16)],
-        [pltpu.VMEM((2, slices, 2, margin, tile), F32), pltpu.SemaphoreType.DMA((3,))],
+        [
+            pltpu.VMEM((2, slices, 2, margin, tile), F32),
+            pltpu.VMEM((2, slices, 2, tile, LANES), F32),
+            pltpu.SMEM(places.shape, jnp.int32),
+            pltpu.SMEM(counts.shape, jnp.int32),
+            pltpu.SemaphoreType.DMA((7,)),
+        ],
     )
     near_object, near_patterns = near(object_slices), near(near_patterns)
-    tx_a, tx_b = call(columns_kernel, (near_object,), [VMEM], strips)
 
     def pair_rows(value, k):
         return send(value, "ty", [(i, rounds[k][i]) for i in range(n_ty)])
@@ -580,12 +595,18 @@
     ext_shape = (planes, tiles + 2, tile + extent, LANES)
     ty_in = [swap(ty_a, "ty", 0), swap(ty_b, "ty", 1)]
     tx_in = [swap(tx_a, "tx", 0), swap(tx_b, "tx", 1)]
-    ext, grad, *routed = call(
+    tables = make_tables(extent)
+    ext, grad, *routed, first, second, kern = call(
         lambda *r: tile_kernel(sizes, *r),
-        (near_object, near_patterns, far(places), far(counts)),
-        [VMEM, VMEM, SMEM, SMEM],
-        [pltpu.VMEM(ext_shape, F32)] * 2 + [pltpu.VMEM((CAP, extent, extent), BF16)] * (k_n - 1),
-    )
+        (far(object_slices), near_patterns, far(places), far(counts))
+        + tuple(far(c) for c in tables),
+        [ANY, VMEM, SMEM, SMEM] + [ANY] * 3,
+        [pltpu.VMEM(ext_shape, F32)] * 2
+        + [pltpu.VMEM((CAP, extent, extent), BF16)] * (k_n - 1)
+        + [pltpu.VMEM(c.shape, c.dtype) for c in tables],
+        [pltpu.SemaphoreType.DMA((parts + 3,))],
+    )
+    constants = tuple(near(c) for c in (first, second, kern))
     corners = call(
         lambda *r: corner_kernel(slices, tiles, *r),
         tuple(ty_in),
@@ -595,35 +616,32 @@
     corner_in = [swap(corners[j], "tx", j) for j in range(2)]
     pat_in = [ty_in[0]] + [pair_rows(routed[k - 1], k) for k in range(1, k_n)]
 
-    first, second, kern = make_tables(extent)
     slots = (k_n + 1) * CAP
     chunk = modes * 2 * extent // n_tx
-    constants = (first, second, kern)
     field = (slots, 2 * modes, extent, extent)
-    tables = [pltpu.SMEM((slots,), jnp.int32)] * 2
-    ext, psi, waves, *constants = call(
+    places_near = [pltpu.SMEM((slots,), jnp.int32)] * 2
+    ext, psi, waves = call(
         lambda *r: forward_kernel(sizes, patterns.shape[0], *r),
         (places, counts, near(probe_modes))
-        + tuple(far(c) for c in constants)
+        + constants
         + tuple(ty_in + tx_in + corner_in)
         + (near(ext),),
-        [SMEM, SMEM, VMEM] + [ANY] * 3 + [VMEM] * 7,
-        [pltpu.VMEM(ext_shape, F32), pltpu.VMEM(field, F32), pltpu.VMEM((slices - 1,) + field, F32)]
-        + [pltpu.VMEM(c.shape, c.dtype) for c in constants],
-        tables + [pltpu.SemaphoreType.DMA((3,))],
+        [SMEM, SMEM] + [VMEM] * 11,
+        [pltpu.VMEM(ext_shape, F32), pltpu.VMEM(field, F32), pltpu.VMEM((slices - 1,) + field, F32)],
+        places_near,
         {12: 0},
     )
     results = call(
         lambda *r: backward_kernel(sizes, *r),
         (near_patterns, places, counts, near(probe_modes))
-        + tuple(near(c) for c in constants)
+        + constants
         + (near(ext), near(psi), near(waves), *pat_in, near(grad)),
         [VMEM, SMEM, SMEM] + [VMEM] * (7 + k_n + 1),
         [pltpu.VMEM(ext_shape, F32)]
         + rows_out
         + [pltpu.VMEM((n_tx // 2, chunk, LANES), F32)] * 2,
         [pltpu.VMEM((slots, extent, extent), BF16), pltpu.VMEM((2 * modes, extent, extent), F32)]
-        + tables
+        + places_near
         + [pltpu.SMEM((slots,), F32)],
         {10 + k_n: 0},
     )

time: 83.4 us -> 84.3 us (1.011)
  waiting for transfers between devices: 19.3 us -> 24.7 us
  local copies, waits for them, and re-layouts: 2.21 us -> 0.02 us
  starting transfers between devices: 35.9 us -> 33.8 us
    ppermute x23, waiting for transfers between devices: 19.3 us -> 24.7 us  [send(): return near(lax.ppermute(value, axis, pairs))]
    unnamed x10 -> x8, local copies, waits for them, and re-layouts: 2.21 us -> 0.02 us
    ppermute x23, starting transfers between devices: 35.9 us -> 33.8 us  [send(): return near(lax.ppermute(value, axis, pairs))]
    pallas_call x14 -> x13, Pallas kernels: 24.8 us -> 24.7 us  [call(): pl.pallas_call(kernel, out_shape=outs, in_specs=specs, out_specs=out_spec...]
  transfers between devices with their start and end apart: 23 -> 23, of which waited for: 8 -> 8; matrix products, arithmetic and copies ran while one was open for 0% -> 0% of each run, Pallas kernels for 14% -> 15%
where the time goes in v3:
time: 84.3 us; the launch traced here: 84 us
  starting transfers between devices  33.8 us (40%)
  Pallas kernels  24.7 us (29%)
  waiting for transfers between devices  24.7 us (29%)
  between operations  0.89 us (1%)
    ppermute x23, starting transfers between devices, send(): return near(lax.ppermute(value, axis, pairs))  33.8 us
    ppermute x23, waiting for transfers between devices, send(): return near(lax.ppermute(value, axis, pairs))  24.7 us
    pallas_call x13, Pallas kernels, call(): pl.pallas_call(kernel, out_shape=outs, in_specs=specs, out_specs=out_spec...  24.7 us
  transfers between devices with their start and end apart: 23, of which 8 were waited for; matrix products, arithmetic and copies ran while one was open for 0% of the time, Pallas kernels for 15%

profile of v3, /device:TPU:0, one launch (start us, length us, event | category | flops | bytes accessed | tf_op | source)
XLA Modules:
  0.0 84.0 jit_solution(116058471207889022)
XLA Ops:
  0.7 2.2 %shard_map.95 = (bf16[20,64,128]{2,1,0:T(8,128)(2,1)S(1)}, bf16[16,64,128]{2,1,0:T(8,128)(2,1)S(1)}, bf16[2,512,128]{2,1,0:T(8,128)(2,1)S(1)}, bf16[2,512,128]{2,1,0:T(8,128)(2,1)S(1)}, bf16[8,128,128]{2,1,0:T(8,128)(2,1)S(1)}) custom-call(f32[2,2,512,512]{3,2,1,0:T(8,128)} %obj.3, bf16[8,128,128]{2,1,0:T(8,128)(2,1)} %r_1_.2, s32[2,256]{1,0:T(2,128)} %bitcast.1, ...), custom_call_target="tpu_custom_call" | custom-call | tf_op jit(solution)/shard_map/pallas_call | solution.py:531
  2.9 3.1 %collective-permute-start = (bf16[20,64,128]{2,1,0:T(8,128)(2,1)S(1)}, bf16[20,64,128]{2,1,0:T(8,128)(2,1)S(1)}, u32[]{:S(2)}, u32[]{:S(2)}) collective-permute-start(bf16[20,64,128]{2,1,0:T(8,128)(2,1)S(1)} %get-tuple-element.35), channel_id=1, source_target_pairs={{0,8},{8,0},{16,24},{24,16},{1,9},{9,1},{17,25},{25,17},{2,10},{10... | collective-permute-start | bytes 983048 | tf_op jit(solution)/shard_map/ppermute | solution.py:551
  6.0 0.7 collective-permute-start.1
  6.8 0.7 collective-permute-start.3
  7.4 6.3 %collective-permute-done.r_0_.r_6_.r_10_ = bf16[20,64,128]{2,1,0:T(8,128)(2,1)S(1)} collective-permute-done((bf16[20,64,128]{2,1,0:T(8,128)(2,1)S(1)}, bf16[20,64,128]{2,1,0:T(8,128)(2,1)S(1)}, u32[]{:S(2)}, u32[]{:S(2)}) %collective-permute-start) | collective-permute-done | bytes 327712 | tf_op jit(solution)/shard_map/ppermute | solution.py:551
  13.9 0.7 collective-permute-start.5
  14.6 3.2 %shard_map.96 = (f32[4,6,640,128]{3,2,1,0:T(8,128)S(1)}, f32[4,6,640,128]{3,2,1,0:T(8,128)S(1)}, bf16[2,128,128]{2,1,0:T(8,128)(2,1)S(1)}, bf16[2,128,128]{2,1,0...) custom-call(f32[2,2,512,512]{3,2,1,0:T(8,128)} %obj.3, ...), custom_call_target="tpu_custom_call" | custom-call | tf_op jit(solution)/shard_map/pallas_call | solution.py:531
  17.8 3.8 %collective-permute-start.6 = (bf16[2,128,128]{2,1,0:T(8,128)(2,1)S(1)}, bf16[2,128,128]{2,1,0:T(8,128)(2,1)S(1)}, u32[]{:S(2)}, u32[]{:S(2)}) collective-permute-start(bf16[2,128,128]{2,1,0:T(8,128)(2,1)S(1)} %get-tuple-element.45), channel_id=1, source_target_pairs={{0,24},{8,16},{16,8},{24,0},{1,25},{9,17},{17,9},{25,1},{2,26},{10... | collective-permute-start | bytes 196616 | tf_op jit(solution)/shard_map/ppermute | solution.py:551
  21.6 1.1 %collective-permute-start.7 = (bf16[2,128,128]{2,1,0:T(8,128)(2,1)S(1)}, bf16[2,128,128]{2,1,0:T(8,128)(2,1)S(1)}, u32[]{:S(2)}, u32[]{:S(2)}) collective-permute-start(bf16[2,128,128]{2,1,0:T(8,128)(2,1)S(1)} %get-tuple-element.46), channel_id=1, source_target_pairs={{0,16},{8,24},{16,0},{24,8},{1,17},{9,25},{17,1},{25,9},{2,18},{10... | collective-permute-start | bytes 196616 | tf_op jit(solution)/shard_map/ppermute | solution.py:551
  22.7 5.8 %shard_map.98 = (f32[4,6,640,128]{3,2,1,0:T(8,128)S(1)}, f32[8,8,128,128]{3,2,1,0:T(8,128)S(1)}, f32[1,8,8,128,128]{4,3,2,1,0:T(8,128)S(1)}) custom-call(s32[2,256]{1,0:T(2,128)S(1)} %bitcast.3, s32[32]{0:T(128)S(1)} %copy-done.3, f32[4,2,128,128]{3,2,1,0:T(8,128)S(1)} %copy-done.1, ...), custom_call_target="tpu_custom_call", output_to_operand_aliasing={{0}: (12, {})} | custom-call | tf_op jit(solution)/shard_map/pallas_call | solution.py:531
  28.5 8.0 %shard_map.99 = (f32[4,6,640,128]{3,2,1,0:T(8,128)S(1)}, bf16[20,64,128]{2,1,0:T(8,128)(2,1)S(1)}, bf16[20,64,128]{2,1,0:T(8,128)(2,1)S(1)}, f32[4,128,128]{2,1,0:T(8,128)S(1)}, f32[4,128,128]{2,1,0:T(8,128)S(1)}) custom-call(bf16[8,128,128]{2,1,0:T(8,128)(2,1)S(1)} %get-tuple-element.31.r_1_.r_0_, ...), custom_call_target="tpu_custom_call", output_to_operand_aliasing={{0}: (13, {})} | custom-call | tf_op jit(solution)/shard_map/pallas_call | solution.py:531
  37.2 0.8 collective-permute-start.9
  38.0 2.0 %collective-permute-start.12 = (f32[4,128,128]{2,1,0:T(8,128)S(1)}, f32[4,128,128]{2,1,0:T(8,128)S(1)}, u32[]{:S(2)}, u32[]{:S(2)}) collective-permute-start(f32[4,128,128]{2,1,0:T(8,128)S(1)} %get-tuple-element.55), channel_id=1, source_target_pairs={{0,1},{1,0},{2,3},{3,2},{4,5},{5,4},{6,7},{7,6},{8,9},{9,8},{10,11... | collective-permute-start | bytes 786440 | tf_op jit(solution)/shard_map/ppermute | solution.py:551
  40.0 5.7 %collective-permute-done.8.r_1_ = bf16[20,64,128]{2,1,0:T(8,128)(2,1)S(1)} collective-permute-done((bf16[20,64,128]{2,1,0:T(8,128)(2,1)S(1)}, bf16[20,64,128]{2,1,0:T(8,128)(2,1)S(1)}, u32[]{:S(2)}, u32[]{:S(2)}) %collective-permute-start.8) | collective-permute-done | bytes 327712 | tf_op jit(solution)/shard_map/ppermute | solution.py:551
  46.2 1.3 %collective-permute-start.10 = (bf16[2,512,128]{2,1,0:T(8,128)(2,1)S(1)}, bf16[2,512,128]{2,1,0:T(8,128)(2,1)S(1)}, u32[]{:S(2)}, u32[]{:S(2)}) collective-permute-start(bf16[2,512,128]{2,1,0:T(8,128)(2,1)S(1)} %get-tuple-element.52), channel_id=1, source_target_pairs={{0,1},{1,0},{2,3},{3,2},{4,5},{5,4},{6,7},{7,6},{8,9},{9,8},{10,11... | collective-permute-start | bytes 786440 | tf_op jit(solution)/shard_map/ppermute | solution.py:551
  47.5 0.7 collective-permute-start.11
  48.2 4.4 %collective-permute-start.13 = (bf16[128,128]{1,0:T(8,128)(2,1)S(1)}, bf16[128,128]{1,0:T(8,128)(2,1)S(1)}, u32[]{:S(2)}, u32[]{:S(2)}) collective-permute-start(bf16[128,128]{1,0:T(8,128)(2,1)S(1)} %get-tuple-element.57), channel_id=1, source_target_pairs={{0,2},{1,3},{2,0},{3,1},{4,6},{5,7},{6,4},{7,5},{8,10},{9,11},{10,... | collective-permute-start | bytes 98312 | tf_op jit(solution)/shard_map/ppermute | solution.py:551
  52.6 2.1 %collective-permute-start.14 = (bf16[128,128]{1,0:T(8,128)(2,1)S(1)}, bf16[128,128]{1,0:T(8,128)(2,1)S(1)}, u32[]{:S(2)}, u32[]{:S(2)}) collective-permute-start(bf16[128,128]{1,0:T(8,128)(2,1)S(1)} %get-tuple-element.58), channel_id=1, source_target_pairs={{0,4},{1,5},{2,6},{3,7},{4,0},{5,1},{6,2},{7,3},{8,12},{9,13},{10,... | collective-permute-start | bytes 98312 | tf_op jit(solution)/shard_map/ppermute | solution.py:551
  54.7 0.9 %collective-permute-start.15 = (bf16[128,128]{1,0:T(8,128)(2,1)S(1)}, bf16[128,128]{1,0:T(8,128)(2,1)S(1)}, u32[]{:S(2)}, u32[]{:S(2)}) collective-permute-start(bf16[128,128]{1,0:T(8,128)(2,1)S(1)} %get-tuple-element.59), channel_id=1, source_target_pairs={{0,6},{1,7},{2,4},{3,5},{4,2},{5,3},{6,0},{7,1},{8,14},{9,15},{10,... | collective-permute-start | bytes 98312 | tf_op jit(solution)/shard_map/ppermute | solution.py:551
  55.6 3.9 %collective-permute-done.13.refs_0_ = bf16[128,128]{1,0:T(8,128)(2,1)S(1)} collective-permute-done((bf16[128,128]{1,0:T(8,128)(2,1)S(1)}, bf16[128,128]{1,0:T(8,128)(2,1)S(1)}, u32[]{:S(2)}, u32[]{:S(2)}) %collective-permute-start.13) | collective-permute-done | bytes 32800 | tf_op jit(solution)/shard_map/ppermute | solution.py:551
  59.5 5.8 %collective-permute-start.18 = (bf16[128,128]{1,0:T(8,128)(2,1)S(1)}, bf16[128,128]{1,0:T(8,128)(2,1)S(1)}, u32[]{:S(2)}, u32[]{:S(2)}) collective-permute-start(bf16[128,128]{1,0:T(8,128)(2,1)S(1)} %shard_map.104.r_0_), channel_id=1, source_target_pairs={{0,16},{8,24},{16,0},{24,8},{1,17},{9,25},{17,1},{25,9},{2,18},{10... | collective-permute-start | bytes 98312 | tf_op jit(solution)/shard_map/ppermute | solution.py:551
  65.3 1.2 %collective-permute-start.17 = (bf16[128,128]{1,0:T(8,128)(2,1)S(1)}, bf16[128,128]{1,0:T(8,128)(2,1)S(1)}, u32[]{:S(2)}, u32[]{:S(2)}) collective-permute-start(bf16[128,128]{1,0:T(8,128)(2,1)S(1)} %shard_map.104.r_0_), channel_id=1, source_target_pairs={{0,24},{8,16},{16,8},{24,0},{1,25},{9,17},{17,9},{25,1},{2,26},{10... | collective-permute-start | bytes 98312 | tf_op jit(solution)/shard_map/ppermute | solution.py:551
  66.5 0.9 %collective-permute-done.18.r_3_ = bf16[128,128]{1,0:T(8,128)(2,1)S(1)} collective-permute-done((bf16[128,128]{1,0:T(8,128)(2,1)S(1)}, bf16[128,128]{1,0:T(8,128)(2,1)S(1)}, u32[]{:S(2)}, u32[]{:S(2)}) %collective-permute-start.18) | collective-permute-done | bytes 32800 | tf_op jit(solution)/shard_map/ppermute | solution.py:551
  67.4 4.0 %collective-permute-done.17.r_2_ = bf16[128,128]{1,0:T(8,128)(2,1)S(1)} collective-permute-done((bf16[128,128]{1,0:T(8,128)(2,1)S(1)}, bf16[128,128]{1,0:T(8,128)(2,1)S(1)}, u32[]{:S(2)}, u32[]{:S(2)}) %collective-permute-start.17) | collective-permute-done | bytes 32800 | tf_op jit(solution)/shard_map/ppermute | solution.py:551
  71.4 1.9 %collective-permute-start.21 = (bf16[128,128]{1,0:T(8,128)(2,1)S(1)}, bf16[128,128]{1,0:T(8,128)(2,1)S(1)}, u32[]{:S(2)}, u32[]{:S(2)}) collective-permute-start(bf16[128,128]{1,0:T(8,128)(2,1)S(1)} %shard_map.105.refs_0_), channel_id=1, source_target_pairs={{0,6},{1,7},{2,4},{3,5},{4,2},{5,3},{6,0},{7,1},{8,14},{9,15},{10,... | collective-permute-start | bytes 98312 | tf_op jit(solution)/shard_map/ppermute | solution.py:551
  73.3 1.8 %collective-permute-start.20 = (bf16[128,128]{1,0:T(8,128)(2,1)S(1)}, bf16[128,128]{1,0:T(8,128)(2,1)S(1)}, u32[]{:S(2)}, u32[]{:S(2)}) collective-permute-start(bf16[128,128]{1,0:T(8,128)(2,1)S(1)} %shard_map.105.refs_0_), channel_id=1, source_target_pairs={{0,4},{1,5},{2,6},{3,7},{4,0},{5,1},{6,2},{7,3},{8,12},{9,13},{10,... | collective-permute-start | bytes 98312 | tf_op jit(solution)/shard_map/ppermute | solution.py:551
  75.1 1.2 %collective-permute-done.21.refs_3_ = bf16[128,128]{1,0:T(8,128)(2,1)S(1)} collective-permute-done((bf16[128,128]{1,0:T(8,128)(2,1)S(1)}, bf16[128,128]{1,0:T(8,128)(2,1)S(1)}, u32[]{:S(2)}, u32[]{:S(2)}) %collective-permute-start.21) | collective-permute-done | bytes 32800 | tf_op jit(solution)/shard_map/ppermute | solution.py:551
  76.4 0.9 %collective-permute-done.20.refs_2_ = bf16[128,128]{1,0:T(8,128)(2,1)S(1)} collective-permute-done((bf16[128,128]{1,0:T(8,128)(2,1)S(1)}, bf16[128,128]{1,0:T(8,128)(2,1)S(1)}, u32[]{:S(2)}, u32[]{:S(2)}) %collective-permute-start.20) | collective-permute-done | bytes 32800 | tf_op jit(solution)/shard_map/ppermute | solution.py:551
  77.2 1.8 %collective-permute-done.19.refs_1_ = bf16[128,128]{1,0:T(8,128)(2,1)S(1)} collective-permute-done((bf16[128,128]{1,0:T(8,128)(2,1)S(1)}, bf16[128,128]{1,0:T(8,128)(2,1)S(1)}, u32[]{:S(2)}, u32[]{:S(2)}) %collective-permute-start.19) | collective-permute-done | bytes 32800 | tf_op jit(solution)/shard_map/ppermute | solution.py:551
  79.1 1.7 %shard_map.101.old = f32[2,2,512,512]{3,2,1,0:T(8,128)} custom-call(f32[2,2,512,512]{3,2,1,0:T(8,128)S(1)} %copy-done, f32[4,6,640,128]{3,2,1,0:T(8,128)S(1)} %get-tuple-element.51.grad, f32[4,2,128,128]{3,2,1,0:T(8,128)S(1)} %copy-done.1), custom_call_target="tpu_custom_call" | custom-call | tf_op jit(solution)/shard_map/pallas_call | solution.py:531
  80.9 1.1 %shard_map.107 = f32[4,2,128,128]{3,2,1,0:T(8,128)} custom-call(f32[4,2,128,128]{3,2,1,0:T(8,128)S(1)} %copy-done.1, bf16[4,128,128]{2,1,0:T(8,128)(2,1)S(1)} %shard_map.106.joined, bf16[4,128,128]{2,1,0:T(8,128)(2,1)S(1)} %collective-permute-done.22.other), custom_call_target="tpu_custom_call" | custom-call | tf_op jit(solution)/shard_map/pallas_call | solution.py:531
  82.0 2.0 %shard_map.102 = f32[2,2,512,512]{3,2,1,0:T(8,128)} custom-call(f32[2,2,512,512]{3,2,1,0:T(8,128)S(1)} %copy-done, f32[4,6,640,128]{3,2,1,0:T(8,128)S(1)} %get-tuple-element.51.grad, bf16[2,512,128]{2,1,0:T(8,128)(2,1)S(1)} %collective-permute-done.10.tx_a, bf16[2,512,128]{2,1,0:T(8,128)(2,1)S(1)} %collective-permute-done.11.tx_b, ...), custom_call_target="tpu_custom_call", output_to_operand_aliasing={{}: (5, {})} | custom-call | tf_op jit(solution)/shard_map/pallas_call | solution.py:531
  (35 shorter events, 1.6 us)
Async XLA Ops:
  0.6 22.0 %copy-start.3 = (s32[32]{0:T(128)S(1)}, s32[32]{0:T(128)}, u32[]{:S(2)}) copy-start(s32[32]{0:T(128)} %r_2_.3) | copy-start | bytes 388
  0.6 22.0 %copy-start.2 = (s32[256,2]{0,1:T(2,128)S(1)}, s32[256,2]{0,1:T(2,128)}, u32[]{:S(2)}) copy-start(s32[256,2]{0,1:T(2,128)} %param.11) | copy-start | bytes 6148
  0.7 22.0 %copy-start.1 = (f32[4,2,128,128]{3,2,1,0:T(8,128)S(1)}, f32[4,2,128,128]{3,2,1,0:T(8,128)}, u32[]{:S(2)}) copy-start(f32[4,2,128,128]{3,2,1,0:T(8,128)} %probe.5) | copy-start | bytes 1572868
  2.9 10.8 %collective-permute-start = (bf16[20,64,128]{2,1,0:T(8,128)(2,1)S(1)}, bf16[20,64,128]{2,1,0:T(8,128)(2,1)S(1)}, u32[]{:S(2)}, u32[]{:S(2)}) collective-permute-start(bf16[20,64,128]{2,1,0:T(8,128)(2,1)S(1)} %get-tuple-element.35), channel_id=1, source_target_pairs={{0,8},{8,0},{16,24},{24,16},{1,9},{9,1},{17,25},{25,17},{2,10},{10... | collective-permute-start | bytes 983048 | tf_op jit(solution)/shard_map/ppermute | solution.py:551
  6.0 1.4 %collective-permute-start.1 = (bf16[16,64,128]{2,1,0:T(8,128)(2,1)S(1)}, bf16[16,64,128]{2,1,0:T(8,128)(2,1)S(1)}, u32[]{:S(2)}, u32[]{:S(2)}) collective-permute-start(bf16[16,64,128]{2,1,0:T(8,128)(2,1)S(1)} %get-tuple-element.36), channel_id=1, source_target_pairs={{8,16},{16,8},{9,17},{17,9},{10,18},{18,10},{11,19},{19,11},{12,20... | collective-permute-start | bytes 786440 | tf_op jit(solution)/shard_map/ppermute | solution.py:551
  6.7 14.9 %collective-permute-start.2 = (bf16[2,512,128]{2,1,0:T(8,128)(2,1)S(1)}, bf16[2,512,128]{2,1,0:T(8,128)(2,1)S(1)}, u32[]{:S(2)}, u32[]{:S(2)}) collective-permute-start(bf16[2,512,128]{2,1,0:T(8,128)(2,1)S(1)} %get-tuple-element.37), channel_id=1, source_target_pairs={{0,1},{1,0},{2,3},{3,2},{4,5},{5,4},{6,7},{7,6},{8,9},{9,8},{10,11... | collective-permute-start | bytes 786440 | tf_op jit(solution)/shard_map/ppermute | solution.py:551
  6.8 15.9 %collective-permute-start.3 = (bf16[2,512,128]{2,1,0:T(8,128)(2,1)S(1)}, bf16[2,512,128]{2,1,0:T(8,128)(2,1)S(1)}, u32[]{:S(2)}, u32[]{:S(2)}) collective-permute-start(bf16[2,512,128]{2,1,0:T(8,128)(2,1)S(1)} %get-tuple-element.38), channel_id=1, source_target_pairs={{1,2},{2,1},{3,4},{4,3},{5,6},{6,5},{9,10},{10,9},{11,12},{12,11},... | collective-permute-start | bytes 786440 | tf_op jit(solution)/shard_map/ppermute | solution.py:551
  13.8 8.8 %collective-permute-start.4 = (bf16[4,64,128]{2,1,0:T(8,128)(2,1)S(1)}, bf16[4,64,128]{2,1,0:T(8,128)(2,1)S(1)}, u32[]{:S(2)}, u32[]{:S(2)}) collective-permute-start(bf16[4,64,128]{2,1,0:T(8,128)(2,1)S(1)} %get-tuple-element.39), channel_id=1, source_target_pairs={{0,1},{1,0},{2,3},{3,2},{4,5},{5,4},{6,7},{7,6},{8,9},{9,8},{10,11... | collective-permute-start | bytes 196616 | tf_op jit(solution)/shard_map/ppermute | solution.py:551
  13.9 8.8 %collective-permute-start.5 = (bf16[4,64,128]{2,1,0:T(8,128)(2,1)S(1)}, bf16[4,64,128]{2,1,0:T(8,128)(2,1)S(1)}, u32[]{:S(2)}, u32[]{:S(2)}) collective-permute-start(bf16[4,64,128]{2,1,0:T(8,128)(2,1)S(1)} %get-tuple-element.40), channel_id=1, source_target_pairs={{1,2},{2,1},{3,4},{4,3},{5,6},{6,5},{9,10},{10,9},{11,12},{12,11},... | collective-permute-start | bytes 196616 | tf_op jit(solution)/shard_map/ppermute | solution.py:551
  17.8 10.7 %collective-permute-start.6 = (bf16[2,128,128]{2,1,0:T(8,128)(2,1)S(1)}, bf16[2,128,128]{2,1,0:T(8,128)(2,1)S(1)}, u32[]{:S(2)}, u32[]{:S(2)}) collective-permute-start(bf16[2,128,128]{2,1,0:T(8,128)(2,1)S(1)} %get-tuple-element.45), channel_id=1, source_target_pairs={{0,24},{8,16},{16,8},{24,0},{1,25},{9,17},{17,9},{25,1},{2,26},{10... | collective-permute-start | bytes 196616 | tf_op jit(solution)/shard_map/ppermute | solution.py:551
  21.6 6.9 %collective-permute-start.7 = (bf16[2,128,128]{2,1,0:T(8,128)(2,1)S(1)}, bf16[2,128,128]{2,1,0:T(8,128)(2,1)S(1)}, u32[]{:S(2)}, u32[]{:S(2)}) collective-permute-start(bf16[2,128,128]{2,1,0:T(8,128)(2,1)S(1)} %get-tuple-element.46), channel_id=1, source_target_pairs={{0,16},{8,24},{16,0},{24,8},{1,17},{9,25},{17,1},{25,9},{2,18},{10... | collective-permute-start | bytes 196616 | tf_op jit(solution)/shard_map/ppermute | solution.py:551
  36.5 42.6 %copy-start = (f32[2,2,512,512]{3,2,1,0:T(8,128)S(1)}, f32[2,2,512,512]{3,2,1,0:T(8,128)}, u32[]{:S(2)}) copy-start(f32[2,2,512,512]{3,2,1,0:T(8,128)} %obj.3) | copy-start | bytes 12582916
  36.5 9.2 %collective-permute-start.8 = (bf16[20,64,128]{2,1,0:T(8,128)(2,1)S(1)}, bf16[20,64,128]{2,1,0:T(8,128)(2,1)S(1)}, u32[]{:S(2)}, u32[]{:S(2)}) collective-permute-start(bf16[20,64,128]{2,1,0:T(8,128)(2,1)S(1)} %get-tuple-element.49), channel_id=1, source_target_pairs={{0,8},{8,0},{16,24},{24,16},{1,9},{9,1},{17,25},{25,17},{2,10},{10... | collective-permute-start | bytes 983048 | tf_op jit(solution)/shard_map/ppermute | solution.py:551
  37.2 8.6 %collective-permute-start.9 = (bf16[20,64,128]{2,1,0:T(8,128)(2,1)S(1)}, bf16[20,64,128]{2,1,0:T(8,128)(2,1)S(1)}, u32[]{:S(2)}, u32[]{:S(2)}) collective-permute-start(bf16[20,64,128]{2,1,0:T(8,128)(2,1)S(1)} %get-tuple-element.50), channel_id=1, source_target_pairs={{8,16},{16,8},{9,17},{17,9},{10,18},{18,10},{11,19},{19,11},{12,20... | collective-permute-start | bytes 983048 | tf_op jit(solution)/shard_map/ppermute | solution.py:551
  38.0 10.2 %collective-permute-start.12 = (f32[4,128,128]{2,1,0:T(8,128)S(1)}, f32[4,128,128]{2,1,0:T(8,128)S(1)}, u32[]{:S(2)}, u32[]{:S(2)}) collective-permute-start(f32[4,128,128]{2,1,0:T(8,128)S(1)} %get-tuple-element.55), channel_id=1, source_target_pairs={{0,1},{1,0},{2,3},{3,2},{4,5},{5,4},{6,7},{7,6},{8,9},{9,8},{10,11... | collective-permute-start | bytes 786440 | tf_op jit(solution)/shard_map/ppermute | solution.py:551
  46.2 35.8 %collective-permute-start.10 = (bf16[2,512,128]{2,1,0:T(8,128)(2,1)S(1)}, bf16[2,512,128]{2,1,0:T(8,128)(2,1)S(1)}, u32[]{:S(2)}, u32[]{:S(2)}) collective-permute-start(bf16[2,512,128]{2,1,0:T(8,128)(2,1)S(1)} %get-tuple-element.52), channel_id=1, source_target_pairs={{0,1},{1,0},{2,3},{3,2},{4,5},{5,4},{6,7},{7,6},{8,9},{9,8},{10,11... | collective-permute-start | bytes 786440 | tf_op jit(solution)/shard_map/ppermute | solution.py:551
  47.5 34.5 %collective-permute-start.11 = (bf16[2,512,128]{2,1,0:T(8,128)(2,1)S(1)}, bf16[2,512,128]{2,1,0:T(8,128)(2,1)S(1)}, u32[]{:S(2)}, u32[]{:S(2)}) collective-permute-start(bf16[2,512,128]{2,1,0:T(8,128)(2,1)S(1)} %get-tuple-element.53), channel_id=1, source_target_pairs={{1,2},{2,1},{3,4},{4,3},{5,6},{6,5},{9,10},{10,9},{11,12},{12,11},... | collective-permute-start | bytes 786440 | tf_op jit(solution)/shard_map/ppermute | solution.py:551
  48.2 11.2 %collective-permute-start.13 = (bf16[128,128]{1,0:T(8,128)(2,1)S(1)}, bf16[128,128]{1,0:T(8,128)(2,1)S(1)}, u32[]{:S(2)}, u32[]{:S(2)}) collective-permute-start(bf16[128,128]{1,0:T(8,128)(2,1)S(1)} %get-tuple-element.57), channel_id=1, source_target_pairs={{0,2},{1,3},{2,0},{3,1},{4,6},{5,7},{6,4},{7,5},{8,10},{9,11},{10,... | collective-permute-start | bytes 98312 | tf_op jit(solution)/shard_map/ppermute | solution.py:551
  52.6 6.9 %collective-permute-start.14 = (bf16[128,128]{1,0:T(8,128)(2,1)S(1)}, bf16[128,128]{1,0:T(8,128)(2,1)S(1)}, u32[]{:S(2)}, u32[]{:S(2)}) collective-permute-start(bf16[128,128]{1,0:T(8,128)(2,1)S(1)} %get-tuple-element.58), channel_id=1, source_target_pairs={{0,4},{1,5},{2,6},{3,7},{4,0},{5,1},{6,2},{7,3},{8,12},{9,13},{10,... | collective-permute-start | bytes 98312 | tf_op jit(solution)/shard_map/ppermute | solution.py:551
  54.7 4.8 %collective-permute-start.15 = (bf16[128,128]{1,0:T(8,128)(2,1)S(1)}, bf16[128,128]{1,0:T(8,128)(2,1)S(1)}, u32[]{:S(2)}, u32[]{:S(2)}) collective-permute-start(bf16[128,128]{1,0:T(8,128)(2,1)S(1)} %get-tuple-element.59), channel_id=1, source_target_pairs={{0,6},{1,7},{2,4},{3,5},{4,2},{5,3},{6,0},{7,1},{8,14},{9,15},{10,... | collective-permute-start | bytes 98312 | tf_op jit(solution)/shard_map/ppermute | solution.py:551
  59.5 7.9 %collective-permute-start.18 = (bf16[128,128]{1,0:T(8,128)(2,1)S(1)}, bf16[128,128]{1,0:T(8,128)(2,1)S(1)}, u32[]{:S(2)}, u32[]{:S(2)}) collective-permute-start(bf16[128,128]{1,0:T(8,128)(2,1)S(1)} %shard_map.104.r_0_), channel_id=1, source_target_pairs={{0,16},{8,24},{16,0},{24,8},{1,17},{9,25},{17,1},{25,9},{2,18},{10... | collective-permute-start | bytes 98312 | tf_op jit(solution)/shard_map/ppermute | solution.py:551
  65.3 6.0 %collective-permute-start.17 = (bf16[128,128]{1,0:T(8,128)(2,1)S(1)}, bf16[128,128]{1,0:T(8,128)(2,1)S(1)}, u32[]{:S(2)}, u32[]{:S(2)}) collective-permute-start(bf16[128,128]{1,0:T(8,128)(2,1)S(1)} %shard_map.104.r_0_), channel_id=1, source_target_pairs={{0,24},{8,16},{16,8},{24,0},{1,25},{9,17},{17,9},{25,1},{2,26},{10... | collective-permute-start | bytes 98312 | tf_op jit(solution)/shard_map/ppermute | solution.py:551
  66.5 4.9 %collective-permute-start.16 = (bf16[128,128]{1,0:T(8,128)(2,1)S(1)}, bf16[128,128]{1,0:T(8,128)(2,1)S(1)}, u32[]{:S(2)}, u32[]{:S(2)}) collective-permute-start(bf16[128,128]{1,0:T(8,128)(2,1)S(1)} %shard_map.104.r_0_), channel_id=1, source_target_pairs={{0,8},{8,0},{16,24},{24,16},{1,9},{9,1},{17,25},{25,17},{2,10},{10... | collective-permute-start | bytes 98312 | tf_op jit(solution)/shard_map/ppermute | solution.py:551
  71.4 4.9 %collective-permute-start.21 = (bf16[128,128]{1,0:T(8,128)(2,1)S(1)}, bf16[128,128]{1,0:T(8,128)(2,1)S(1)}, u32[]{:S(2)}, u32[]{:S(2)}) collective-permute-start(bf16[128,128]{1,0:T(8,128)(2,1)S(1)} %shard_map.105.refs_0_), channel_id=1, source_target_pairs={{0,6},{1,7},{2,4},{3,5},{4,2},{5,3},{6,0},{7,1},{8,14},{9,15},{10,... | collective-permute-start | bytes 98312 | tf_op jit(solution)/shard_map/ppermute | solution.py:551
  73.3 3.9 %collective-permute-start.20 = (bf16[128,128]{1,0:T(8,128)(2,1)S(1)}, bf16[128,128]{1,0:T(8,128)(2,1)S(1)}, u32[]{:S(2)}, u32[]{:S(2)}) collective-permute-start(bf16[128,128]{1,0:T(8,128)(2,1)S(1)} %shard_map.105.refs_0_), channel_id=1, source_target_pairs={{0,4},{1,5},{2,6},{3,7},{4,0},{5,1},{6,2},{7,3},{8,12},{9,13},{10,... | collective-permute-start | bytes 98312 | tf_op jit(solution)/shard_map/ppermute | solution.py:551
  75.1 3.9 %collective-permute-start.19 = (bf16[128,128]{1,0:T(8,128)(2,1)S(1)}, bf16[128,128]{1,0:T(8,128)(2,1)S(1)}, u32[]{:S(2)}, u32[]{:S(2)}) collective-permute-start(bf16[128,128]{1,0:T(8,128)(2,1)S(1)} %shard_map.105.refs_0_), channel_id=1, source_target_pairs={{0,2},{1,3},{2,0},{3,1},{4,6},{5,7},{6,4},{7,5},{8,10},{9,11},{10,... | collective-permute-start | bytes 98312 | tf_op jit(solution)/shard_map/ppermute | solution.py:551
  79.1 1.8 %collective-permute-start.22 = (bf16[4,128,128]{2,1,0:T(8,128)(2,1)S(1)}, bf16[4,128,128]{2,1,0:T(8,128)(2,1)S(1)}, u32[]{:S(2)}, u32[]{:S(2)}) collective-permute-start(bf16[4,128,128]{2,1,0:T(8,128)(2,1)S(1)} %shard_map.106.joined), channel_id=1, source_target_pairs={{0,1},{1,0},{2,3},{3,2},{4,5},{5,4},{6,7},{7,6},{8,9},{9,8},{10,11... | collective-permute-start | bytes 393224 | tf_op jit(solution)/shard_map/ppermute | solution.py:551

commit v4 on v3

--- a/solution.py
+++ b/solution.py
@@ -114,7 +114,8 @@
     return found, ys, xs, lives
 
 
-def pack_kernel(sizes, obj, pat, pos_in, cnt_in, ty_a, ty_b, tx_a, tx_b, held, rows, columns, pos, cnt, sems):
+def pack_kernel(sizes, obj, pat, pos_in, cnt_in, ty_a, ty_b, tx_a, tx_b, held, ext, grad, *refs):
+    routed, (rows, pos, cnt, sems) = refs[:-4], refs[-4:]
     slices, tile, margin = obj.shape[0], obj.shape[2], rows.shape[3]
     planes, tiles = slices * 2, obj.shape[3] // LANES
     row, col = lax.axis_index("ty"), lax.axis_index("tx")
@@ -127,9 +128,16 @@
     for k in range(2):
         start = pl.multiple_of(up_y[k] * (tile - margin), margin)
         copies.append(pltpu.make_async_copy(obj.at[:, :, pl.ds(start, margin), :], rows.at[k], sems.at[3 + k]))
-    for j in range(2):
-        lane = pl.multiple_of(up_x[j] * (tile - LANES), LANES)
-        copies.append(pltpu.make_async_copy(obj.at[:, :, :, pl.ds(lane, LANES)], columns.at[j], sems.at[5 + j]))
+    outer = sorted({0, tiles - 1})
+    inner = slice(margin, margin + tile)
+    for p in range(planes):
+        for i, t in enumerate(outer):
+            lanes = slice(t * LANES, (t + 1) * LANES)
+            copies.append(
+                pltpu.make_async_copy(
+                    obj.at[p // 2, p % 2, :, lanes], ext.at[p, 1 + t, inner, :], sems.at[5 + 2 * p + i]
+                )
+            )
     for copy in copies:
         copy.start()
     for copy in copies[:3]:
@@ -145,24 +153,30 @@
             for t in range(tiles):
                 block = rows[k, p // 2, p % 2, :, t * LANES : (t + 1) * LANES]
                 out[p * tiles + t] = block.astype(BF16)
+    grad[...] = jnp.zeros(grad.shape, F32)
+    for k, out in enumerate(routed, 1):
+        target = pick(row, sizes[2][k]) * tile
+        found = slot_scan(pos, cnt, sizes, row, col, pat.shape[0], target, tile)[0]
+        for c in range(CAP):
+            out[c] = held[found[c]]
+    for copy in copies[5:]:
+        copy.wait()
     for j, out in enumerate((tx_a, tx_b)):
-        copies[5 + j].wait()
+        side = 1 + up_x[j] * (tiles - 1)
         for s in range(slices):
-            re, im = columns[j, s, 0], columns[j, s, 1]
+            re, im = ext[2 * s, side, inner], ext[2 * s + 1, side, inner]
             packed = jnp.where(half_mask(tile, up_x[j]), re, pltpu.roll(im, LANES // 2, 1))
             out[s] = packed.astype(BF16)
 
 
-def tile_kernel(sizes, obj, pat, pos, cnt, *refs):
-    rounds = sizes[2]
-    sources, ext, grad = refs[:3], refs[3], refs[4]
-    routed, near_tables, sems = refs[5:-4], refs[-4:-1], refs[-1]
+def tile_kernel(obj, *refs):
+    sources, ext, near_tables, sems = refs[:3], refs[4], refs[5:-1], refs[-1]
     slices, tile = obj.shape[0], obj.shape[2]
     tiles = obj.shape[3] // LANES
     margin = (ext.shape[2] - tile) // 2
     copies = []
     for p in range(slices * 2):
-        for t in range(tiles):
+        for t in range(1, tiles - 1):
             copies.append(
                 pltpu.make_async_copy(
                     obj.at[p // 2, p % 2, :, t * LANES : (t + 1) * LANES],
@@ -174,13 +188,6 @@
         copies.append(pltpu.make_async_copy(a, b, sems.at[slices * 2 * tiles + i]))
     for copy in copies:
         copy.start()
-    row, col = lax.axis_index("ty"), lax.axis_index("tx")
-    targets = [pick(row, partner) * tile for partner in rounds[1:]]
-    found = [slot_scan(pos, cnt, sizes, row, col, pat.shape[0], t, tile)[0] for t in targets]
-    for k, out in enumerate(routed):
-        for c in range(CAP):
-            out[c] = pat[found[k][c]]
-    grad[...] = jnp.zeros(grad.shape, F32)
     for copy in copies:
         copy.wait()
 
@@ -563,22 +570,24 @@
     places = positions.T
     planes = slices * 2
     block = (margin, LANES)
+    ext_shape = (planes, tiles + 2, tile + extent, LANES)
     strips = [pltpu.VMEM((slices, tile, LANES), BF16)] * 2
     strips = [pltpu.VMEM((slices, tile, LANES), BF16)] * 2
     rows_out = [pltpu.VMEM((parts + 2 * slices,) + block, BF16)] * 2
-    ty_a, ty_b, tx_a, tx_b, near_patterns = call(
+    ty_a, ty_b, tx_a, tx_b, near_patterns, ext, grad, *routed = call(
         lambda *r: pack_kernel(sizes, *r),
         (far(object_slices), far(patterns), far(places), far(counts)),
         [ANY] * 4,
         [pltpu.VMEM((parts + extra,) + block, BF16) for extra in (2 * CAP, 0)]
         + strips
-        + [pltpu.VMEM(patterns.shape, BF16)],
+        + [pltpu.VMEM(patterns.shape, BF16)]
+        + [pltpu.VMEM(ext_shape, F32)] * 2
+        + [pltpu.VMEM((CAP, extent, extent), BF16)] * (k_n - 1),
         [
             pltpu.VMEM((2, slices, 2, margin, tile), F32),
-            pltpu.VMEM((2, slices, 2, tile, LANES), F32),
             pltpu.SMEM(places.shape, jnp.int32),
             pltpu.SMEM(counts.shape, jnp.int32),
-            pltpu.SemaphoreType.DMA((7,)),
+            pltpu.SemaphoreType.DMA((5 + 2 * planes,)),
         ],
     )
     near_object, near_patterns = near(object_slices), near(near_patterns)
@@ -592,19 +601,16 @@
     def cross(value, k):
         return send(value, "tx", [(i, i ^ k) for i in range(n_tx)])
 
-    ext_shape = (planes, tiles + 2, tile + extent, LANES)
     ty_in = [swap(ty_a, "ty", 0), swap(ty_b, "ty", 1)]
     tx_in = [swap(tx_a, "tx", 0), swap(tx_b, "tx", 1)]
     tables = make_tables(extent)
-    ext, grad, *routed, first, second, kern = call(
-        lambda *r: tile_kernel(sizes, *r),
-        (far(object_slices), near_patterns, far(places), far(counts))
-        + tuple(far(c) for c in tables),
-        [ANY, VMEM, SMEM, SMEM] + [ANY] * 3,
-        [pltpu.VMEM(ext_shape, F32)] * 2
-        + [pltpu.VMEM((CAP, extent, extent), BF16)] * (k_n - 1)
-        + [pltpu.VMEM(c.shape, c.dtype) for c in tables],
+    ext, first, second, kern = call(
+        tile_kernel,
+        (far(object_slices),) + tuple(far(c) for c in tables) + (near(ext),),
+        [ANY] * 4 + [VMEM],
+        [pltpu.VMEM(ext_shape, F32)] + [pltpu.VMEM(c.shape, c.dtype) for c in tables],
         [pltpu.SemaphoreType.DMA((parts + 3,))],
+        {4: 0},
     )
     constants = tuple(near(c) for c in (first, second, kern))
     corners = call(

time: 84.3 us -> 82.5 us (0.979)
  Pallas kernels: 24.7 us -> 23.5 us
    pallas_call x13, Pallas kernels: 24.7 us -> 23.5 us  [call(): pl.pallas_call(kernel, out_shape=outs, in_specs=specs, out_specs=out_spec...]
  transfers between devices with their start and end apart: 23 -> 23, of which waited for: 8 -> 8; matrix products, arithmetic and copies ran while one was open for 0% -> 0% of each run, Pallas kernels for 15% -> 14%
where the time goes in v4:
time: 82.5 us; the launch traced here: 82.2 us
  starting transfers between devices  33.2 us (40%)
  waiting for transfers between devices  24.6 us (30%)
  Pallas kernels  23.5 us (28%)
  between operations  0.91 us (1%)
    ppermute x23, starting transfers between devices, send(): return near(lax.ppermute(value, axis, pairs))  33.2 us
    ppermute x23, waiting for transfers between devices, send(): return near(lax.ppermute(value, axis, pairs))  24.6 us
    pallas_call x13, Pallas kernels, call(): pl.pallas_call(kernel, out_shape=outs, in_specs=specs, out_specs=out_spec...  23.5 us
  transfers between devices with their start and end apart: 23, of which 8 were waited for; matrix products, arithmetic and copies ran while one was open for 0% of the time, Pallas kernels for 14%

profile of v4, /device:TPU:0, one launch (start us, length us, event | category | flops | bytes accessed | tf_op | source)
XLA Modules:
  0.0 82.2 jit_solution(12475360585215186915)
XLA Ops:
  0.7 2.3 %shard_map.95 = (bf16[20,64,128]{2,1,0:T(8,128)(2,1)S(1)}, bf16[16,64,128]{2,1,0:T(8,128)(2,1)S(1)}, bf16[2,512,128]{2,1,0:T(8,128)(2,1)S(1)}, bf16[2,512,128]{2...) custom-call(f32[2,2,512,512]{3,2,1,0:T(8,128)} %obj.5, ...), custom_call_target="tpu_custom_call" | custom-call | tf_op jit(solution)/shard_map/pallas_call | solution.py:538
  3.0 3.1 %collective-permute-start = (bf16[20,64,128]{2,1,0:T(8,128)(2,1)S(1)}, bf16[20,64,128]{2,1,0:T(8,128)(2,1)S(1)}, u32[]{:S(2)}, u32[]{:S(2)}) collective-permute-start(bf16[20,64,128]{2,1,0:T(8,128)(2,1)S(1)} %get-tuple-element.37), channel_id=1, source_target_pairs={{0,8},{8,0},{16,24},{24,16},{1,9},{9,1},{17,25},{25,17},{2,10},{10... | collective-permute-start | bytes 983048 | tf_op jit(solution)/shard_map/ppermute | solution.py:558
  6.1 0.7 collective-permute-start.1
  6.8 0.7 collective-permute-start.3
  7.5 6.3 %collective-permute-done.r_0_.r_6_.r_10_ = bf16[20,64,128]{2,1,0:T(8,128)(2,1)S(1)} collective-permute-done((bf16[20,64,128]{2,1,0:T(8,128)(2,1)S(1)}, bf16[20,64,128]{2,1,0:T(8,128)(2,1)S(1)}, u32[]{:S(2)}, u32[]{:S(2)}) %collective-permute-start) | collective-permute-done | bytes 327712 | tf_op jit(solution)/shard_map/ppermute | solution.py:558
  14.0 0.7 collective-permute-start.5
  14.7 3.8 %collective-permute-start.6 = (bf16[2,128,128]{2,1,0:T(8,128)(2,1)S(1)}, bf16[2,128,128]{2,1,0:T(8,128)(2,1)S(1)}, u32[]{:S(2)}, u32[]{:S(2)}) collective-permute-start(bf16[2,128,128]{2,1,0:T(8,128)(2,1)S(1)} %get-tuple-element.47), channel_id=1, source_target_pairs={{0,24},{8,16},{16,8},{24,0},{1,25},{9,17},{17,9},{25,1},{2,26},{10... | collective-permute-start | bytes 196616 | tf_op jit(solution)/shard_map/ppermute | solution.py:558
  18.5 1.1 %collective-permute-start.7 = (bf16[2,128,128]{2,1,0:T(8,128)(2,1)S(1)}, bf16[2,128,128]{2,1,0:T(8,128)(2,1)S(1)}, u32[]{:S(2)}, u32[]{:S(2)}) collective-permute-start(bf16[2,128,128]{2,1,0:T(8,128)(2,1)S(1)} %get-tuple-element.48), channel_id=1, source_target_pairs={{0,16},{8,24},{16,0},{24,8},{1,17},{9,25},{17,1},{25,9},{2,18},{10... | collective-permute-start | bytes 196616 | tf_op jit(solution)/shard_map/ppermute | solution.py:558
  19.6 1.8 %shard_map.96 = (f32[4,6,640,128]{3,2,1,0:T(8,128)S(1)}, bf16[256,256]{1,0:T(8,128)(2,1)S(1)}, bf16[256,256]{1,0:T(8,128)(2,1)S(1)}, f32[2,128,128]{2,1,0:T(8,128)S(1)}) custom-call(f32[2,2,512,512]{3,2,1,0:T(8,128)} %obj.5, bf16[256,256]{1,0:T(8,128)(2,1)} %constant.15.refs_0_, bf16[256,256]{1,0:T(8,128)(2,1)} %constant.18.refs_1_, ...), custom_call_target="tpu_custom_call", output_to_operand_aliasing={{0}: (4, {})} | custom-call | tf_op jit(solution)/shard_map/pallas_call | solution.py:538
  21.4 5.8 %shard_map.98 = (f32[4,6,640,128]{3,2,1,0:T(8,128)S(1)}, f32[8,8,128,128]{3,2,1,0:T(8,128)S(1)}, f32[1,8,8,128,128]{4,3,2,1,0:T(8,128)S(1)}) custom-call(s32[2,256]{1,0:T(2,128)S(1)} %bitcast.2, s32[32]{0:T(128)S(1)} %copy-done.3, f32[4,2,128,128]{3,2,1,0:T(8,128)S(1)} %copy-done.1, ...), custom_call_target="tpu_custom_call", output_to_operand_aliasing={{0}: (12, {})} | custom-call | tf_op jit(solution)/shard_map/pallas_call | solution.py:538
  27.3 8.0 %shard_map.99 = (f32[4,6,640,128]{3,2,1,0:T(8,128)S(1)}, bf16[20,64,128]{2,1,0:T(8,128)(2,1)S(1)}, bf16[20,64,128]{2,1,0:T(8,128)(2,1)S(1)}, f32[4,128,128]{2,1,0:T(8,128)S(1)}, f32[4,128,128]{2,1,0:T(8,128)S(1)}) custom-call(bf16[8,128,128]{2,1,0:T(8,128)(2,1)S(1)} %get-tuple-element.32.r_0_, ...), custom_call_target="tpu_custom_call", output_to_operand_aliasing={{0}: (13, {})} | custom-call | tf_op jit(solution)/shard_map/pallas_call | solution.py:538
  35.6 0.8 collective-permute-start.9
  36.5 2.4 %collective-permute-start.12 = (f32[4,128,128]{2,1,0:T(8,128)S(1)}, f32[4,128,128]{2,1,0:T(8,128)S(1)}, u32[]{:S(2)}, u32[]{:S(2)}) collective-permute-start(f32[4,128,128]{2,1,0:T(8,128)S(1)} %get-tuple-element.57), channel_id=1, source_target_pairs={{0,1},{1,0},{2,3},{3,2},{4,5},{5,4},{6,7},{7,6},{8,9},{9,8},{10,11... | collective-permute-start | bytes 786440 | tf_op jit(solution)/shard_map/ppermute | solution.py:558
  38.8 5.8 %collective-permute-done.8.r_1_ = bf16[20,64,128]{2,1,0:T(8,128)(2,1)S(1)} collective-permute-done((bf16[20,64,128]{2,1,0:T(8,128)(2,1)S(1)}, bf16[20,64,128]{2,1,0:T(8,128)(2,1)S(1)}, u32[]{:S(2)}, u32[]{:S(2)}) %collective-permute-start.8) | collective-permute-done | bytes 327712 | tf_op jit(solution)/shard_map/ppermute | solution.py:558
  45.0 1.3 %collective-permute-start.10 = (bf16[2,512,128]{2,1,0:T(8,128)(2,1)S(1)}, bf16[2,512,128]{2,1,0:T(8,128)(2,1)S(1)}, u32[]{:S(2)}, u32[]{:S(2)}) collective-permute-start(bf16[2,512,128]{2,1,0:T(8,128)(2,1)S(1)} %get-tuple-element.54), channel_id=1, source_target_pairs={{0,1},{1,0},{2,3},{3,2},{4,5},{5,4},{6,7},{7,6},{8,9},{9,8},{10,11... | collective-permute-start | bytes 786440 | tf_op jit(solution)/shard_map/ppermute | solution.py:558
  46.3 0.7 collective-permute-start.11
  47.0 4.4 %collective-permute-start.13 = (bf16[128,128]{1,0:T(8,128)(2,1)S(1)}, bf16[128,128]{1,0:T(8,128)(2,1)S(1)}, u32[]{:S(2)}, u32[]{:S(2)}) collective-permute-start(bf16[128,128]{1,0:T(8,128)(2,1)S(1)} %get-tuple-element.59), channel_id=1, source_target_pairs={{0,2},{1,3},{2,0},{3,1},{4,6},{5,7},{6,4},{7,5},{8,10},{9,11},{10,... | collective-permute-start | bytes 98312 | tf_op jit(solution)/shard_map/ppermute | solution.py:558
  51.4 2.1 %collective-permute-start.14 = (bf16[128,128]{1,0:T(8,128)(2,1)S(1)}, bf16[128,128]{1,0:T(8,128)(2,1)S(1)}, u32[]{:S(2)}, u32[]{:S(2)}) collective-permute-start(bf16[128,128]{1,0:T(8,128)(2,1)S(1)} %get-tuple-element.60), channel_id=1, source_target_pairs={{0,4},{1,5},{2,6},{3,7},{4,0},{5,1},{6,2},{7,3},{8,12},{9,13},{10,... | collective-permute-start | bytes 98312 | tf_op jit(solution)/shard_map/ppermute | solution.py:558
  53.5 0.9 %collective-permute-start.15 = (bf16[128,128]{1,0:T(8,128)(2,1)S(1)}, bf16[128,128]{1,0:T(8,128)(2,1)S(1)}, u32[]{:S(2)}, u32[]{:S(2)}) collective-permute-start(bf16[128,128]{1,0:T(8,128)(2,1)S(1)} %get-tuple-element.61), channel_id=1, source_target_pairs={{0,6},{1,7},{2,4},{3,5},{4,2},{5,3},{6,0},{7,1},{8,14},{9,15},{10,... | collective-permute-start | bytes 98312 | tf_op jit(solution)/shard_map/ppermute | solution.py:558
  54.4 3.9 %collective-permute-done.13.refs_0_ = bf16[128,128]{1,0:T(8,128)(2,1)S(1)} collective-permute-done((bf16[128,128]{1,0:T(8,128)(2,1)S(1)}, bf16[128,128]{1,0:T(8,128)(2,1)S(1)}, u32[]{:S(2)}, u32[]{:S(2)}) %collective-permute-start.13) | collective-permute-done | bytes 32800 | tf_op jit(solution)/shard_map/ppermute | solution.py:558
  58.3 4.9 %collective-permute-start.18 = (bf16[128,128]{1,0:T(8,128)(2,1)S(1)}, bf16[128,128]{1,0:T(8,128)(2,1)S(1)}, u32[]{:S(2)}, u32[]{:S(2)}) collective-permute-start(bf16[128,128]{1,0:T(8,128)(2,1)S(1)} %shard_map.104.r_0_), channel_id=1, source_target_pairs={{0,16},{8,24},{16,0},{24,8},{1,17},{9,25},{17,1},{25,9},{2,18},{10... | collective-permute-start | bytes 98312 | tf_op jit(solution)/shard_map/ppermute | solution.py:558
  63.3 1.3 %collective-permute-start.17 = (bf16[128,128]{1,0:T(8,128)(2,1)S(1)}, bf16[128,128]{1,0:T(8,128)(2,1)S(1)}, u32[]{:S(2)}, u32[]{:S(2)}) collective-permute-start(bf16[128,128]{1,0:T(8,128)(2,1)S(1)} %shard_map.104.r_0_), channel_id=1, source_target_pairs={{0,24},{8,16},{16,8},{24,0},{1,25},{9,17},{17,9},{25,1},{2,26},{10... | collective-permute-start | bytes 98312 | tf_op jit(solution)/shard_map/ppermute | solution.py:558
  64.5 0.7 collective-permute-done.18.r_3_
  65.3 4.1 %collective-permute-done.17.r_2_ = bf16[128,128]{1,0:T(8,128)(2,1)S(1)} collective-permute-done((bf16[128,128]{1,0:T(8,128)(2,1)S(1)}, bf16[128,128]{1,0:T(8,128)(2,1)S(1)}, u32[]{:S(2)}, u32[]{:S(2)}) %collective-permute-start.17) | collective-permute-done | bytes 32800 | tf_op jit(solution)/shard_map/ppermute | solution.py:558
  69.4 2.1 %collective-permute-start.21 = (bf16[128,128]{1,0:T(8,128)(2,1)S(1)}, bf16[128,128]{1,0:T(8,128)(2,1)S(1)}, u32[]{:S(2)}, u32[]{:S(2)}) collective-permute-start(bf16[128,128]{1,0:T(8,128)(2,1)S(1)} %shard_map.105.refs_0_), channel_id=1, source_target_pairs={{0,6},{1,7},{2,4},{3,5},{4,2},{5,3},{6,0},{7,1},{8,14},{9,15},{10,... | collective-permute-start | bytes 98312 | tf_op jit(solution)/shard_map/ppermute | solution.py:558
  71.5 1.8 %collective-permute-start.20 = (bf16[128,128]{1,0:T(8,128)(2,1)S(1)}, bf16[128,128]{1,0:T(8,128)(2,1)S(1)}, u32[]{:S(2)}, u32[]{:S(2)}) collective-permute-start(bf16[128,128]{1,0:T(8,128)(2,1)S(1)} %shard_map.105.refs_0_), channel_id=1, source_target_pairs={{0,4},{1,5},{2,6},{3,7},{4,0},{5,1},{6,2},{7,3},{8,12},{9,13},{10,... | collective-permute-start | bytes 98312 | tf_op jit(solution)/shard_map/ppermute | solution.py:558
  73.3 1.0 %collective-permute-done.21.refs_3_ = bf16[128,128]{1,0:T(8,128)(2,1)S(1)} collective-permute-done((bf16[128,128]{1,0:T(8,128)(2,1)S(1)}, bf16[128,128]{1,0:T(8,128)(2,1)S(1)}, u32[]{:S(2)}, u32[]{:S(2)}) %collective-permute-start.21) | collective-permute-done | bytes 32800 | tf_op jit(solution)/shard_map/ppermute | solution.py:558
  74.4 1.1 %collective-permute-done.20.refs_2_ = bf16[128,128]{1,0:T(8,128)(2,1)S(1)} collective-permute-done((bf16[128,128]{1,0:T(8,128)(2,1)S(1)}, bf16[128,128]{1,0:T(8,128)(2,1)S(1)}, u32[]{:S(2)}, u32[]{:S(2)}) %collective-permute-start.20) | collective-permute-done | bytes 32800 | tf_op jit(solution)/shard_map/ppermute | solution.py:558
  75.4 1.8 %collective-permute-done.19.refs_1_ = bf16[128,128]{1,0:T(8,128)(2,1)S(1)} collective-permute-done((bf16[128,128]{1,0:T(8,128)(2,1)S(1)}, bf16[128,128]{1,0:T(8,128)(2,1)S(1)}, u32[]{:S(2)}, u32[]{:S(2)}) %collective-permute-start.19) | collective-permute-done | bytes 32800 | tf_op jit(solution)/shard_map/ppermute | solution.py:558
  77.3 1.7 %shard_map.101.old = f32[2,2,512,512]{3,2,1,0:T(8,128)} custom-call(f32[2,2,512,512]{3,2,1,0:T(8,128)S(1)} %copy-done, f32[4,6,640,128]{3,2,1,0:T(8,128)S(1)} %get-tuple-element.53.grad, f32[4,2,128,128]{3,2,1,0:T(8,128)S(1)} %copy-done.1), custom_call_target="tpu_custom_call" | custom-call | tf_op jit(solution)/shard_map/pallas_call | solution.py:538
  79.1 1.1 %shard_map.107 = f32[4,2,128,128]{3,2,1,0:T(8,128)} custom-call(f32[4,2,128,128]{3,2,1,0:T(8,128)S(1)} %copy-done.1, bf16[4,128,128]{2,1,0:T(8,128)(2,1)S(1)} %shard_map.106.joined, bf16[4,128,128]{2,1,0:T(8,128)(2,1)S(1)} %collective-permute-done.22.other), custom_call_target="tpu_custom_call" | custom-call | tf_op jit(solution)/shard_map/pallas_call | solution.py:538
  80.2 2.0 %shard_map.102 = f32[2,2,512,512]{3,2,1,0:T(8,128)} custom-call(f32[2,2,512,512]{3,2,1,0:T(8,128)S(1)} %copy-done, f32[4,6,640,128]{3,2,1,0:T(8,128)S(1)} %get-tuple-element.53.grad, bf16[2,512,128]{2,1,0:T(8,128)(2,1)S(1)} %collective-permute-done.10.tx_a, bf16[2,512,128]{2,1,0:T(8,128)(2,1)S(1)} %collective-permute-done.11.tx_b, ...), custom_call_target="tpu_custom_call", output_to_operand_aliasing={{}: (5, {})} | custom-call | tf_op jit(solution)/shard_map/pallas_call | solution.py:538
  (35 shorter events, 1.2 us)
Async XLA Ops:
  0.6 20.8 %copy-start.1 = (f32[4,2,128,128]{3,2,1,0:T(8,128)S(1)}, f32[4,2,128,128]{3,2,1,0:T(8,128)}, u32[]{:S(2)}) copy-start(f32[4,2,128,128]{3,2,1,0:T(8,128)} %probe.5) | copy-start | bytes 1572868
  0.6 20.8 %copy-start.2 = (s32[256,2]{0,1:T(2,128)S(1)}, s32[256,2]{0,1:T(2,128)}, u32[]{:S(2)}) copy-start(s32[256,2]{0,1:T(2,128)} %param.11) | copy-start | bytes 6148
  0.7 20.8 %copy-start.3 = (s32[32]{0:T(128)S(1)}, s32[32]{0:T(128)}, u32[]{:S(2)}) copy-start(s32[32]{0:T(128)} %r_2_.3) | copy-start | bytes 388
  3.0 10.8 %collective-permute-start = (bf16[20,64,128]{2,1,0:T(8,128)(2,1)S(1)}, bf16[20,64,128]{2,1,0:T(8,128)(2,1)S(1)}, u32[]{:S(2)}, u32[]{:S(2)}) collective-permute-start(bf16[20,64,128]{2,1,0:T(8,128)(2,1)S(1)} %get-tuple-element.37), channel_id=1, source_target_pairs={{0,8},{8,0},{16,24},{24,16},{1,9},{9,1},{17,25},{25,17},{2,10},{10... | collective-permute-start | bytes 983048 | tf_op jit(solution)/shard_map/ppermute | solution.py:558
  6.1 1.4 %collective-permute-start.1 = (bf16[16,64,128]{2,1,0:T(8,128)(2,1)S(1)}, bf16[16,64,128]{2,1,0:T(8,128)(2,1)S(1)}, u32[]{:S(2)}, u32[]{:S(2)}) collective-permute-start(bf16[16,64,128]{2,1,0:T(8,128)(2,1)S(1)} %get-tuple-element.38), channel_id=1, source_target_pairs={{8,16},{16,8},{9,17},{17,9},{10,18},{18,10},{11,19},{19,11},{12,20... | collective-permute-start | bytes 786440 | tf_op jit(solution)/shard_map/ppermute | solution.py:558
  6.8 11.7 %collective-permute-start.2 = (bf16[2,512,128]{2,1,0:T(8,128)(2,1)S(1)}, bf16[2,512,128]{2,1,0:T(8,128)(2,1)S(1)}, u32[]{:S(2)}, u32[]{:S(2)}) collective-permute-start(bf16[2,512,128]{2,1,0:T(8,128)(2,1)S(1)} %get-tuple-element.39), channel_id=1, source_target_pairs={{0,1},{1,0},{2,3},{3,2},{4,5},{5,4},{6,7},{7,6},{8,9},{9,8},{10,11... | collective-permute-start | bytes 786440 | tf_op jit(solution)/shard_map/ppermute | solution.py:558
  6.8 14.5 %collective-permute-start.3 = (bf16[2,512,128]{2,1,0:T(8,128)(2,1)S(1)}, bf16[2,512,128]{2,1,0:T(8,128)(2,1)S(1)}, u32[]{:S(2)}, u32[]{:S(2)}) collective-permute-start(bf16[2,512,128]{2,1,0:T(8,128)(2,1)S(1)} %get-tuple-element.40), channel_id=1, source_target_pairs={{1,2},{2,1},{3,4},{4,3},{5,6},{6,5},{9,10},{10,9},{11,12},{12,11},... | collective-permute-start | bytes 786440 | tf_op jit(solution)/shard_map/ppermute | solution.py:558
  13.9 7.5 %collective-permute-start.4 = (bf16[4,64,128]{2,1,0:T(8,128)(2,1)S(1)}, bf16[4,64,128]{2,1,0:T(8,128)(2,1)S(1)}, u32[]{:S(2)}, u32[]{:S(2)}) collective-permute-start(bf16[4,64,128]{2,1,0:T(8,128)(2,1)S(1)} %get-tuple-element.41), channel_id=1, source_target_pairs={{0,1},{1,0},{2,3},{3,2},{4,5},{5,4},{6,7},{7,6},{8,9},{9,8},{10,11... | collective-permute-start | bytes 196616 | tf_op jit(solution)/shard_map/ppermute | solution.py:558
  14.0 7.4 %collective-permute-start.5 = (bf16[4,64,128]{2,1,0:T(8,128)(2,1)S(1)}, bf16[4,64,128]{2,1,0:T(8,128)(2,1)S(1)}, u32[]{:S(2)}, u32[]{:S(2)}) collective-permute-start(bf16[4,64,128]{2,1,0:T(8,128)(2,1)S(1)} %get-tuple-element.42), channel_id=1, source_target_pairs={{1,2},{2,1},{3,4},{4,3},{5,6},{6,5},{9,10},{10,9},{11,12},{12,11},... | collective-permute-start | bytes 196616 | tf_op jit(solution)/shard_map/ppermute | solution.py:558
  14.7 12.6 %collective-permute-start.6 = (bf16[2,128,128]{2,1,0:T(8,128)(2,1)S(1)}, bf16[2,128,128]{2,1,0:T(8,128)(2,1)S(1)}, u32[]{:S(2)}, u32[]{:S(2)}) collective-permute-start(bf16[2,128,128]{2,1,0:T(8,128)(2,1)S(1)} %get-tuple-element.47), channel_id=1, source_target_pairs={{0,24},{8,16},{16,8},{24,0},{1,25},{9,17},{17,9},{25,1},{2,26},{10... | collective-permute-start | bytes 196616 | tf_op jit(solution)/shard_map/ppermute | solution.py:558
  18.5 8.8 %collective-permute-start.7 = (bf16[2,128,128]{2,1,0:T(8,128)(2,1)S(1)}, bf16[2,128,128]{2,1,0:T(8,128)(2,1)S(1)}, u32[]{:S(2)}, u32[]{:S(2)}) collective-permute-start(bf16[2,128,128]{2,1,0:T(8,128)(2,1)S(1)} %get-tuple-element.48), channel_id=1, source_target_pairs={{0,16},{8,24},{16,0},{24,8},{1,17},{9,25},{17,1},{25,9},{2,18},{10... | collective-permute-start | bytes 196616 | tf_op jit(solution)/shard_map/ppermute | solution.py:558
  35.3 42.0 %copy-start = (f32[2,2,512,512]{3,2,1,0:T(8,128)S(1)}, f32[2,2,512,512]{3,2,1,0:T(8,128)}, u32[]{:S(2)}) copy-start(f32[2,2,512,512]{3,2,1,0:T(8,128)} %obj.5) | copy-start | bytes 12582916
  35.3 9.3 %collective-permute-start.8 = (bf16[20,64,128]{2,1,0:T(8,128)(2,1)S(1)}, bf16[20,64,128]{2,1,0:T(8,128)(2,1)S(1)}, u32[]{:S(2)}, u32[]{:S(2)}) collective-permute-start(bf16[20,64,128]{2,1,0:T(8,128)(2,1)S(1)} %get-tuple-element.51), channel_id=1, source_target_pairs={{0,8},{8,0},{16,24},{24,16},{1,9},{9,1},{17,25},{25,17},{2,10},{10... | collective-permute-start | bytes 983048 | tf_op jit(solution)/shard_map/ppermute | solution.py:558
  35.6 9.0 %collective-permute-start.9 = (bf16[20,64,128]{2,1,0:T(8,128)(2,1)S(1)}, bf16[20,64,128]{2,1,0:T(8,128)(2,1)S(1)}, u32[]{:S(2)}, u32[]{:S(2)}) collective-permute-start(bf16[20,64,128]{2,1,0:T(8,128)(2,1)S(1)} %get-tuple-element.52), channel_id=1, source_target_pairs={{8,16},{16,8},{9,17},{17,9},{10,18},{18,10},{11,19},{19,11},{12,20... | collective-permute-start | bytes 983048 | tf_op jit(solution)/shard_map/ppermute | solution.py:558
  36.5 10.5 %collective-permute-start.12 = (f32[4,128,128]{2,1,0:T(8,128)S(1)}, f32[4,128,128]{2,1,0:T(8,128)S(1)}, u32[]{:S(2)}, u32[]{:S(2)}) collective-permute-start(f32[4,128,128]{2,1,0:T(8,128)S(1)} %get-tuple-element.57), channel_id=1, source_target_pairs={{0,1},{1,0},{2,3},{3,2},{4,5},{5,4},{6,7},{7,6},{8,9},{9,8},{10,11... | collective-permute-start | bytes 786440 | tf_op jit(solution)/shard_map/ppermute | solution.py:558
  45.0 35.2 %collective-permute-start.10 = (bf16[2,512,128]{2,1,0:T(8,128)(2,1)S(1)}, bf16[2,512,128]{2,1,0:T(8,128)(2,1)S(1)}, u32[]{:S(2)}, u32[]{:S(2)}) collective-permute-start(bf16[2,512,128]{2,1,0:T(8,128)(2,1)S(1)} %get-tuple-element.54), channel_id=1, source_target_pairs={{0,1},{1,0},{2,3},{3,2},{4,5},{5,4},{6,7},{7,6},{8,9},{9,8},{10,11... | collective-permute-start | bytes 786440 | tf_op jit(solution)/shard_map/ppermute | solution.py:558
  46.3 33.9 %collective-permute-start.11 = (bf16[2,512,128]{2,1,0:T(8,128)(2,1)S(1)}, bf16[2,512,128]{2,1,0:T(8,128)(2,1)S(1)}, u32[]{:S(2)}, u32[]{:S(2)}) collective-permute-start(bf16[2,512,128]{2,1,0:T(8,128)(2,1)S(1)} %get-tuple-element.55), channel_id=1, source_target_pairs={{1,2},{2,1},{3,4},{4,3},{5,6},{6,5},{9,10},{10,9},{11,12},{12,11},... | collective-permute-start | bytes 786440 | tf_op jit(solution)/shard_map/ppermute | solution.py:558
  47.0 11.2 %collective-permute-start.13 = (bf16[128,128]{1,0:T(8,128)(2,1)S(1)}, bf16[128,128]{1,0:T(8,128)(2,1)S(1)}, u32[]{:S(2)}, u32[]{:S(2)}) collective-permute-start(bf16[128,128]{1,0:T(8,128)(2,1)S(1)} %get-tuple-element.59), channel_id=1, source_target_pairs={{0,2},{1,3},{2,0},{3,1},{4,6},{5,7},{6,4},{7,5},{8,10},{9,11},{10,... | collective-permute-start | bytes 98312 | tf_op jit(solution)/shard_map/ppermute | solution.py:558
  51.4 6.9 %collective-permute-start.14 = (bf16[128,128]{1,0:T(8,128)(2,1)S(1)}, bf16[128,128]{1,0:T(8,128)(2,1)S(1)}, u32[]{:S(2)}, u32[]{:S(2)}) collective-permute-start(bf16[128,128]{1,0:T(8,128)(2,1)S(1)} %get-tuple-element.60), channel_id=1, source_target_pairs={{0,4},{1,5},{2,6},{3,7},{4,0},{5,1},{6,2},{7,3},{8,12},{9,13},{10,... | collective-permute-start | bytes 98312 | tf_op jit(solution)/shard_map/ppermute | solution.py:558
  53.5 4.8 %collective-permute-start.15 = (bf16[128,128]{1,0:T(8,128)(2,1)S(1)}, bf16[128,128]{1,0:T(8,128)(2,1)S(1)}, u32[]{:S(2)}, u32[]{:S(2)}) collective-permute-start(bf16[128,128]{1,0:T(8,128)(2,1)S(1)} %get-tuple-element.61), channel_id=1, source_target_pairs={{0,6},{1,7},{2,4},{3,5},{4,2},{5,3},{6,0},{7,1},{8,14},{9,15},{10,... | collective-permute-start | bytes 98312 | tf_op jit(solution)/shard_map/ppermute | solution.py:558
  58.3 6.9 %collective-permute-start.18 = (bf16[128,128]{1,0:T(8,128)(2,1)S(1)}, bf16[128,128]{1,0:T(8,128)(2,1)S(1)}, u32[]{:S(2)}, u32[]{:S(2)}) collective-permute-start(bf16[128,128]{1,0:T(8,128)(2,1)S(1)} %shard_map.104.r_0_), channel_id=1, source_target_pairs={{0,16},{8,24},{16,0},{24,8},{1,17},{9,25},{17,1},{25,9},{2,18},{10... | collective-permute-start | bytes 98312 | tf_op jit(solution)/shard_map/ppermute | solution.py:558
  63.3 6.1 %collective-permute-start.17 = (bf16[128,128]{1,0:T(8,128)(2,1)S(1)}, bf16[128,128]{1,0:T(8,128)(2,1)S(1)}, u32[]{:S(2)}, u32[]{:S(2)}) collective-permute-start(bf16[128,128]{1,0:T(8,128)(2,1)S(1)} %shard_map.104.r_0_), channel_id=1, source_target_pairs={{0,24},{8,16},{16,8},{24,0},{1,25},{9,17},{17,9},{25,1},{2,26},{10... | collective-permute-start | bytes 98312 | tf_op jit(solution)/shard_map/ppermute | solution.py:558
  64.5 4.8 %collective-permute-start.16 = (bf16[128,128]{1,0:T(8,128)(2,1)S(1)}, bf16[128,128]{1,0:T(8,128)(2,1)S(1)}, u32[]{:S(2)}, u32[]{:S(2)}) collective-permute-start(bf16[128,128]{1,0:T(8,128)(2,1)S(1)} %shard_map.104.r_0_), channel_id=1, source_target_pairs={{0,8},{8,0},{16,24},{24,16},{1,9},{9,1},{17,25},{25,17},{2,10},{10... | collective-permute-start | bytes 98312 | tf_op jit(solution)/shard_map/ppermute | solution.py:558
  69.4 5.0 %collective-permute-start.21 = (bf16[128,128]{1,0:T(8,128)(2,1)S(1)}, bf16[128,128]{1,0:T(8,128)(2,1)S(1)}, u32[]{:S(2)}, u32[]{:S(2)}) collective-permute-start(bf16[128,128]{1,0:T(8,128)(2,1)S(1)} %shard_map.105.refs_0_), channel_id=1, source_target_pairs={{0,6},{1,7},{2,4},{3,5},{4,2},{5,3},{6,0},{7,1},{8,14},{9,15},{10,... | collective-permute-start | bytes 98312 | tf_op jit(solution)/shard_map/ppermute | solution.py:558
  71.5 3.9 %collective-permute-start.20 = (bf16[128,128]{1,0:T(8,128)(2,1)S(1)}, bf16[128,128]{1,0:T(8,128)(2,1)S(1)}, u32[]{:S(2)}, u32[]{:S(2)}) collective-permute-start(bf16[128,128]{1,0:T(8,128)(2,1)S(1)} %shard_map.105.refs_0_), channel_id=1, source_target_pairs={{0,4},{1,5},{2,6},{3,7},{4,0},{5,1},{6,2},{7,3},{8,12},{9,13},{10,... | collective-permute-start | bytes 98312 | tf_op jit(solution)/shard_map/ppermute | solution.py:558
  73.3 3.9 %collective-permute-start.19 = (bf16[128,128]{1,0:T(8,128)(2,1)S(1)}, bf16[128,128]{1,0:T(8,128)(2,1)S(1)}, u32[]{:S(2)}, u32[]{:S(2)}) collective-permute-start(bf16[128,128]{1,0:T(8,128)(2,1)S(1)} %shard_map.105.refs_0_), channel_id=1, source_target_pairs={{0,2},{1,3},{2,0},{3,1},{4,6},{5,7},{6,4},{7,5},{8,10},{9,11},{10,... | collective-permute-start | bytes 98312 | tf_op jit(solution)/shard_map/ppermute | solution.py:558
  77.2 1.8 %collective-permute-start.22 = (bf16[4,128,128]{2,1,0:T(8,128)(2,1)S(1)}, bf16[4,128,128]{2,1,0:T(8,128)(2,1)S(1)}, u32[]{:S(2)}, u32[]{:S(2)}) collective-permute-start(bf16[4,128,128]{2,1,0:T(8,128)(2,1)S(1)} %shard_map.106.joined), channel_id=1, source_target_pairs={{0,1},{1,0},{2,3},{3,2},{4,5},{5,4},{6,7},{7,6},{8,9},{9,8},{10,11... | collective-permute-start | bytes 393224 | tf_op jit(solution)/shard_map/ppermute | solution.py:558
